TPU v7x, 32 devices: a 4x4x1 block of a 4x4x8 slice. The times are simulated.
32 devices in a mesh: dp: 1 (over z), sp: 32 (over y, x, core).
Axes of the slice: x: 4, y: 4, z: 1, core: 2. Of those that a mesh axis runs over, the one named last changes fastest.
The devices are a block of a 4x4x8 slice.
Arguments:
- tokens: bfloat16 [8192, 2048], P(('dp', 'sp'))
- w_q: bfloat16 [2048, 2048], replicated
- w_k: bfloat16 [2048, 2048], replicated
- w_v: bfloat16 [2048, 2048], replicated
- w_o: bfloat16 [2048, 2048], replicated
- grad_y: bfloat16 [8192, 2048], P(('dp', 'sp'))
Outputs:
- output 1: bfloat16 [8192, 2048], P(('dp', 'sp'))
- output 2: bfloat16 [8192, 2048], P(('dp', 'sp'))
- output 3: float32 [2048, 2048], P('dp')
- output 4: float32 [2048, 2048], P('dp')
- output 5: float32 [2048, 2048], P('dp')
- output 6: float32 [2048, 2048], P('dp')
All inputs are finite; a program needn't handle non-finite values.
Results may differ from a plain program's by a relative error of at most 0.00456876.
Values are sent between devices in bfloat16 or wider.
A program may use at most 768 MiB of HBM per device.

v0:
```python
import math
import jax
import jax.numpy as jnp
from jax import lax
from jax.sharding import PartitionSpec as P

HEAD_DIM = 128
BLOCK_LEN = 128


def solution(mesh):
    n_seq = mesh.shape["sp"]
    fwd_perm = [(j, j + 1) for j in range(n_seq - 1)]
    rev_perm = [(j + 1, j) for j in range(n_seq - 1)]
    row_spec = P(("dp", "sp"), None)
    grad_spec = P("dp", None)

    def local_layer(tokens, w_q, w_k, w_v, w_o, grad_y):
        n_rows, model_dim = tokens.shape
        n_heads = model_dim // HEAD_DIM
        n_blocks = n_rows // BLOCK_LEN
        att_scale = 1.0 / math.sqrt(n_rows * n_seq * HEAD_DIM)
        causal = jnp.arange(BLOCK_LEN)[:, None] >= jnp.arange(BLOCK_LEN)[None, :]

        def project(operand, weight):
            return jnp.dot(operand, weight, preferred_element_type=jnp.float32).astype(jnp.bfloat16)

        def back_proj(rows, weight):
            return jnp.einsum("ne,de->nd", rows, weight, preferred_element_type=jnp.float32)

        def weight_grad(left_rows, right_rows):
            return jnp.einsum("nd,ne->de", left_rows, right_rows, preferred_element_type=jnp.float32)

        def split_heads(tensor):
            return tensor.reshape(n_blocks, BLOCK_LEN, n_heads, HEAD_DIM)

        def to_rows(tensor):
            return (tensor * att_scale).astype(jnp.bfloat16).reshape(n_rows, model_dim)

        q_heads = split_heads(project(tokens, w_q))
        k_heads = split_heads(project(tokens, w_k))
        v_heads = split_heads(project(tokens, w_v))
        block_kv = jnp.einsum("nshd,nshe->nhde", k_heads, v_heads, preferred_element_type=jnp.float32)
        kv_total = jnp.sum(block_kv, axis=0)

        def fwd_hop(hop_index, carried):
            return lax.ppermute(carried + kv_total, "sp", perm=fwd_perm)

        kv_in = lax.fori_loop(0, n_seq - 1, fwd_hop, jnp.zeros_like(kv_total))
        fwd_state = (kv_in + jnp.cumsum(block_kv, axis=0) - block_kv).astype(jnp.bfloat16)
        scores = jnp.einsum("nthd,nshd->nhts", q_heads, k_heads, preferred_element_type=jnp.float32)
        masked_scores = jnp.where(causal, scores, 0.0).astype(jnp.bfloat16)
        out_rows = to_rows(jnp.einsum("nhts,nshe->nthe", masked_scores, v_heads, preferred_element_type=jnp.float32) + jnp.einsum("nthd,nhde->nthe", q_heads, fwd_state, preferred_element_type=jnp.float32))
        out_y = project(out_rows, w_o)

        do_heads = split_heads(back_proj(grad_y, w_o).astype(jnp.bfloat16))
        block_qdo = jnp.einsum("nthd,nthe->nhde", q_heads, do_heads, preferred_element_type=jnp.float32)
        qdo_total = jnp.sum(block_qdo, axis=0)

        def rev_hop(hop_index, carried):
            return lax.ppermute(carried + qdo_total, "sp", perm=rev_perm)

        qdo_in = lax.fori_loop(0, n_seq - 1, rev_hop, jnp.zeros_like(qdo_total))
        rev_state = (qdo_in + qdo_total - jnp.cumsum(block_qdo, axis=0)).astype(jnp.bfloat16)
        d_scores = jnp.einsum("nthe,nshe->nhts", do_heads, v_heads, preferred_element_type=jnp.float32)
        masked_grads = jnp.where(causal, d_scores, 0.0).astype(jnp.bfloat16)
        dq_rows = to_rows(jnp.einsum("nhts,nshd->nthd", masked_grads, k_heads, preferred_element_type=jnp.float32) + jnp.einsum("nthe,nhde->nthd", do_heads, fwd_state, preferred_element_type=jnp.float32))
        dk_rows = to_rows(jnp.einsum("nhts,nthd->nshd", masked_grads, q_heads, preferred_element_type=jnp.float32) + jnp.einsum("nshe,nhde->nshd", v_heads, rev_state, preferred_element_type=jnp.float32))
        dv_rows = to_rows(jnp.einsum("nhts,nthe->nshe", masked_scores, do_heads, preferred_element_type=jnp.float32) + jnp.einsum("nshd,nhde->nshe", k_heads, rev_state, preferred_element_type=jnp.float32))
        grad_x = (back_proj(dq_rows, w_q) + back_proj(dk_rows, w_k) + back_proj(dv_rows, w_v)).astype(jnp.bfloat16)
        grads = lax.psum((weight_grad(tokens, dq_rows), weight_grad(tokens, dk_rows), weight_grad(tokens, dv_rows), weight_grad(out_rows, grad_y)), "sp")
        return (out_y, grad_x) + tuple(grads)

    return jax.shard_map(local_layer, mesh=mesh, in_specs=(row_spec, P(), P(), P(), P(), row_spec), out_specs=(row_spec, row_spec, grad_spec, grad_spec, grad_spec, grad_spec), check_vma=False)
```

profile of v0, /device:TPU:97, one launch (start us, length us, event | category | flops | bytes accessed | tf_op | source)
XLA Modules:
  0.0 1893.5 jit_solution(554155457907398861)
XLA Ops:
  56.9 606.2 %while.20 = (s32[]{:T(128)}, f32[16,128,128]{2,1,0:T(8,128)S(1)}, f32[16,128,128]{2,1,0:T(8,128)}, s32[]{:T(128)}) while((s32[]{:T(128)}, f32[16,128,128]{2,1,0:T(8,128)S(1)}, f32[16,128,128]{2,1,0:T(8,128)}, s32[]{:T(128)}) %tuple.39), condition=%wide.region_2.0_spmd, body=%wide.region_1.0_spmd.sunk | while | flops 262146 | bytes 7340125 | solution.py:49
  674.1 607.9 %while.21 = (s32[]{:T(128)}, f32[16,128,128]{2,1,0:T(8,128)S(1)}, f32[16,128,128]{2,1,0:T(8,128)S(1)}, s32[]{:T(128)}) while((s32[]{:T(128)}, f32[16,128,128]{2,1,0:T(8,128)S(1)}, f32[16,128,128]{2,1,0:T(8,128)S(1)}, s32[]{:T(128)}) %tuple.42), condition=%wide.region_6.7_spmd, body=%wide.region_5.6_spmd.sunk | while | flops 262146 | bytes 7340125 | solution.py:63
  677.2 17.1 collective-permute-done.1
  716.8 17.1 collective-permute-done.1
  756.3 17.1 collective-permute-done.1
  795.9 17.1 collective-permute-done.1
  816.1 16.5 collective-permute-done.1
  835.7 16.5 collective-permute-done.1
  855.2 16.5 collective-permute-done.1
  874.7 16.5 collective-permute-done.1
  894.3 16.5 collective-permute-done.1
  913.8 16.5 collective-permute-done.1
  933.4 16.5 collective-permute-done.1
  1148.3 16.5 collective-permute-done.1
  1167.8 16.5 collective-permute-done.1
  1187.4 16.5 collective-permute-done.1
  1206.9 16.5 collective-permute-done.1
  1226.4 16.5 collective-permute-done.1
  1246.0 16.5 collective-permute-done.1
  1265.5 16.5 collective-permute-done.1
  1347.5 474.2 %all-reduce.3.cloned.1.call-done = (f32[2048,2048]{0,1:T(8,128)}, f32[2048,2048]{0,1:T(8,128)}, f32[2048,2048]{0,1:T(8,128)}, f32[2048,2048]{1,0:T(8,128)}) async-done(((f32[2048,2048]{0,1:T(8,128)}, f32[2048,2048]{0,1:T(8,128)}, f32[2048,2048]{0,1:T(8,128)}, f32[2048,2048]{1,0:T(8,128)}), (f32[2048,2048]{0,1:T(8,128)}, f32[2048,2048]{0,1:T(8,128)}, f32[2048,2048]{0,1:T(8,128)}, ...) | async-done | bytes 67108880 | tf_op jit(solution)/shard_map/psum | solution.py:71
  1821.7 17.6 copy.55
  1839.3 17.6 copy.56
  1856.9 17.6 copy.57
  (265 shorter events, 1039.1 us)
Async XLA Ops:
  7.2 1814.5 %all-reduce.3.cloned.1.call-start = ((), (), s32[]{:S(2)}) async-start(), calls=%async_computation | async-start | bytes 134217728 | tf_op jit(solution)/shard_map/psum | solution.py:71
  561.2 18.5 collective-permute-start
  582.1 18.5 collective-permute-start
  602.9 18.5 collective-permute-start
  623.8 18.5 collective-permute-start
  644.6 18.5 collective-permute-start
  675.2 19.1 %collective-permute-start.1 = (f32[16,128,128]{2,1,0:T(8,128)}, f32[16,128,128]{2,1,0:T(8,128)S(1)}, u32[]{:S(2)}, u32[]{:S(2)}) collective-permute-start(f32[16,128,128]{2,1,0:T(8,128)} %add.87), channel_id=1, source_target_pairs={{1,0},{2,1},{3,2},{4,3},{5,4},{6,5},{7,6},{8,7},{9,8},{10,9},{11,1... | collective-permute-start | bytes 3145736 | tf_op jit(solution)/shard_map/while/body/eval_jaxpr/ppermute | solution.py:61
  714.8 19.1 %collective-permute-start.1 = (f32[16,128,128]{2,1,0:T(8,128)}, f32[16,128,128]{2,1,0:T(8,128)S(1)}, u32[]{:S(2)}, u32[]{:S(2)}) collective-permute-start(f32[16,128,128]{2,1,0:T(8,128)} %add.87), channel_id=1, source_target_pairs={{1,0},{2,1},{3,2},{4,3},{5,4},{6,5},{7,6},{8,7},{9,8},{10,9},{11,1... | collective-permute-start | bytes 3145736 | tf_op jit(solution)/shard_map/while/body/eval_jaxpr/ppermute | solution.py:61
  754.4 19.1 %collective-permute-start.1 = (f32[16,128,128]{2,1,0:T(8,128)}, f32[16,128,128]{2,1,0:T(8,128)S(1)}, u32[]{:S(2)}, u32[]{:S(2)}) collective-permute-start(f32[16,128,128]{2,1,0:T(8,128)} %add.87), channel_id=1, source_target_pairs={{1,0},{2,1},{3,2},{4,3},{5,4},{6,5},{7,6},{8,7},{9,8},{10,9},{11,1... | collective-permute-start | bytes 3145736 | tf_op jit(solution)/shard_map/while/body/eval_jaxpr/ppermute | solution.py:61
  794.0 19.1 %collective-permute-start.1 = (f32[16,128,128]{2,1,0:T(8,128)}, f32[16,128,128]{2,1,0:T(8,128)S(1)}, u32[]{:S(2)}, u32[]{:S(2)}) collective-permute-start(f32[16,128,128]{2,1,0:T(8,128)} %add.87), channel_id=1, source_target_pairs={{1,0},{2,1},{3,2},{4,3},{5,4},{6,5},{7,6},{8,7},{9,8},{10,9},{11,1... | collective-permute-start | bytes 3145736 | tf_op jit(solution)/shard_map/while/body/eval_jaxpr/ppermute | solution.py:61
  814.2 18.5 collective-permute-start.1
  833.7 18.5 collective-permute-start.1
  853.2 18.5 collective-permute-start.1
  872.8 18.5 collective-permute-start.1
  892.3 18.5 collective-permute-start.1
  911.9 18.5 collective-permute-start.1
  931.4 18.5 collective-permute-start.1
  1146.3 18.5 collective-permute-start.1
  1165.9 18.5 collective-permute-start.1
  1185.4 18.5 collective-permute-start.1
  1204.9 18.5 collective-permute-start.1
  1224.5 18.5 collective-permute-start.1
  1244.0 18.5 collective-permute-start.1
  1263.6 18.5 collective-permute-start.1
  (65 other events, 836.9 us)
Sparse Core Ops, SparseCore 0:
  1325.5 496.2 all-reduce.2
where the time goes:
time: 1900 us; the launch traced here: 1890 us
  waiting for transfers between devices  1360 us (72%)
  starting transfers between devices  206 us (11%)
  other arithmetic  111 us (6%)
  matrix products  99.8 us (5%)
  local copies, waits for them, and re-layouts  87.4 us (5%)
    ppermute x31, waiting for transfers between devices, rev_hop(): return lax.ppermute(carried + qdo_total, 'sp', perm=rev_perm)  514 us
    psum x1, waiting for transfers between devices, local_layer(): lax.psum((weight_grad(tokens, dq_rows), weight_grad(tokens, dk_rows), wei...  474 us
    ppermute x31, waiting for transfers between devices, fwd_hop(): return lax.ppermute(carried + kv_total, 'sp', perm=fwd_perm)  373 us
    ppermute x31, starting transfers between devices, fwd_hop(): return lax.ppermute(carried + kv_total, 'sp', perm=fwd_perm)  146 us
    unnamed x60, local copies, waits for them, and re-layouts  74.6 us
    add x31, other arithmetic, fwd_hop(): return lax.ppermute(carried + kv_total, 'sp', perm=fwd_perm)  74.1 us
    ppermute x31, starting transfers between devices, rev_hop(): return lax.ppermute(carried + qdo_total, 'sp', perm=rev_perm)  60.1 us
  transfers between devices with their start and end apart: 63, of which 63 were waited for; matrix products, arithmetic and copies ran while one was open for 1% of the time, Pallas kernels for 0%

commit v1 on v0

v1 whole, which is shorter than its diff:
```python
import functools
import math
import jax
import jax.numpy as jnp
from jax import lax
from jax.experimental import pallas as pl
from jax.experimental.pallas import tpu as pltpu
from jax.sharding import PartitionSpec as P


HEAD_DIM = 128
BLOCK_LEN = 128
N_CORES = 2
N_GRADS = 4


F32 = jnp.float32
BF16 = jnp.bfloat16
VMEM = pltpu.VMEM


def dot(a, b, dims):
    return lax.dot_general(a, b, ((dims[:1], dims[1:]), ((), ())), preferred_element_type=F32)


def project_kernel(x_ref, dy_ref, wq_ref, wk_ref, wv_ref, wo_ref, q_ref, k_ref, v_ref, do_ref, totals_ref):
    x = x_ref[...]
    q_ref[...] = dot(x, wq_ref[...], (1, 0)).astype(BF16)
    k_ref[...] = dot(x, wk_ref[...], (1, 0)).astype(BF16)
    v_ref[...] = dot(x, wv_ref[...], (1, 0)).astype(BF16)
    do_ref[...] = dot(dy_ref[...], wo_ref[...], (1, 1)).astype(BF16)
    rows = totals_ref.shape[2]
    per_head = HEAD_DIM // rows
    for head in range(q_ref.shape[1] // HEAD_DIM):
        cols = slice(head * HEAD_DIM, (head + 1) * HEAD_DIM)
        kv = dot(k_ref[:, cols], v_ref[:, cols], (0, 0))
        qdo = dot(q_ref[:, cols], do_ref[:, cols], (0, 0))
        for part in range(per_head):
            totals_ref[head * per_head + part, 0] = kv[part * rows : (part + 1) * rows]
            totals_ref[head * per_head + part, 1] = qdo[part * rows : (part + 1) * rows]


def prefix_kernel(parts_ref, out_ref):
    n_parts = parts_ref.shape[0]
    before = jnp.zeros_like(parts_ref[0, 0])
    after = jnp.zeros_like(parts_ref[0, 1])
    for step in range(n_parts):
        last = n_parts - 1 - step
        out_ref[step, 0] = before
        out_ref[last, 1] = after
        before = before + parts_ref[step, 0]
        after = after + parts_ref[last, 1]


def attend_kernel(scale, q_ref, k_ref, v_ref, do_ref, x_ref, dy_ref, state_ref, left_ref, right_ref):
    n_blocks = q_ref.shape[0] // BLOCK_LEN
    left_ref[0] = x_ref[...]
    right_ref[3] = dy_ref[...]
    rows = [pl.ds(b * BLOCK_LEN, BLOCK_LEN) for b in range(n_blocks)]
    fwd = [state_ref[:, 0].reshape(HEAD_DIM, HEAD_DIM)]
    for b in range(n_blocks - 1):
        fwd.append(fwd[-1] + dot(k_ref[rows[b]], v_ref[rows[b]], (0, 0)))
    rev = [state_ref[:, 1].reshape(HEAD_DIM, HEAD_DIM)]
    for b in range(n_blocks - 1, 0, -1):
        rev.insert(0, rev[0] + dot(q_ref[rows[b]], do_ref[rows[b]], (0, 0)))
    shape = (BLOCK_LEN, BLOCK_LEN)
    causal = lax.broadcasted_iota(jnp.int32, shape, 0) >= lax.broadcasted_iota(jnp.int32, shape, 1)
    for b in range(n_blocks):
        q, k, v, do = q_ref[rows[b]], k_ref[rows[b]], v_ref[rows[b]], do_ref[rows[b]]
        s = fwd[b].astype(BF16)
        r = rev[b].astype(BF16)
        att = jnp.where(causal, dot(q, k, (1, 1)), 0.0).astype(BF16)
        d_att = jnp.where(causal, dot(do, v, (1, 1)), 0.0).astype(BF16)
        left_ref[1, rows[b]] = ((dot(att, v, (1, 0)) + dot(q, s, (1, 0))) * scale).astype(BF16)
        right_ref[0, rows[b]] = ((dot(d_att, k, (1, 0)) + dot(do, s, (1, 1))) * scale).astype(BF16)
        right_ref[1, rows[b]] = ((dot(d_att, q, (0, 0)) + dot(v, r, (1, 1))) * scale).astype(BF16)
        right_ref[2, rows[b]] = ((dot(att, do, (0, 0)) + dot(k, r, (1, 0))) * scale).astype(BF16)


def place_kernel(side, step, fresh, *refs):
    blocks = refs[:4]
    grads = refs[4 if fresh else 4 + N_GRADS :][:N_GRADS]
    buf, sem_in, sem_out = refs[-3:]
    index = lax.axis_index("sp")
    core = lax.rem(index, N_CORES)
    col = lax.rem(index // N_CORES, side)
    row = index // (N_CORES * side)
    height = blocks[0].shape[0]
    half = grads[0].shape[0] // 2
    granule = buf.shape[1]
    per_block = height // granule
    jobs = []
    for k, src in enumerate(blocks):
        own, part = k < 2, k % 2
        at = col if part == 0 else row
        c = core if own else 1 - core
        which = lax.rem(at - (1 - 2 * c) * step + 2 * side, side)
        start = part * half + c * height
        for g in range(per_block):
            jobs.append((src.at[pl.ds(g * granule, granule)], which, pl.multiple_of(start + g * granule, granule)))
    for n, (src, which, start) in enumerate(jobs):
        pltpu.make_async_copy(src, buf.at[n], sem_in.at[n]).start()
    for n, (src, which, start) in enumerate(jobs):
        pltpu.make_async_copy(src, buf.at[n], sem_in.at[n]).wait()
        for m in range(N_GRADS):

            @pl.when(which == m)
            def _():
                pltpu.make_async_copy(buf.at[n], grads[m].at[pl.ds(start, granule)], sem_out.at[n]).start()

    for n, (src, which, start) in enumerate(jobs):
        pltpu.make_async_copy(buf.at[n], grads[0].at[pl.ds(0, granule)], sem_out.at[n]).wait()


def solution(mesh):
    n_seq = mesh.shape["sp"]
    side = math.isqrt(n_seq // N_CORES)
    row_spec = P(("dp", "sp"), None)
    grad_spec = P("dp", None)

    def device_at(row, col, core):
        return ((row % side) * side + col % side) * N_CORES + core

    def ring_perm(axis, hops):
        pairs = []
        for row in range(side):
            for col in range(side):
                for core in range(N_CORES):
                    shift = hops * (1 - 2 * core)
                    target = device_at(row, col + shift, core) if axis == "x" else device_at(row + shift, col, core)
                    pairs.append((device_at(row, col, core), target))
        return pairs

    core_perm = [(j, j ^ 1) for j in range(n_seq)]

    def local_layer(tokens, w_q, w_k, w_v, w_o, grad_y):
        n_rows, model_dim = tokens.shape
        n_heads = model_dim // HEAD_DIM
        att_scale = 1.0 / math.sqrt(n_rows * n_seq * HEAD_DIM)
        index = lax.axis_index("sp")
        core = lax.rem(index, N_CORES)
        sign = 1 - 2 * core
        place = {"x": lax.rem(index // N_CORES, side), "y": index // (N_CORES * side)}

        def swap_cores(value):
            return lax.ppermute(value, "sp", perm=core_perm)

        def hop(value, axis, hops):
            return lax.ppermute(value, "sp", perm=ring_perm(axis, hops))

        def at_shift(axis, shift):
            return lax.rem(place[axis] + sign * shift + 2 * side, side)

        def project(operand, weight):
            return jnp.dot(operand, weight, preferred_element_type=F32).astype(BF16)

        def back_proj(rows, weight):
            return jnp.einsum("ne,de->nd", rows, weight, preferred_element_type=F32)

        tile = 2 * HEAD_DIM
        slice_rows = n_heads * HEAD_DIM // n_seq
        per_tile = tile // slice_rows
        full = pl.BlockSpec((n_rows, model_dim), lambda i: (0, 0))
        in_cols = pl.BlockSpec((model_dim, tile), lambda i: (0, i))
        in_rows = pl.BlockSpec((tile, model_dim), lambda i: (i, 0))
        out_cols = pl.BlockSpec((n_rows, tile), lambda i: (0, i))
        act = jax.ShapeDtypeStruct((n_rows, model_dim), BF16)
        q, k, v, do, totals = pl.pallas_call(
            project_kernel,
            grid=(model_dim // tile,),
            in_specs=[full, full, in_cols, in_cols, in_cols, in_rows],
            out_specs=[out_cols] * 4 + [pl.BlockSpec((per_tile, 2, slice_rows, HEAD_DIM), lambda i: (i, 0, 0, 0))],
            out_shape=[act] * 4 + [jax.ShapeDtypeStruct((n_seq, 2, slice_rows, HEAD_DIM), F32)],
            cost_estimate=pl.CostEstimate(flops=8 * n_rows * model_dim * model_dim, bytes_accessed=8 * model_dim * model_dim, transcendentals=0),
            compiler_params=pltpu.CompilerParams(vmem_limit_bytes=48 * 2**20),
            name="project",
        )(tokens, grad_y, w_q, w_k, w_v, w_o)

        parts = lax.all_to_all(totals, "sp", 0, 0)
        prefixes = pl.pallas_call(
            prefix_kernel,
            out_shape=jax.ShapeDtypeStruct(parts.shape, parts.dtype),
            in_specs=[pl.BlockSpec(memory_space=VMEM)],
            out_specs=pl.BlockSpec(memory_space=VMEM),
            cost_estimate=pl.CostEstimate(flops=2 * parts.size, bytes_accessed=8 * parts.size, transcendentals=0),
            name="state_prefix",
        )(parts)
        states = lax.all_to_all(prefixes, "sp", 0, 0)

        head_cols = pl.BlockSpec((n_rows, HEAD_DIM), lambda h: (0, h))
        per_head = HEAD_DIM // slice_rows
        lefts, rights = pl.pallas_call(
            functools.partial(attend_kernel, att_scale),
            grid=(n_heads,),
            in_specs=[head_cols] * 6 + [pl.BlockSpec((per_head, 2, slice_rows, HEAD_DIM), lambda h: (h, 0, 0, 0))],
            out_specs=[pl.BlockSpec((2, n_rows, HEAD_DIM), lambda h: (0, 0, h)), pl.BlockSpec((4, n_rows, HEAD_DIM), lambda h: (0, 0, h))],
            out_shape=[jax.ShapeDtypeStruct((2, n_rows, model_dim), BF16), jax.ShapeDtypeStruct((4, n_rows, model_dim), BF16)],
            cost_estimate=pl.CostEstimate(flops=n_heads * 24 * 2 * 128**3, bytes_accessed=2**24, transcendentals=0),
            name="attend",
        )(q, k, v, do, tokens, grad_y, states)

        half = model_dim // 2
        block = half // N_CORES

        def packet(which, part):
            left = lax.dynamic_index_in_dim(lefts, which // (N_GRADS - 1), 0, keepdims=False)[:, part * half : (part + 1) * half]
            right = lax.dynamic_index_in_dim(rights, which, 0, keepdims=False)
            return jnp.concatenate([left, right], axis=1)

        axes = (("x", "y"), ("y", "x"))
        received = []
        for part, (first, second) in enumerate(axes):
            far = hop(packet(at_shift(first, 2), part), first, 1)
            near = hop(packet(at_shift(first, 1), part), first, 1)
            back = hop(packet(at_shift(first, -1), part), first, -1)
            received.append([packet(place[first], part), near, back, hop(far, first, 1)])

        def block_product(left, right):
            return jnp.einsum("nd,ne->de", left, right, preferred_element_type=F32)

        sums = []
        for part in range(2):
            total = None
            for pack in received[part]:
                left, right = pack[:, :half], pack[:, half:]
                mine = lax.dynamic_slice_in_dim(left, core * block, block, 1)
                yours = lax.dynamic_slice_in_dim(left, (1 - core) * block, block, 1)
                other = swap_cores(jnp.concatenate([yours, right], axis=1))
                here = block_product(mine, right)
                total = here if total is None else total + here
                total = total + block_product(other[:, :block], other[:, block:])
            sums.append(total)

        piece = block // side
        pieces = [None, None]
        for step in range(side):
            for part, (first, second) in enumerate(axes):
                own = lax.dynamic_slice_in_dim(sums[part], at_shift(second, -(step + 1)) * piece, piece, 0)
                pieces[part] = own if step == 0 else pieces[part] + own
                if step < side - 1:
                    pieces[part] = hop(pieces[part], second, 1)

        blocks = [jnp.zeros((block, model_dim), F32) for _ in axes]
        for step in range(side):
            for part, (first, second) in enumerate(axes):
                if step:
                    pieces[part] = hop(pieces[part], second, 1)
                blocks[part] = lax.dynamic_update_slice_in_dim(blocks[part], pieces[part], at_shift(second, -step) * piece, 0)

        grads = []
        granule = 128
        n_copies = 4 * block // granule
        for step in range(side):
            if step:
                for part, (first, second) in enumerate(axes):
                    blocks[part] = hop(blocks[part], first, 1)
            others = [swap_cores(b) for b in blocks]
            place_blocks = pl.pallas_call(
                functools.partial(place_kernel, side, step, step == 0),
                in_specs=[pl.BlockSpec(memory_space=pl.ANY)] * (4 + len(grads)),
                out_specs=[pl.BlockSpec(memory_space=pl.ANY)] * N_GRADS,
                out_shape=[jax.ShapeDtypeStruct((model_dim, model_dim), F32)] * N_GRADS,
                scratch_shapes=[VMEM((n_copies, granule, model_dim), F32), pltpu.SemaphoreType.DMA((n_copies,)), pltpu.SemaphoreType.DMA((n_copies,))],
                input_output_aliases={} if step == 0 else {4 + m: m for m in range(N_GRADS)},
                cost_estimate=pl.CostEstimate(flops=5 * 10**9, bytes_accessed=8 * 4 * block * model_dim, transcendentals=0),
            )
            grads = place_blocks(*blocks, *others, *grads)

        out_y = project(lefts[1], w_o)
        grad_x = (back_proj(rights[0], w_q) + back_proj(rights[1], w_k) + back_proj(rights[2], w_v)).astype(BF16)
        return (out_y, grad_x) + tuple(grads)

    return jax.shard_map(local_layer, mesh=mesh, in_specs=(row_spec, P(), P(), P(), P(), row_spec), out_specs=(row_spec, row_spec, grad_spec, grad_spec, grad_spec, grad_spec), check_vma=False)
```

time: 1900 us -> 561 us (0.30)
  waiting for transfers between devices: 1360 us -> 240 us
  starting transfers between devices: 206 us -> 91.1 us
  other arithmetic: 111 us -> 13.9 us
  Pallas kernels: 0 us -> 86.2 us
  local copies, waits for them, and re-layouts: 87.4 us -> 24.8 us
  blocking collectives: 0 us -> 37.5 us
  matrix products: 99.8 us -> 64.7 us
    ppermute x62 -> x42, waiting for transfers between devices: 887 us -> 212 us  [the longest x26 211 us: hop(): return lax.ppermute(value, 'sp', perm=ring_perm(axis, hops))]
    psum x1 -> x0, waiting for transfers between devices: 474 us -> none  [local_layer(): lax.psum((weight_grad(tokens, dq_rows), weight_grad(tokens, dk_rows), wei...]
    ppermute x62 -> x42, starting transfers between devices: 206 us -> 88 us  [the longest x16 47.7 us: swap_cores(): return lax.ppermute(value, 'sp', perm=core_perm)]
    add x63 -> x4, other arithmetic: 108 us -> 7.92 us  [local_layer(): pieces[part] = own if step == 0 else pieces[part] + own]
    pallas_call x0 -> x7, Pallas kernels: none -> 86.2 us  [the longest x4 47.9 us: local_layer(): grads = place_blocks(*blocks, *others, *grads)]
    unnamed x60 -> x48, local copies, waits for them, and re-layouts: 74.6 us -> 10.2 us
    all_to_all x0 -> x1, blocking collectives: none -> 37.5 us  [local_layer(): parts = lax.all_to_all(totals, 'sp', 0, 0)]
    dot_general x24 -> x20, matrix products: 99.8 us -> 64.7 us  [the longest x16 46.4 us: block_product(): return jnp.einsum('nd,ne->de', left, right, preferred_element_type=F32)]
  transfers between devices with their start and end apart: 63 -> 43, of which waited for: 63 -> 16; matrix products, arithmetic and copies ran while one was open for 1% -> 15% of each run, Pallas kernels for 0% -> 6%
where the time goes in v1:
time: 561 us; the launch traced here: 560 us
  waiting for transfers between devices  240 us (43%)
  starting transfers between devices  91.1 us (16%)
  Pallas kernels  86.2 us (15%)
  matrix products  64.7 us (12%)
  blocking collectives  37.5 us (7%)
  local copies, waits for them, and re-layouts  24.8 us (4%)
  other arithmetic  13.9 us (2%)
    ppermute x26, waiting for transfers between devices, hop(): return lax.ppermute(value, 'sp', perm=ring_perm(axis, hops))  211 us
    pallas_call x4, Pallas kernels, local_layer(): grads = place_blocks(*blocks, *others, *grads)  47.9 us
    ppermute x16, starting transfers between devices, swap_cores(): return lax.ppermute(value, 'sp', perm=core_perm)  47.7 us
    dot_general x16, matrix products, block_product(): return jnp.einsum('nd,ne->de', left, right, preferred_element_type=F32)  46.4 us
    ppermute x26, starting transfers between devices, hop(): return lax.ppermute(value, 'sp', perm=ring_perm(axis, hops))  40.3 us
    all_to_all x1, blocking collectives, local_layer(): parts = lax.all_to_all(totals, 'sp', 0, 0)  37.5 us
    all_to_all x1, waiting for transfers between devices, local_layer(): states = lax.all_to_all(prefixes, 'sp', 0, 0)  28.5 us
    pallas_call x1, Pallas kernels, local_layer(): pl.pallas_call(project_kernel, grid=(model_dim // tile,), in_specs=[full,...  19.1 us
  transfers between devices with their start and end apart: 43, of which 16 were waited for; matrix products, arithmetic and copies ran while one was open for 15% of the time, Pallas kernels for 6%

profile of v1, /device:TPU:97, one launch (start us, length us, event | category | flops | bytes accessed | tf_op | source)
XLA Modules:
  0.0 560.3 jit_solution(7677886306876070524)
XLA Ops:
  1.9 19.1 %project.1 = (bf16[256,2048]{1,0:T(8,128)(2,1)S(1)}, bf16[256,2048]{1,0:T(8,128)(2,1)S(1)}, bf16[256,2048]{1,0:T(8,128)(2,1)S(1)}, bf16[256,2048]{1,0:T(8,128)(2,1)S(1)}, f32[32,2,64,128]{3,2,1,0:T(8,128)}) custom-call(bf16[256,2048]{1,0:T(8,128)(2,1)S(1)} %copy-done, bf16[256,2048]{1,0:T(8,128)(2,1)} %dy_ref.3, bf16[2048,2048]{1,0:T(8,128)(2,1)} %wq_ref.1, ...), custom_call_target="tpu_custom_call" | custom-call | flops 8589934592 | bytes 33554432 | tf_op jit(solution)/shard_map/project/pallas_call | solution.py:168
  24.8 37.5 %all_to_all.10.parts_ref = f32[32,2,64,128]{3,2,1,0:T(8,128)} all-to-all(f32[32,2,64,128]{3,2,1,0:T(8,128)} %get-tuple-element.33), channel_id=1, replica_groups=mesh['dp'=1,'sp'=32] {'sp'}, dimensions={0} | all-to-all | bytes 4194304 | tf_op jit(solution)/shard_map/all_to_all | solution.py:179
  68.7 28.5 %all-to-all-done.1.state_ref = f32[32,2,64,128]{3,2,1,0:T(8,128)S(1)} async-done(((f32[32,2,64,128]{3,2,1,0:T(8,128)}), f32[32,2,64,128]{3,2,1,0:T(8,128)S(1)}, u32[]{:S(2)}, u32[]{:S(2)}) %all-to-all-start.1) | async-done | bytes 2097184 | tf_op jit(solution)/shard_map/all_to_all | solution.py:188
  98.5 16.1 %attend.1 = (bf16[2,256,2048]{2,1,0:T(8,128)(2,1)}, bf16[4,256,2048]{2,1,0:T(8,128)(2,1)}) custom-call(bf16[256,2048]{1,0:T(8,128)(2,1)} %copy-done.1, bf16[256,2048]{1,0:T(8,128)(2,1)} %copy-done.2, bf16[256,2048]{1,0:T(8,128)(2,1)} %copy-done.3, bf16[256,2048]{1,0:T(8,128)(2,1)} %copy-done.4, bf16[256,2048]{1,0:T(8,128)(2,1)} %x_ref.3, ...), custom_call_target="tpu_custom_call" | custom-call | flops 1610612736 | bytes 16777216 | tf_op jit(solution)/shard_map/attend/pallas_call | solution.py:192
  114.6 8.1 %dynamic-slice_bitcast_fusion.6 = (bf16[256,2048]{1,0:T(8,128)(2,1)S(1)}, bf16[256,2048]{1,0:T(8,128)(2,1)S(1)}, bf16[256,2048]{1,0:T(8,128)(2,1)S(1)}, bf16[256...) fusion(bf16[4,256,2048]{2,1,0:T(8,128)(2,1)} %get-tuple-element, ...), kind=kLoop, calls=%fused_computation.50 | loop fusion | bytes 33554496 | tf_op jit(solution)/shard_map/jit(dynamic_index_in_dim)/squeeze | solution.py:207
  134.5 22.4 %collective-permute-done.18 = bf16[256,3072]{1,0:T(8,128)(2,1)S(1)} collective-permute-done((bf16[256,3072]{1,0:T(8,128)(2,1)S(1)}, bf16[256,3072]{1,0:T(8,128)(2,1)S(1)}, u32[]{:S(2)}, u32[]{:S(2)}) %collective-permute-start.18) | collective-permute-done | bytes 1572896 | tf_op jit(solution)/shard_map/ppermute | solution.py:149
  214.0 10.4 %add_add_fusion = f32[512,2048]{1,0:T(8,128)} fusion(f32[512,2048]{1,0:T(8,128)} %fusion.1, f32[512,2048]{1,0:T(8,128)} %fusion.3, f32[512,2048]{1,0:T(8,128)} %fusion.35, f32[512,2048]{1,0:T(8,128)} %fusion.5, f32[512,2048]{1,0:T(8,128)S(1)} %fusion.37, f32[512,2048]{1,0:T(8,128)S(1)} %fusion.39, f32[512,2048]{1,0:T(8,128)S(1)} %fusion.7, ...), kind=kOutput, calls=%fused_computation | convolution fusion | flops 544210944 | bytes 34865156 | tf_op jit(solution)/shard_map/nd,ne->de/dot_general | solution.py:219
  229.5 8.0 %add_add_fusion.1 = f32[512,2048]{1,0:T(8,128)} fusion(f32[512,2048]{1,0:T(8,128)S(1)} %fusion.9, f32[512,2048]{1,0:T(8,128)} %fusion.11, f32[512,2048]{1,0:T(8,128)S(1)} %copy-done.7, f32[512,2048]{1,0:T(8,128)} %fusion.13, f32[512,2048]{1,0:T(8,128)S(1)} %copy-done.6, f32[512,2048]{1,0:T(8,128)S(1)} %fusion.46, f32[512,2048]{1,0:T(8,128)S(1)} %fusion.15, ...), kind=kOutput, calls=%fused_computation.1 | convolution fusion | flops 544210944 | bytes 34865156 | tf_op jit(solution)/shard_map/nd,ne->de/dot_general | solution.py:219
  243.9 9.1 %collective-permute-done.8 = f32[128,2048]{1,0:T(8,128)S(1)} collective-permute-done((f32[128,2048]{1,0:T(8,128)S(1)}, f32[128,2048]{1,0:T(8,128)S(1)}, u32[]{:S(2)}, u32[]{:S(2)}) %collective-permute-start.8) | collective-permute-done | bytes 1048608 | tf_op jit(solution)/shard_map/ppermute | solution.py:149
  260.6 10.2 %collective-permute-done.9 = f32[128,2048]{1,0:T(8,128)S(1)} collective-permute-done((f32[128,2048]{1,0:T(8,128)}, f32[128,2048]{1,0:T(8,128)S(1)}, u32[]{:S(2)}, u32[]{:S(2)}) %collective-permute-start.9) | collective-permute-done | bytes 1048608 | tf_op jit(solution)/shard_map/ppermute | solution.py:149
  278.5 10.0 %collective-permute-done.10 = f32[128,2048]{1,0:T(8,128)S(1)} collective-permute-done((f32[128,2048]{1,0:T(8,128)}, f32[128,2048]{1,0:T(8,128)S(1)}, u32[]{:S(2)}, u32[]{:S(2)}) %collective-permute-start.10) | collective-permute-done | bytes 1048608 | tf_op jit(solution)/shard_map/ppermute | solution.py:149
  294.1 11.7 %collective-permute-done.11 = f32[128,2048]{1,0:T(8,128)S(1)} collective-permute-done((f32[128,2048]{1,0:T(8,128)S(1)}, f32[128,2048]{1,0:T(8,128)S(1)}, u32[]{:S(2)}, u32[]{:S(2)}) %collective-permute-start.11) | collective-permute-done | bytes 1048608 | tf_op jit(solution)/shard_map/ppermute | solution.py:149
  309.2 11.7 %collective-permute-done.12 = f32[128,2048]{1,0:T(8,128)S(1)} collective-permute-done((f32[128,2048]{1,0:T(8,128)S(1)}, f32[128,2048]{1,0:T(8,128)S(1)}, u32[]{:S(2)}, u32[]{:S(2)}) %collective-permute-start.12) | collective-permute-done | bytes 1048608 | tf_op jit(solution)/shard_map/ppermute | solution.py:149
  325.1 11.0 %collective-permute-done.13 = f32[128,2048]{1,0:T(8,128)S(1)} collective-permute-done((f32[128,2048]{1,0:T(8,128)S(1)}, f32[128,2048]{1,0:T(8,128)S(1)}, u32[]{:S(2)}, u32[]{:S(2)}) %collective-permute-start.13) | collective-permute-done | bytes 1048608 | tf_op jit(solution)/shard_map/ppermute | solution.py:149
  336.4 44.7 %collective-permute-done.31.refs_1_ = f32[512,2048]{1,0:T(8,128)S(1)} collective-permute-done((f32[512,2048]{1,0:T(8,128)S(1)}, f32[512,2048]{1,0:T(8,128)S(1)}, u32[]{:S(2)}, u32[]{:S(2)}) %collective-permute-start.31) | collective-permute-done | bytes 4194336 | tf_op jit(solution)/shard_map/ppermute | solution.py:149
  385.2 8.4 %collective-permute-start.41 = (f32[512,2048]{1,0:T(8,128)S(1)}, f32[512,2048]{1,0:T(8,128)S(1)}, u32[]{:S(2)}, u32[]{:S(2)}) collective-permute-start(f32[512,2048]{1,0:T(8,128)S(1)} %constant_dynamic-update-slice_fusion.refs_1_), channel_id=1, source_target_pairs={{0,1},{1,0},{2,3},{3,2},{4,5},{5,4},{6,7},{7,6},{8,9},{9,8},{10,11... | collective-permute-start | bytes 12582920 | tf_op jit(solution)/shard_map/ppermute | solution.py:146
  394.2 35.9 %collective-permute-done.32.refs_1_ = f32[512,2048]{1,0:T(8,128)} collective-permute-done((f32[512,2048]{1,0:T(8,128)S(1)}, f32[512,2048]{1,0:T(8,128)}, u32[]{:S(2)}, u32[]{:S(2)}) %collective-permute-start.32) | collective-permute-done | bytes 4194336 | tf_op jit(solution)/shard_map/ppermute | solution.py:149
  434.4 9.4 %collective-permute-start.38 = (f32[512,2048]{1,0:T(8,128)}, f32[512,2048]{1,0:T(8,128)}, u32[]{:S(2)}, u32[]{:S(2)}) collective-permute-start(f32[512,2048]{1,0:T(8,128)} %collective-permute-done.14.refs_0_), channel_id=1, source_target_pairs={{0,1},{1,0},{2,3},{3,2},{4,5},{5,4},{6,7},{7,6},{8,9},{9,8},{10,11... | collective-permute-start | bytes 12582920 | tf_op jit(solution)/shard_map/ppermute | solution.py:146
  446.7 32.6 %collective-permute-done.33.refs_1_ = f32[512,2048]{1,0:T(8,128)} collective-permute-done((f32[512,2048]{1,0:T(8,128)}, f32[512,2048]{1,0:T(8,128)}, u32[]{:S(2)}, u32[]{:S(2)}) %collective-permute-start.33) | collective-permute-done | bytes 4194336 | tf_op jit(solution)/shard_map/ppermute | solution.py:149
  479.3 9.1 %collective-permute-start.35 = (f32[512,2048]{1,0:T(8,128)}, f32[512,2048]{1,0:T(8,128)}, u32[]{:S(2)}, u32[]{:S(2)}) collective-permute-start(f32[512,2048]{1,0:T(8,128)} %collective-permute-done.33.refs_1_), channel_id=1, source_target_pairs={{0,1},{1,0},{2,3},{3,2},{4,5},{5,4},{6,7},{7,6},{8,9},{9,8},{10,11... | collective-permute-start | bytes 12582920 | tf_op jit(solution)/shard_map/ppermute | solution.py:146
  512.1 12.0 %shard_map.109 = (f32[2048,2048]{1,0:T(8,128)}, f32[2048,2048]{1,0:T(8,128)}, f32[2048,2048]{1,0:T(8,128)}, f32[2048,2048]{1,0:T(8,128)}) custom-call(f32[512,2048]{1,0:T(8,128)} %copy-done.14, f32[512,2048]{1,0:T(8,128)} %copy-done.15, f32[512,2048]{1,0:T(8,128)} %copy-done.19, f32[512,2048]{1,0:T(8,128)} %copy-done.18), custom_call_target="tpu_custom_call" | custom-call | flops 5000000000 | bytes 33554432 | tf_op jit(solution)/shard_map/pallas_call | solution.py:267
  524.1 12.0 %shard_map.110 = (f32[2048,2048]{1,0:T(8,128)}, f32[2048,2048]{1,0:T(8,128)}, f32[2048,2048]{1,0:T(8,128)}, f32[2048,2048]{1,0:T(8,128)}) custom-call(f32[512,2048]{1,0:T(8,128)} %collective-permute-done.14.refs_0_, f32[512,2048]{1,0:T(8,128)} %copy-done.12, ...), custom_call_target="tpu_custom_call", output_to_operand_aliasing={{0}: (4, {}), {1}: (5, {}), {2}: (6, {}), {3}: (7, {})} | custom-call | flops 5000000000 | bytes 33554432 | tf_op jit(solution)/shard_map/pallas_call | solution.py:267
  536.1 12.0 %shard_map.111 = (f32[2048,2048]{1,0:T(8,128)}, f32[2048,2048]{1,0:T(8,128)}, f32[2048,2048]{1,0:T(8,128)}, f32[2048,2048]{1,0:T(8,128)}) custom-call(f32[512,2048]{1,0:T(8,128)} %collective-permute-done.15.refs_0_, f32[512,2048]{1,0:T(8,128)} %collective-permute-done.32.refs_1_, ...), custom_call_target="tpu_custom_call", output_to_operand_aliasing={{0}: (4, {}), {1}: (5, {}), {2}: (6, {}), {3}: (7, {})} | custom-call | flops 5000000000 | bytes 33554432 | tf_op jit(solution)/shard_map/pallas_call | solution.py:267
  548.1 12.0 %shard_map.112 = (f32[2048,2048]{1,0:T(8,128)}, f32[2048,2048]{1,0:T(8,128)}, f32[2048,2048]{1,0:T(8,128)}, f32[2048,2048]{1,0:T(8,128)}) custom-call(f32[512,2048]{1,0:T(8,128)} %collective-permute-done.16.refs_0_, f32[512,2048]{1,0:T(8,128)} %collective-permute-done.33.refs_1_, ...), custom_call_target="tpu_custom_call", output_to_operand_aliasing={{0}: (4, {}), {1}: (5, {}), {2}: (6, {}), {3}: (7, {})} | custom-call | flops 5000000000 | bytes 33554432 | tf_op jit(solution)/shard_map/pallas_call | solution.py:267
  (199 shorter events, 156.4 us)
Async XLA Ops:
  65.4 31.9 %all-to-all-start.1 = ((f32[32,2,64,128]{3,2,1,0:T(8,128)}), f32[32,2,64,128]{3,2,1,0:T(8,128)S(1)}, u32[]{:S(2)}, u32[]{:S(2)}) async-start(f32[32,2,64,128]{3,2,1,0:T(8,128)} %state_prefix.1), calls=%async_computation.1 | async-start | bytes 4194304 | tf_op jit(solution)/shard_map/all_to_all | solution.py:188
  122.9 34.0 %collective-permute-start.18 = (bf16[256,3072]{1,0:T(8,128)(2,1)S(1)}, bf16[256,3072]{1,0:T(8,128)(2,1)S(1)}, u32[]{:S(2)}, u32[]{:S(2)}) collective-permute-start(bf16[256,3072]{1,0:T(8,128)(2,1)S(1)} %pad_maximum_fusion.3), channel_id=1, source_target_pairs={{0,8},{1,25},{2,10},{3,27},{4,12},{5,29},{6,14},{7,31},{8,16},{9,1... | collective-permute-start | bytes 4718600 | tf_op jit(solution)/shard_map/ppermute | solution.py:149
  123.2 37.5 %collective-permute-start.20 = (bf16[256,3072]{1,0:T(8,128)(2,1)S(1)}, bf16[256,3072]{1,0:T(8,128)(2,1)S(1)}, u32[]{:S(2)}, u32[]{:S(2)}) collective-permute-start(bf16[256,3072]{1,0:T(8,128)(2,1)S(1)} %pad_maximum_fusion.4), channel_id=1, source_target_pairs={{0,24},{1,9},{2,26},{3,11},{4,28},{5,13},{6,30},{7,15},{8,0},{9,17... | collective-permute-start | bytes 4718600 | tf_op jit(solution)/shard_map/ppermute | solution.py:149
  124.9 51.4 %collective-permute-start.22 = (bf16[256,3072]{1,0:T(8,128)(2,1)S(1)}, bf16[256,3072]{1,0:T(8,128)(2,1)S(1)}, u32[]{:S(2)}, u32[]{:S(2)}) collective-permute-start(bf16[256,3072]{1,0:T(8,128)(2,1)S(1)} %pad_maximum_fusion.5), channel_id=1, source_target_pairs={{0,8},{1,25},{2,10},{3,27},{4,12},{5,29},{6,14},{7,31},{8,16},{9,1... | collective-permute-start | bytes 4718600 | tf_op jit(solution)/shard_map/ppermute | solution.py:149
  131.5 33.7 %collective-permute-start.1 = (bf16[256,3072]{1,0:T(8,128)(2,1)S(1)}, bf16[256,3072]{1,0:T(8,128)(2,1)S(1)}, u32[]{:S(2)}, u32[]{:S(2)}) collective-permute-start(bf16[256,3072]{1,0:T(8,128)(2,1)S(1)} %pad_maximum_fusion), channel_id=1, source_target_pairs={{0,2},{1,7},{2,4},{3,1},{4,6},{5,3},{6,0},{7,5},{8,10},{9,15},{10,... | collective-permute-start | bytes 4718600 | tf_op jit(solution)/shard_map/ppermute | solution.py:149
  133.4 46.9 %collective-permute-start.3 = (bf16[256,3072]{1,0:T(8,128)(2,1)S(1)}, bf16[256,3072]{1,0:T(8,128)(2,1)S(1)}, u32[]{:S(2)}, u32[]{:S(2)}) collective-permute-start(bf16[256,3072]{1,0:T(8,128)(2,1)S(1)} %pad_maximum_fusion.1), channel_id=1, source_target_pairs={{0,6},{1,3},{2,0},{3,5},{4,2},{5,7},{6,4},{7,1},{8,14},{9,11},{10,... | collective-permute-start | bytes 4718600 | tf_op jit(solution)/shard_map/ppermute | solution.py:149
  156.9 30.3 %collective-permute-start.5 = (bf16[256,3072]{1,0:T(8,128)(2,1)S(1)}, bf16[256,3072]{1,0:T(8,128)(2,1)S(1)}, u32[]{:S(2)}, u32[]{:S(2)}) collective-permute-start(bf16[256,3072]{1,0:T(8,128)(2,1)S(1)} %pad_maximum_fusion.2), channel_id=1, source_target_pairs={{0,2},{1,7},{2,4},{3,1},{4,6},{5,3},{6,0},{7,5},{8,10},{9,15},{10,... | collective-permute-start | bytes 4718600 | tf_op jit(solution)/shard_map/ppermute | solution.py:149
  160.7 26.5 %collective-permute-start.19 = (bf16[256,2560]{1,0:T(8,128)(2,1)S(1)}, bf16[256,2560]{1,0:T(8,128)(2,1)S(1)}, u32[]{:S(2)}, u32[]{:S(2)}) collective-permute-start(bf16[256,2560]{1,0:T(8,128)(2,1)S(1)} %pad_maximum_fusion.11), channel_id=1, source_target_pairs={{0,1},{1,0},{2,3},{3,2},{4,5},{5,4},{6,7},{7,6},{8,9},{9,8},{10,11... | collective-permute-start | bytes 3932168 | tf_op jit(solution)/shard_map/ppermute | solution.py:146
  165.2 36.0 %collective-permute-start.21 = (bf16[256,2560]{1,0:T(8,128)(2,1)S(1)}, bf16[256,2560]{1,0:T(8,128)(2,1)S(1)}, u32[]{:S(2)}, u32[]{:S(2)}) collective-permute-start(bf16[256,2560]{1,0:T(8,128)(2,1)S(1)} %pad_maximum_fusion.12), channel_id=1, source_target_pairs={{0,1},{1,0},{2,3},{3,2},{4,5},{5,4},{6,7},{7,6},{8,9},{9,8},{10,11... | collective-permute-start | bytes 3932168 | tf_op jit(solution)/shard_map/ppermute | solution.py:146
  180.3 23.7 %collective-permute-start.2 = (bf16[256,2560]{1,0:T(8,128)(2,1)S(1)}, bf16[256,2560]{1,0:T(8,128)(2,1)S(1)}, u32[]{:S(2)}, u32[]{:S(2)}) collective-permute-start(bf16[256,2560]{1,0:T(8,128)(2,1)S(1)} %pad_maximum_fusion.7), channel_id=1, source_target_pairs={{0,1},{1,0},{2,3},{3,2},{4,5},{5,4},{6,7},{7,6},{8,9},{9,8},{10,11... | collective-permute-start | bytes 3932168 | tf_op jit(solution)/shard_map/ppermute | solution.py:146
  325.0 56.1 %collective-permute-start.31 = (f32[512,2048]{1,0:T(8,128)S(1)}, f32[512,2048]{1,0:T(8,128)S(1)}, u32[]{:S(2)}, u32[]{:S(2)}) collective-permute-start(f32[512,2048]{1,0:T(8,128)S(1)} %constant_dynamic-update-slice_fusion.refs_1_), channel_id=1, source_target_pairs={{0,8},{1,25},{2,10},{3,27},{4,12},{5,29},{6,14},{7,31},{8,16},{9,1... | collective-permute-start | bytes 12582920 | tf_op jit(solution)/shard_map/ppermute | solution.py:149
  336.2 48.3 %collective-permute-start.14 = (f32[512,2048]{1,0:T(8,128)S(1)}, f32[512,2048]{1,0:T(8,128)}, u32[]{:S(2)}, u32[]{:S(2)}) collective-permute-start(f32[512,2048]{1,0:T(8,128)S(1)} %constant_dynamic-update-slice_fusion.4.refs_0_), channel_id=1, source_target_pairs={{0,2},{1,7},{2,4},{3,1},{4,6},{5,3},{6,0},{7,5},{8,10},{9,15},{10,... | collective-permute-start | bytes 12582920 | tf_op jit(solution)/shard_map/ppermute | solution.py:149
  381.1 49.0 %collective-permute-start.32 = (f32[512,2048]{1,0:T(8,128)S(1)}, f32[512,2048]{1,0:T(8,128)}, u32[]{:S(2)}, u32[]{:S(2)}) collective-permute-start(f32[512,2048]{1,0:T(8,128)S(1)} %collective-permute-done.31.refs_1_), channel_id=1, source_target_pairs={{0,8},{1,25},{2,10},{3,27},{4,12},{5,29},{6,14},{7,31},{8,16},{9,1... | collective-permute-start | bytes 12582920 | tf_op jit(solution)/shard_map/ppermute | solution.py:149
  384.6 49.0 %collective-permute-start.15 = (f32[512,2048]{1,0:T(8,128)}, f32[512,2048]{1,0:T(8,128)}, u32[]{:S(2)}, u32[]{:S(2)}) collective-permute-start(f32[512,2048]{1,0:T(8,128)} %collective-permute-done.14.refs_0_), channel_id=1, source_target_pairs={{0,2},{1,7},{2,4},{3,1},{4,6},{5,3},{6,0},{7,5},{8,10},{9,15},{10,... | collective-permute-start | bytes 12582920 | tf_op jit(solution)/shard_map/ppermute | solution.py:149
  385.2 49.2 %collective-permute-start.41 = (f32[512,2048]{1,0:T(8,128)S(1)}, f32[512,2048]{1,0:T(8,128)S(1)}, u32[]{:S(2)}, u32[]{:S(2)}) collective-permute-start(f32[512,2048]{1,0:T(8,128)S(1)} %constant_dynamic-update-slice_fusion.refs_1_), channel_id=1, source_target_pairs={{0,1},{1,0},{2,3},{3,2},{4,5},{5,4},{6,7},{7,6},{8,9},{9,8},{10,11... | collective-permute-start | bytes 12582920 | tf_op jit(solution)/shard_map/ppermute | solution.py:146
  393.7 50.1 %collective-permute-start.40 = (f32[512,2048]{1,0:T(8,128)S(1)}, f32[512,2048]{1,0:T(8,128)S(1)}, u32[]{:S(2)}, u32[]{:S(2)}) collective-permute-start(f32[512,2048]{1,0:T(8,128)S(1)} %constant_dynamic-update-slice_fusion.4.refs_0_), channel_id=1, source_target_pairs={{0,1},{1,0},{2,3},{3,2},{4,5},{5,4},{6,7},{7,6},{8,9},{9,8},{10,11... | collective-permute-start | bytes 12582920 | tf_op jit(solution)/shard_map/ppermute | solution.py:146
  393.7 50.3 %collective-permute-start.39 = (f32[512,2048]{1,0:T(8,128)S(1)}, f32[512,2048]{1,0:T(8,128)S(1)}, u32[]{:S(2)}, u32[]{:S(2)}) collective-permute-start(f32[512,2048]{1,0:T(8,128)S(1)} %collective-permute-done.31.refs_1_), channel_id=1, source_target_pairs={{0,1},{1,0},{2,3},{3,2},{4,5},{5,4},{6,7},{7,6},{8,9},{9,8},{10,11... | collective-permute-start | bytes 12582920 | tf_op jit(solution)/shard_map/ppermute | solution.py:146
  430.0 49.3 %collective-permute-start.33 = (f32[512,2048]{1,0:T(8,128)}, f32[512,2048]{1,0:T(8,128)}, u32[]{:S(2)}, u32[]{:S(2)}) collective-permute-start(f32[512,2048]{1,0:T(8,128)} %collective-permute-done.32.refs_1_), channel_id=1, source_target_pairs={{0,8},{1,25},{2,10},{3,27},{4,12},{5,29},{6,14},{7,31},{8,16},{9,1... | collective-permute-start | bytes 12582920 | tf_op jit(solution)/shard_map/ppermute | solution.py:149
  433.5 54.9 %collective-permute-start.16 = (f32[512,2048]{1,0:T(8,128)}, f32[512,2048]{1,0:T(8,128)}, u32[]{:S(2)}, u32[]{:S(2)}) collective-permute-start(f32[512,2048]{1,0:T(8,128)} %collective-permute-done.15.refs_0_), channel_id=1, source_target_pairs={{0,2},{1,7},{2,4},{3,1},{4,6},{5,3},{6,0},{7,5},{8,10},{9,15},{10,... | collective-permute-start | bytes 12582920 | tf_op jit(solution)/shard_map/ppermute | solution.py:149
  434.4 89.7 %collective-permute-start.38 = (f32[512,2048]{1,0:T(8,128)}, f32[512,2048]{1,0:T(8,128)}, u32[]{:S(2)}, u32[]{:S(2)}) collective-permute-start(f32[512,2048]{1,0:T(8,128)} %collective-permute-done.14.refs_0_), channel_id=1, source_target_pairs={{0,1},{1,0},{2,3},{3,2},{4,5},{5,4},{6,7},{7,6},{8,9},{9,8},{10,11... | collective-permute-start | bytes 12582920 | tf_op jit(solution)/shard_map/ppermute | solution.py:146
  443.8 92.3 %collective-permute-start.37 = (f32[512,2048]{1,0:T(8,128)}, f32[512,2048]{1,0:T(8,128)}, u32[]{:S(2)}, u32[]{:S(2)}) collective-permute-start(f32[512,2048]{1,0:T(8,128)} %collective-permute-done.32.refs_1_), channel_id=1, source_target_pairs={{0,1},{1,0},{2,3},{3,2},{4,5},{5,4},{6,7},{7,6},{8,9},{9,8},{10,11... | collective-permute-start | bytes 12582920 | tf_op jit(solution)/shard_map/ppermute | solution.py:146
  446.0 90.0 %collective-permute-start.36 = (f32[512,2048]{1,0:T(8,128)}, f32[512,2048]{1,0:T(8,128)}, u32[]{:S(2)}, u32[]{:S(2)}) collective-permute-start(f32[512,2048]{1,0:T(8,128)} %collective-permute-done.15.refs_0_), channel_id=1, source_target_pairs={{0,1},{1,0},{2,3},{3,2},{4,5},{5,4},{6,7},{7,6},{8,9},{9,8},{10,11... | collective-permute-start | bytes 12582920 | tf_op jit(solution)/shard_map/ppermute | solution.py:146
  479.3 68.8 %collective-permute-start.35 = (f32[512,2048]{1,0:T(8,128)}, f32[512,2048]{1,0:T(8,128)}, u32[]{:S(2)}, u32[]{:S(2)}) collective-permute-start(f32[512,2048]{1,0:T(8,128)} %collective-permute-done.33.refs_1_), channel_id=1, source_target_pairs={{0,1},{1,0},{2,3},{3,2},{4,5},{5,4},{6,7},{7,6},{8,9},{9,8},{10,11... | collective-permute-start | bytes 12582920 | tf_op jit(solution)/shard_map/ppermute | solution.py:146
  488.4 59.7 %collective-permute-start.34 = (f32[512,2048]{1,0:T(8,128)}, f32[512,2048]{1,0:T(8,128)}, u32[]{:S(2)}, u32[]{:S(2)}) collective-permute-start(f32[512,2048]{1,0:T(8,128)} %collective-permute-done.16.refs_0_), channel_id=1, source_target_pairs={{0,1},{1,0},{2,3},{3,2},{4,5},{5,4},{6,7},{7,6},{8,9},{9,8},{10,11... | collective-permute-start | bytes 12582920 | tf_op jit(solution)/shard_map/ppermute | solution.py:146
  (43 other events, 1763.2 us)

commit v2 on v1

--- a/solution.py
+++ b/solution.py
@@ -17,6 +17,7 @@
 F32 = jnp.float32
 BF16 = jnp.bfloat16
 VMEM = pltpu.VMEM
+MESH = pl.DeviceIdType.MESH
 
 
 def dot(a, b, dims):
@@ -75,6 +76,159 @@
         right_ref[0, rows[b]] = ((dot(d_att, k, (1, 0)) + dot(do, s, (1, 1))) * scale).astype(BF16)
         right_ref[1, rows[b]] = ((dot(d_att, q, (0, 0)) + dot(v, r, (1, 1))) * scale).astype(BF16)
         right_ref[2, rows[b]] = ((dot(att, do, (0, 0)) + dot(k, r, (1, 0))) * scale).astype(BF16)
+
+
+def exchange_kernel(side, halves, left_ref, right_ref, out0_ref, out1_ref, near_left, near_right, far_left, far_right, pair_left, pair_right, total, landed, gathered, send_sem, recv_sem, ring_send, ring_recv, out_sem):
+    me = lax.axis_index("sp")
+    core = lax.rem(me, N_CORES)
+    sign = 1 - 2 * core
+    col = lax.rem(me // N_CORES, side)
+    row = me // (N_CORES * side)
+
+    def wrap(value):
+        return lax.rem(value + 2 * side, side)
+
+    def device(r, c):
+        return (r * side + c) * N_CORES + core
+
+    ahead = (device(row, wrap(col + sign)), device(wrap(row + sign), col))
+    behind = (device(row, wrap(col - sign)), device(wrap(row - sign), col))
+    partner = me + sign
+    at = (col, row)
+
+    barrier = pltpu.get_barrier_semaphore()
+    for other in ahead + behind + (partner,):
+        pl.semaphore_signal(barrier, inc=1, device_id={"sp": other}, device_id_type=MESH)
+    pl.semaphore_wait(barrier, 5)
+
+    half = left_ref.shape[2] // 2
+    block = half // N_CORES
+    outs = (out0_ref, out1_ref)
+
+    def send(src, dst, send, recv, target):
+        copy = pltpu.make_async_remote_copy(src_ref=src, dst_ref=dst, send_sem=send, recv_sem=recv, device_id={"sp": target}, device_id_type=MESH)
+        copy.start()
+        return copy
+
+    def send_pair(part, kind, left, right, left_dst, right_dst, target):
+        return (
+            send(right, right_dst, send_sem.at[part, kind, 1], recv_sem.at[part, kind, 1], target),
+            send(left, left_dst, send_sem.at[part, kind, 0], recv_sem.at[part, kind, 0], target),
+        )
+
+    def left_half(which, part):
+        return left_ref.at[which // (N_GRADS - 1), :, pl.ds(part * half, half)]
+
+    def own_left(part, owner):
+        start = pl.multiple_of(part * half + owner * block, block)
+        return left_ref.at[at[part] // (N_GRADS - 1), :, pl.ds(start, block)]
+
+    copies = {}
+    for part in range(2):
+        which = wrap(at[part] + 2)
+        copies[part, 3] = send_pair(part, 3, left_half(which, part), right_ref.at[which], far_left.at[part], far_right.at[part], ahead[part])
+    for part in range(2):
+        which = wrap(at[part] - sign)
+        copies[part, 1] = send_pair(part, 1, left_half(which, part), right_ref.at[which], near_left.at[part, 1], near_right.at[part, 1], behind[part])
+        copies[part, 7] = send_pair(part, 7, own_left(part, 1 - core), right_ref.at[at[part]], pair_left.at[part, 3], pair_right.at[part, 3], partner)
+    for part in range(2):
+        which = wrap(at[part] + sign)
+        copies[part, 0] = send_pair(part, 0, left_half(which, part), right_ref.at[which], near_left.at[part, 0], near_right.at[part, 0], ahead[part])
+
+    def wait_pair(part, kind):
+        for copy in copies[part, kind]:
+            copy.wait_recv()
+
+    n_tiles = 4
+    width = total.shape[2] // n_tiles
+
+    def accumulate(part, left, right, fresh=False):
+        left_value = left[...]
+
+        def tile(t, carry):
+            cols = pl.ds(pl.multiple_of(t * width, width), width)
+            product = dot(left_value, right[:, cols], (0, 0))
+            if fresh:
+                total[part, :, cols] = product
+            else:
+                total[part, :, cols] += product
+            return carry
+
+        lax.fori_loop(0, n_tiles, tile, 0)
+
+    def my_cols(owner):
+        return pl.ds(pl.multiple_of(owner * block, block), block)
+
+    def take(part, slot):
+        wait_pair(part, slot)
+        packet_left, packet_right = near_left.at[part, slot], near_right.at[part, slot]
+        copies[part, 4 + slot] = send_pair(part, 4 + slot, packet_left.at[:, my_cols(1 - core)], packet_right, pair_left.at[part, slot], pair_right.at[part, slot], partner)
+        accumulate(part, packet_left.at[:, my_cols(core)], packet_right)
+
+    def take_other(part, slot):
+        wait_pair(part, 4 + slot)
+        accumulate(part, pair_left.at[part, slot], pair_right.at[part, slot])
+
+    for part in range(2):
+        accumulate(part, own_left(part, core), right_ref.at[at[part]], fresh=True)
+    for part in range(2):
+        take_other(part, 3)
+    for part in range(2):
+        wait_pair(part, 3)
+        copies[part, 2] = send_pair(part, 2, far_left.at[part], far_right.at[part], near_left.at[part, 2], near_right.at[part, 2], ahead[part])
+    for slot in (1, 0, 2):
+        for part in range(2):
+            take(part, slot)
+        for part in range(2):
+            take_other(part, slot)
+
+    piece = block // side
+    small = piece // halves
+
+    def rows(part, shift, h):
+        return pl.ds(pl.multiple_of(wrap(at[1 - part] + sign * shift) * piece + h * small, small), small)
+
+    def ring(part, h, step, src, dst):
+        return send(src, dst, ring_send.at[part, h, step], ring_recv.at[part, h, step], ahead[1 - part])
+
+    lanes = [(part, h) for h in range(halves) for part in range(2)]
+    hops = {}
+    for part, h in lanes:
+        hops[part, h, 0] = ring(part, h, 0, total.at[part, rows(part, -1, h)], landed.at[part, h, 0])
+    for step in range(1, side - 1):
+        for part, h in lanes:
+            hops[part, h, step - 1].wait_recv()
+            landed[part, h, step - 1] += total[part, rows(part, -(step + 1), h), :]
+            hops[part, h, step] = ring(part, h, step, landed.at[part, h, step - 1], landed.at[part, h, step])
+    stores = []
+
+    def store(part, h, shift, n):
+        where = rows(part, shift, h)
+        copy = pltpu.make_async_copy(gathered.at[part, where], outs[part].at[where], out_sem.at[part, h, n])
+        copy.start()
+        stores.append(copy)
+
+    last = side - 1
+    for part, h in lanes:
+        hops[part, h, last - 1].wait_recv()
+        mine = rows(part, 0, h)
+        gathered[part, mine, :] = landed[part, h, last - 1] + total[part, mine, :]
+        hops[part, h, last] = ring(part, h, last, gathered.at[part, mine], gathered.at[part, mine])
+        store(part, h, 0, 0)
+    for step in range(1, side):
+        for part, h in lanes:
+            hops[part, h, last + step - 1].wait_recv()
+            where = rows(part, -step, h)
+            if step < side - 1:
+                hops[part, h, last + step] = ring(part, h, last + step, gathered.at[part, where], gathered.at[part, where])
+            store(part, h, -step, step)
+    for copy in stores:
+        copy.wait()
+    for pair in copies.values():
+        for copy in pair:
+            copy.wait_send()
+    for copy in hops.values():
+        copy.wait_send()
 
 
 def place_kernel(side, step, fresh, *refs):
@@ -139,7 +293,6 @@
         att_scale = 1.0 / math.sqrt(n_rows * n_seq * HEAD_DIM)
         index = lax.axis_index("sp")
         core = lax.rem(index, N_CORES)
-        sign = 1 - 2 * core
         place = {"x": lax.rem(index // N_CORES, side), "y": index // (N_CORES * side)}
 
         def swap_cores(value):
@@ -147,9 +300,6 @@
 
         def hop(value, axis, hops):
             return lax.ppermute(value, "sp", perm=ring_perm(axis, hops))
-
-        def at_shift(axis, shift):
-            return lax.rem(place[axis] + sign * shift + 2 * side, side)
 
         def project(operand, weight):
             return jnp.dot(operand, weight, preferred_element_type=F32).astype(BF16)
@@ -201,51 +351,36 @@
 
         half = model_dim // 2
         block = half // N_CORES
-
-        def packet(which, part):
-            left = lax.dynamic_index_in_dim(lefts, which // (N_GRADS - 1), 0, keepdims=False)[:, part * half : (part + 1) * half]
-            right = lax.dynamic_index_in_dim(rights, which, 0, keepdims=False)
-            return jnp.concatenate([left, right], axis=1)
-
+        halves = 2
+        small = block // side // halves
         axes = (("x", "y"), ("y", "x"))
-        received = []
-        for part, (first, second) in enumerate(axes):
-            far = hop(packet(at_shift(first, 2), part), first, 1)
-            near = hop(packet(at_shift(first, 1), part), first, 1)
-            back = hop(packet(at_shift(first, -1), part), first, -1)
-            received.append([packet(place[first], part), near, back, hop(far, first, 1)])
-
-        def block_product(left, right):
-            return jnp.einsum("nd,ne->de", left, right, preferred_element_type=F32)
-
-        sums = []
-        for part in range(2):
-            total = None
-            for pack in received[part]:
-                left, right = pack[:, :half], pack[:, half:]
-                mine = lax.dynamic_slice_in_dim(left, core * block, block, 1)
-                yours = lax.dynamic_slice_in_dim(left, (1 - core) * block, block, 1)
-                other = swap_cores(jnp.concatenate([yours, right], axis=1))
-                here = block_product(mine, right)
-                total = here if total is None else total + here
-                total = total + block_product(other[:, :block], other[:, block:])
-            sums.append(total)
-
-        piece = block // side
-        pieces = [None, None]
-        for step in range(side):
-            for part, (first, second) in enumerate(axes):
-                own = lax.dynamic_slice_in_dim(sums[part], at_shift(second, -(step + 1)) * piece, piece, 0)
-                pieces[part] = own if step == 0 else pieces[part] + own
-                if step < side - 1:
-                    pieces[part] = hop(pieces[part], second, 1)
-
-        blocks = [jnp.zeros((block, model_dim), F32) for _ in axes]
-        for step in range(side):
-            for part, (first, second) in enumerate(axes):
-                if step:
-                    pieces[part] = hop(pieces[part], second, 1)
-                blocks[part] = lax.dynamic_update_slice_in_dim(blocks[part], pieces[part], at_shift(second, -step) * piece, 0)
+        dma = pltpu.SemaphoreType.DMA
+        blocks = pl.pallas_call(
+            functools.partial(exchange_kernel, side, halves),
+            in_specs=[pl.BlockSpec(memory_space=VMEM)] * 2,
+            out_specs=[pl.BlockSpec(memory_space=pl.ANY)] * 2,
+            out_shape=[jax.ShapeDtypeStruct((block, model_dim), F32)] * 2,
+            scratch_shapes=[
+                VMEM((2, 3, n_rows, half), BF16),
+                VMEM((2, 3, n_rows, model_dim), BF16),
+                VMEM((2, n_rows, half), BF16),
+                VMEM((2, n_rows, model_dim), BF16),
+                VMEM((2, 4, n_rows, block), BF16),
+                VMEM((2, 4, n_rows, model_dim), BF16),
+                VMEM((2, block, model_dim), F32),
+                VMEM((2, halves, side - 1, small, model_dim), F32),
+                VMEM((2, block, model_dim), F32),
+                dma((2, 8, 2)),
+                dma((2, 8, 2)),
+                dma((2, halves, 2 * (side - 1))),
+                dma((2, halves, 2 * (side - 1))),
+                dma((2, halves, side)),
+            ],
+            cost_estimate=pl.CostEstimate(flops=2 * 2 * block * model_dim * n_rows * 8, bytes_accessed=2**24, transcendentals=0),
+            compiler_params=pltpu.CompilerParams(collective_id=1, has_side_effects=True, vmem_limit_bytes=60 * 2**20),
+            name="exchange",
+        )(lefts, rights)
+        blocks = list(blocks)
 
         grads = []
         granule = 128

time: 561 us -> 488 us (0.87)
  Pallas kernels: 86.2 us -> 237 us
  waiting for transfers between devices: 240 us -> 133 us
  starting transfers between devices: 91.1 us -> 19.4 us
  matrix products: 64.7 us -> 21.8 us
  blocking collectives: 37.5 us -> 69.9 us
  local copies, waits for them, and re-layouts: 24.8 us -> 5.14 us
  other arithmetic: 13.9 us -> 0.01 us
    pallas_call x0 -> x1, Pallas kernels: none -> 151 us  [local_layer(): pl.pallas_call(functools.partial(exchange_kernel, side, halves), in_specs...]
    ppermute x26 -> x6, waiting for transfers between devices: 211 us -> 133 us  [hop(): return lax.ppermute(value, 'sp', perm=ring_perm(axis, hops))]
    dot_general x16 -> x0, matrix products: 46.4 us -> none  [block_product(): return jnp.einsum('nd,ne->de', left, right, preferred_element_type=F32)]
    ppermute x16 -> x8, starting transfers between devices: 47.7 us -> 7.09 us  [swap_cores(): return lax.ppermute(value, 'sp', perm=core_perm)]
    all_to_all x0 -> x1, blocking collectives: none -> 32.4 us  [local_layer(): states = lax.all_to_all(prefixes, 'sp', 0, 0)]
    all_to_all x1 -> x0, waiting for transfers between devices: 28.5 us -> none  [local_layer(): states = lax.all_to_all(prefixes, 'sp', 0, 0)]
    ppermute x26 -> x6, starting transfers between devices: 40.3 us -> 12.3 us  [hop(): return lax.ppermute(value, 'sp', perm=ring_perm(axis, hops))]
    squeeze x1 -> x0, local copies, waits for them, and re-layouts: 8.09 us -> none  [packet(): right = lax.dynamic_index_in_dim(rights, which, 0, keepdims=False)]
  transfers between devices with their start and end apart: 43 -> 14, of which waited for: 16 -> 3; matrix products, arithmetic and copies ran while one was open for 15% -> 4% of each run, Pallas kernels for 6% -> 7%
where the time goes in v2:
time: 488 us; the launch traced here: 487 us
  Pallas kernels  237 us (49%)
  waiting for transfers between devices  133 us (27%)
  blocking collectives  69.9 us (14%)
  matrix products  21.8 us (4%)
  starting transfers between devices  19.4 us (4%)
  local copies, waits for them, and re-layouts  5.14 us (1%)
    pallas_call x1, Pallas kernels, local_layer(): pl.pallas_call(functools.partial(exchange_kernel, side, halves), in_specs...  151 us
    ppermute x6, waiting for transfers between devices, hop(): return lax.ppermute(value, 'sp', perm=ring_perm(axis, hops))  133 us
    pallas_call x4, Pallas kernels, local_layer(): grads = place_blocks(*blocks, *others, *grads)  47.9 us
    all_to_all x1, blocking collectives, local_layer(): parts = lax.all_to_all(totals, 'sp', 0, 0)  37.5 us
    all_to_all x1, blocking collectives, local_layer(): states = lax.all_to_all(prefixes, 'sp', 0, 0)  32.4 us
    pallas_call x1, Pallas kernels, local_layer(): pl.pallas_call(project_kernel, grid=(model_dim // tile,), in_specs=[full,...  19.1 us
    pallas_call x1, Pallas kernels, local_layer(): pl.pallas_call(functools.partial(attend_kernel, att_scale), grid=(n_heads...  16.1 us
    dot_general x3, matrix products, back_proj(): return jnp.einsum('ne,de->nd', rows, weight, preferred_element_type=F32)  14.9 us
  transfers between devices with their start and end apart: 14, of which 3 were waited for; matrix products, arithmetic and copies ran while one was open for 4% of the time, Pallas kernels for 7%

profile of v2, /device:TPU:97, one launch (start us, length us, event | category | flops | bytes accessed | tf_op | source)
XLA Modules:
  0.0 487.2 jit_solution(13619009826003769827)
XLA Ops:
  0.6 1.2 copy-done
  1.9 19.1 %project.1 = (bf16[256,2048]{1,0:T(8,128)(2,1)S(1)}, bf16[256,2048]{1,0:T(8,128)(2,1)S(1)}, bf16[256,2048]{1,0:T(8,128)(2,1)S(1)}, bf16[256,2048]{1,0:T(8,128)(2,1)S(1)}, f32[32,2,64,128]{3,2,1,0:T(8,128)}) custom-call(bf16[256,2048]{1,0:T(8,128)(2,1)S(1)} %copy-done, bf16[256,2048]{1,0:T(8,128)(2,1)} %dy_ref.3, bf16[2048,2048]{1,0:T(8,128)(2,1)} %wq_ref.1, ...), custom_call_target="tpu_custom_call" | custom-call | flops 8589934592 | bytes 33554432 | tf_op jit(solution)/shard_map/project/pallas_call | solution.py:318
  20.9 1.0 copy-done.1
  24.8 37.5 %all_to_all.10.parts_ref = f32[32,2,64,128]{3,2,1,0:T(8,128)} all-to-all(f32[32,2,64,128]{3,2,1,0:T(8,128)} %get-tuple-element.35), channel_id=1, replica_groups=mesh['dp'=1,'sp'=32] {'sp'}, dimensions={0} | all-to-all | bytes 4194304 | tf_op jit(solution)/shard_map/all_to_all | solution.py:329
  62.3 3.0 state_prefix.1
  65.4 32.4 %all_to_all.11.state_ref = f32[32,2,64,128]{3,2,1,0:T(8,128)} all-to-all(f32[32,2,64,128]{3,2,1,0:T(8,128)} %state_prefix.1), channel_id=1, replica_groups=mesh['dp'=1,'sp'=32] {'sp'}, dimensions={0} | all-to-all | bytes 4194304 | tf_op jit(solution)/shard_map/all_to_all | solution.py:338
  97.7 16.1 %attend.1 = (bf16[2,256,2048]{2,1,0:T(8,128)(2,1)}, bf16[4,256,2048]{2,1,0:T(8,128)(2,1)}) custom-call(bf16[256,2048]{1,0:T(8,128)(2,1)} %copy-done.1, bf16[256,2048]{1,0:T(8,128)(2,1)} %copy-done.2, bf16[256,2048]{1,0:T(8,128)(2,1)} %copy-done.3, bf16[256,2048]{1,0:T(8,128)(2,1)} %copy-done.4, bf16[256,2048]{1,0:T(8,128)(2,1)} %x_ref.3, ...), custom_call_target="tpu_custom_call" | custom-call | flops 1610612736 | bytes 16777216 | tf_op jit(solution)/shard_map/attend/pallas_call | solution.py:342
  113.8 151.0 %exchange.1 = (f32[512,2048]{1,0:T(8,128)}, f32[512,2048]{1,0:T(8,128)}) custom-call(bf16[2,256,2048]{2,1,0:T(8,128)(2,1)} %get-tuple-element.36.left_ref, bf16[4,256,2048]{2,1,0:T(8,128)(2,1)} %get-tuple-element.37.right_ref), custom_call_target="tpu_custom_call" | custom-call | flops 8589934592 | bytes 16777216 | tf_op jit(solution)/shard_map/exchange/pallas_call | solution.py:358
  264.9 2.7 collective-permute-start
  268.5 44.8 %collective-permute-done.refs_0_ = f32[512,2048]{1,0:T(8,128)S(1)} collective-permute-done((f32[512,2048]{1,0:T(8,128)}, f32[512,2048]{1,0:T(8,128)S(1)}, u32[]{:S(2)}, u32[]{:S(2)}) %collective-permute-start) | collective-permute-done | bytes 4194336 | tf_op jit(solution)/shard_map/ppermute | solution.py:302
  313.3 3.4 collective-permute-start.1
  318.0 44.2 %collective-permute-done.1.refs_0_ = f32[512,2048]{1,0:T(8,128)} collective-permute-done((f32[512,2048]{1,0:T(8,128)S(1)}, f32[512,2048]{1,0:T(8,128)}, u32[]{:S(2)}, u32[]{:S(2)}) %collective-permute-start.1) | collective-permute-done | bytes 4194336 | tf_op jit(solution)/shard_map/ppermute | solution.py:302
  362.2 3.5 collective-permute-start.2
  365.7 1.0 collective-permute-start.5
  367.6 43.8 %collective-permute-done.2.refs_0_ = f32[512,2048]{1,0:T(8,128)} collective-permute-done((f32[512,2048]{1,0:T(8,128)}, f32[512,2048]{1,0:T(8,128)}, u32[]{:S(2)}, u32[]{:S(2)}) %collective-permute-start.2) | collective-permute-done | bytes 4194336 | tf_op jit(solution)/shard_map/ppermute | solution.py:302
  411.5 5.1 %collective-permute-start.6 = (f32[512,2048]{1,0:T(8,128)}, f32[512,2048]{1,0:T(8,128)}, u32[]{:S(2)}, u32[]{:S(2)}) collective-permute-start(f32[512,2048]{1,0:T(8,128)} %collective-permute-done.2.refs_0_), channel_id=1, source_target_pairs={{0,1},{1,0},{2,3},{3,2},{4,5},{5,4},{6,7},{7,6},{8,9},{9,8},{10,11... | collective-permute-start | bytes 12582920 | tf_op jit(solution)/shard_map/ppermute | solution.py:299
  417.1 6.2 %fusion.3 = f32[256,2048]{1,0:T(8,128)S(1)} fusion(bf16[2048,2048]{1,0:T(8,128)(2,1)} %wq_ref.1, bf16[4,256,2048]{2,1,0:T(8,128)(2,1)} %get-tuple-element.37.right_ref), kind=kOutput, calls=%fused_computation.6 | convolution fusion | flops 2147483648 | bytes 11534336 | tf_op jit(solution)/shard_map/ne,de->nd/dot_general | solution.py:308
  423.4 6.9 %convolution_convert_fusion = bf16[256,2048]{1,0:T(8,128)(2,1)} fusion(bf16[2048,2048]{1,0:T(8,128)(2,1)} %wo_ref.1, bf16[2,256,2048]{2,1,0:T(8,128)(2,1)S(1)} %copy-done.10), kind=kOutput, calls=%fused_computation.3 | convolution fusion | flops 2148007936 | bytes 10485760 | tf_op jit(solution)/shard_map/dot_general | solution.py:305
  430.3 3.7 convolution_add_fusion.1
  434.0 5.0 %fusion = bf16[256,2048]{1,0:T(8,128)(2,1)} fusion(f32[256,2048]{1,0:T(8,128)} %convolution_add_fusion.1, bf16[2048,2048]{1,0:T(8,128)(2,1)S(1)} %bitcast.19, bf16[4,256,2048]{2,1,0:T(8,128)(2,1)S(1)} %copy-done.7), kind=kOutput, calls=%fused_computation.2 | convolution fusion | flops 2148532224 | bytes 12582912 | tf_op jit(solution)/shard_map/ne,de->nd/dot_general | solution.py:308
  439.0 12.0 %shard_map.109 = (f32[2048,2048]{1,0:T(8,128)}, f32[2048,2048]{1,0:T(8,128)}, f32[2048,2048]{1,0:T(8,128)}, f32[2048,2048]{1,0:T(8,128)}) custom-call(f32[512,2048]{1,0:T(8,128)} %get-tuple-element.38.refs_0_, f32[512,2048]{1,0:T(8,128)} %get-tuple-element.39.refs_1_, f32[512,2048]{1,0:T(8,128)} %copy-done.8, f32[512,2048]{1,0:T(8,128)} %copy-done.9), custom_call_target="tpu_custom_call" | custom-call | flops 5000000000 | bytes 33554432 | tf_op jit(solution)/shard_map/pallas_call | solution.py:402
  451.0 12.0 %shard_map.110 = (f32[2048,2048]{1,0:T(8,128)}, f32[2048,2048]{1,0:T(8,128)}, f32[2048,2048]{1,0:T(8,128)}, f32[2048,2048]{1,0:T(8,128)}) custom-call(f32[512,2048]{1,0:T(8,128)} %copy-done.5, f32[512,2048]{1,0:T(8,128)} %collective-permute-done.3.refs_1_, ...), custom_call_target="tpu_custom_call", output_to_operand_aliasing={{0}: (4, {}), {1}: (5, {}), {2}: (6, {}), {3}: (7, {})} | custom-call | flops 5000000000 | bytes 33554432 | tf_op jit(solution)/shard_map/pallas_call | solution.py:402
  463.0 12.0 %shard_map.111 = (f32[2048,2048]{1,0:T(8,128)}, f32[2048,2048]{1,0:T(8,128)}, f32[2048,2048]{1,0:T(8,128)}, f32[2048,2048]{1,0:T(8,128)}) custom-call(f32[512,2048]{1,0:T(8,128)} %collective-permute-done.1.refs_0_, f32[512,2048]{1,0:T(8,128)} %collective-permute-done.4.refs_1_, ...), custom_call_target="tpu_custom_call", output_to_operand_aliasing={{0}: (4, {}), {1}: (5, {}), {2}: (6, {}), {3}: (7, {})} | custom-call | flops 5000000000 | bytes 33554432 | tf_op jit(solution)/shard_map/pallas_call | solution.py:402
  475.0 12.0 %shard_map.112 = (f32[2048,2048]{1,0:T(8,128)}, f32[2048,2048]{1,0:T(8,128)}, f32[2048,2048]{1,0:T(8,128)}, f32[2048,2048]{1,0:T(8,128)}) custom-call(f32[512,2048]{1,0:T(8,128)} %collective-permute-done.2.refs_0_, f32[512,2048]{1,0:T(8,128)} %collective-permute-done.5.refs_1_, ...), custom_call_target="tpu_custom_call", output_to_operand_aliasing={{0}: (4, {}), {1}: (5, {}), {2}: (6, {}), {3}: (7, {})} | custom-call | flops 5000000000 | bytes 33554432 | tf_op jit(solution)/shard_map/pallas_call | solution.py:402
  (50 shorter events, 6.7 us)
Async XLA Ops:
  264.9 48.5 %collective-permute-start = (f32[512,2048]{1,0:T(8,128)}, f32[512,2048]{1,0:T(8,128)S(1)}, u32[]{:S(2)}, u32[]{:S(2)}) collective-permute-start(f32[512,2048]{1,0:T(8,128)} %get-tuple-element.38.refs_0_), channel_id=1, source_target_pairs={{0,2},{1,7},{2,4},{3,1},{4,6},{5,3},{6,0},{7,5},{8,10},{9,15},{10,... | collective-permute-start | bytes 12582920 | tf_op jit(solution)/shard_map/ppermute | solution.py:302
  267.6 155.8 %copy-start.10 = (bf16[2,256,2048]{2,1,0:T(8,128)(2,1)S(1)}, bf16[2,256,2048]{2,1,0:T(8,128)(2,1)}, u32[]{:S(2)}) copy-start(bf16[2,256,2048]{2,1,0:T(8,128)(2,1)} %get-tuple-element.36.left_ref) | copy-start | bytes 6291460
  267.6 49.2 %collective-permute-start.3 = (f32[512,2048]{1,0:T(8,128)}, f32[512,2048]{1,0:T(8,128)}, u32[]{:S(2)}, u32[]{:S(2)}) collective-permute-start(f32[512,2048]{1,0:T(8,128)} %get-tuple-element.39.refs_1_), channel_id=1, source_target_pairs={{0,8},{1,25},{2,10},{3,27},{4,12},{5,29},{6,14},{7,31},{8,16},{9,1... | collective-permute-start | bytes 12582920 | tf_op jit(solution)/shard_map/ppermute | solution.py:302
  313.3 103.2 %copy-start.5 = (f32[512,2048]{1,0:T(8,128)}, f32[512,2048]{1,0:T(8,128)S(1)}, u32[]{:S(2)}) copy-start(f32[512,2048]{1,0:T(8,128)S(1)} %collective-permute-done.refs_0_) | copy-start | bytes 12582916
  313.3 48.9 %collective-permute-start.1 = (f32[512,2048]{1,0:T(8,128)S(1)}, f32[512,2048]{1,0:T(8,128)}, u32[]{:S(2)}, u32[]{:S(2)}) collective-permute-start(f32[512,2048]{1,0:T(8,128)S(1)} %collective-permute-done.refs_0_), channel_id=1, source_target_pairs={{0,2},{1,7},{2,4},{3,1},{4,6},{5,3},{6,0},{7,5},{8,10},{9,15},{10,... | collective-permute-start | bytes 12582920 | tf_op jit(solution)/shard_map/ppermute | solution.py:302
  316.7 49.0 %collective-permute-start.4 = (f32[512,2048]{1,0:T(8,128)}, f32[512,2048]{1,0:T(8,128)}, u32[]{:S(2)}, u32[]{:S(2)}) collective-permute-start(f32[512,2048]{1,0:T(8,128)} %collective-permute-done.3.refs_1_), channel_id=1, source_target_pairs={{0,8},{1,25},{2,10},{3,27},{4,12},{5,29},{6,14},{7,31},{8,16},{9,1... | collective-permute-start | bytes 12582920 | tf_op jit(solution)/shard_map/ppermute | solution.py:302
  317.5 49.2 %collective-permute-start.12 = (f32[512,2048]{1,0:T(8,128)}, f32[512,2048]{1,0:T(8,128)S(1)}, u32[]{:S(2)}, u32[]{:S(2)}) collective-permute-start(f32[512,2048]{1,0:T(8,128)} %get-tuple-element.38.refs_0_), channel_id=1, source_target_pairs={{0,1},{1,0},{2,3},{3,2},{4,5},{5,4},{6,7},{7,6},{8,9},{9,8},{10,11... | collective-permute-start | bytes 12582920 | tf_op jit(solution)/shard_map/ppermute | solution.py:299
  317.5 49.6 %collective-permute-start.13 = (f32[512,2048]{1,0:T(8,128)}, f32[512,2048]{1,0:T(8,128)S(1)}, u32[]{:S(2)}, u32[]{:S(2)}) collective-permute-start(f32[512,2048]{1,0:T(8,128)} %get-tuple-element.39.refs_1_), channel_id=1, source_target_pairs={{0,1},{1,0},{2,3},{3,2},{4,5},{5,4},{6,7},{7,6},{8,9},{9,8},{10,11... | collective-permute-start | bytes 12582920 | tf_op jit(solution)/shard_map/ppermute | solution.py:299
  318.0 49.2 %collective-permute-start.10 = (f32[512,2048]{1,0:T(8,128)S(1)}, f32[512,2048]{1,0:T(8,128)S(1)}, u32[]{:S(2)}, u32[]{:S(2)}) collective-permute-start(f32[512,2048]{1,0:T(8,128)S(1)} %collective-permute-done.refs_0_), channel_id=1, source_target_pairs={{0,1},{1,0},{2,3},{3,2},{4,5},{5,4},{6,7},{7,6},{8,9},{9,8},{10,11... | collective-permute-start | bytes 12582920 | tf_op jit(solution)/shard_map/ppermute | solution.py:299
  362.2 49.3 %collective-permute-start.2 = (f32[512,2048]{1,0:T(8,128)}, f32[512,2048]{1,0:T(8,128)}, u32[]{:S(2)}, u32[]{:S(2)}) collective-permute-start(f32[512,2048]{1,0:T(8,128)} %collective-permute-done.1.refs_0_), channel_id=1, source_target_pairs={{0,2},{1,7},{2,4},{3,1},{4,6},{5,3},{6,0},{7,5},{8,10},{9,15},{10,... | collective-permute-start | bytes 12582920 | tf_op jit(solution)/shard_map/ppermute | solution.py:302
  365.7 50.9 %collective-permute-start.5 = (f32[512,2048]{1,0:T(8,128)}, f32[512,2048]{1,0:T(8,128)}, u32[]{:S(2)}, u32[]{:S(2)}) collective-permute-start(f32[512,2048]{1,0:T(8,128)} %collective-permute-done.4.refs_1_), channel_id=1, source_target_pairs={{0,8},{1,25},{2,10},{3,27},{4,12},{5,29},{6,14},{7,31},{8,16},{9,1... | collective-permute-start | bytes 12582920 | tf_op jit(solution)/shard_map/ppermute | solution.py:302
  366.7 49.9 %copy-start.8 = (f32[512,2048]{1,0:T(8,128)}, f32[512,2048]{1,0:T(8,128)S(1)}, u32[]{:S(2)}) copy-start(f32[512,2048]{1,0:T(8,128)S(1)} %collective-permute-done.12.refs_2_) | copy-start | bytes 12582916
  366.7 84.3 %collective-permute-start.11 = (f32[512,2048]{1,0:T(8,128)}, f32[512,2048]{1,0:T(8,128)}, u32[]{:S(2)}, u32[]{:S(2)}) collective-permute-start(f32[512,2048]{1,0:T(8,128)} %collective-permute-done.3.refs_1_), channel_id=1, source_target_pairs={{0,1},{1,0},{2,3},{3,2},{4,5},{5,4},{6,7},{7,6},{8,9},{9,8},{10,11... | collective-permute-start | bytes 12582920 | tf_op jit(solution)/shard_map/ppermute | solution.py:299
  367.1 49.5 %copy-start.9 = (f32[512,2048]{1,0:T(8,128)}, f32[512,2048]{1,0:T(8,128)S(1)}, u32[]{:S(2)}) copy-start(f32[512,2048]{1,0:T(8,128)S(1)} %collective-permute-done.13.refs_3_) | copy-start | bytes 12582916
  367.1 95.9 %collective-permute-start.8 = (f32[512,2048]{1,0:T(8,128)}, f32[512,2048]{1,0:T(8,128)}, u32[]{:S(2)}, u32[]{:S(2)}) collective-permute-start(f32[512,2048]{1,0:T(8,128)} %collective-permute-done.1.refs_0_), channel_id=1, source_target_pairs={{0,1},{1,0},{2,3},{3,2},{4,5},{5,4},{6,7},{7,6},{8,9},{9,8},{10,11... | collective-permute-start | bytes 12582920 | tf_op jit(solution)/shard_map/ppermute | solution.py:299
  367.3 49.3 %copy-start.6 = (f32[512,2048]{1,0:T(8,128)}, f32[512,2048]{1,0:T(8,128)S(1)}, u32[]{:S(2)}) copy-start(f32[512,2048]{1,0:T(8,128)S(1)} %collective-permute-done.10.refs_2_) | copy-start | bytes 12582916
  367.3 95.7 %collective-permute-start.9 = (f32[512,2048]{1,0:T(8,128)}, f32[512,2048]{1,0:T(8,128)}, u32[]{:S(2)}, u32[]{:S(2)}) collective-permute-start(f32[512,2048]{1,0:T(8,128)} %collective-permute-done.4.refs_1_), channel_id=1, source_target_pairs={{0,1},{1,0},{2,3},{3,2},{4,5},{5,4},{6,7},{7,6},{8,9},{9,8},{10,11... | collective-permute-start | bytes 12582920 | tf_op jit(solution)/shard_map/ppermute | solution.py:299
  411.5 63.5 %collective-permute-start.6 = (f32[512,2048]{1,0:T(8,128)}, f32[512,2048]{1,0:T(8,128)}, u32[]{:S(2)}, u32[]{:S(2)}) collective-permute-start(f32[512,2048]{1,0:T(8,128)} %collective-permute-done.2.refs_0_), channel_id=1, source_target_pairs={{0,1},{1,0},{2,3},{3,2},{4,5},{5,4},{6,7},{7,6},{8,9},{9,8},{10,11... | collective-permute-start | bytes 12582920 | tf_op jit(solution)/shard_map/ppermute | solution.py:299
  416.6 58.4 %collective-permute-start.7 = (f32[512,2048]{1,0:T(8,128)}, f32[512,2048]{1,0:T(8,128)}, u32[]{:S(2)}, u32[]{:S(2)}) collective-permute-start(f32[512,2048]{1,0:T(8,128)} %collective-permute-done.5.refs_1_), channel_id=1, source_target_pairs={{0,1},{1,0},{2,3},{3,2},{4,5},{5,4},{6,7},{7,6},{8,9},{9,8},{10,11... | collective-permute-start | bytes 12582920 | tf_op jit(solution)/shard_map/ppermute | solution.py:299
  417.1 13.1 %slice-start = ((s8[8388608]{0:T(1024)(128)(4,1)}), s8[4194304]{0:T(1024)(128)(4,1)S(1)}, s32[]{:S(2)}) async-start(s8[8388608]{0:T(1024)(128)(4,1)} %bitcast.16), calls=%async_computation.2 | async-start | bytes 8388608
  417.1 16.8 %slice-start.2 = ((s8[8388608]{0:T(1024)(128)(4,1)}), s8[4194304]{0:T(1024)(128)(4,1)S(1)}, s32[]{:S(2)}) async-start(s8[8388608]{0:T(1024)(128)(4,1)} %bitcast.18), calls=%async_computation.4 | async-start | bytes 8388608
  423.4 6.9 %slice-start.1 = ((s8[8388608]{0:T(1024)(128)(4,1)}), s8[4194304]{0:T(1024)(128)(4,1)S(1)}, s32[]{:S(2)}) async-start(s8[8388608]{0:T(1024)(128)(4,1)} %bitcast.16), calls=%async_computation.3 | async-start | bytes 8388608
  423.4 6.9 %copy-start.7 = (bf16[4,256,2048]{2,1,0:T(8,128)(2,1)S(1)}, bf16[4,256,2048]{2,1,0:T(8,128)(2,1)}, u32[]{:S(2)}) copy-start(bf16[4,256,2048]{2,1,0:T(8,128)(2,1)} %get-tuple-element.37.right_ref) | copy-start | bytes 12582916
  423.4 10.6 %slice-start.3 = ((s8[8388608]{0:T(1024)(128)(4,1)}), s8[4194304]{0:T(1024)(128)(4,1)S(1)}, s32[]{:S(2)}) async-start(s8[8388608]{0:T(1024)(128)(4,1)} %bitcast.18), calls=%async_computation.5 | async-start | bytes 8388608
  (5 other events, 5.1 us)

commit v3 on v2

--- a/solution.py
+++ b/solution.py
@@ -78,7 +78,10 @@
         right_ref[2, rows[b]] = ((dot(att, do, (0, 0)) + dot(k, r, (1, 0))) * scale).astype(BF16)
 
 
-def exchange_kernel(side, halves, left_ref, right_ref, out0_ref, out1_ref, near_left, near_right, far_left, far_right, pair_left, pair_right, total, landed, gathered, send_sem, recv_sem, ring_send, ring_recv, out_sem):
+def exchange_kernel(side, halves, left_ref, right_ref, *refs):
+    own_outs, other_outs = refs[: 2 * halves], refs[2 * halves : 4 * halves]
+    near_left, near_right, far_left, far_right, pair_left, pair_right, total, landed, gathered = refs[4 * halves : -7]
+    send_sem, recv_sem, ring_send, ring_recv, out_sem, swap_send, swap_recv = refs[-7:]
     me = lax.axis_index("sp")
     core = lax.rem(me, N_CORES)
     sign = 1 - 2 * core
@@ -103,7 +106,6 @@
 
     half = left_ref.shape[2] // 2
     block = half // N_CORES
-    outs = (out0_ref, out1_ref)
 
     def send(src, dst, send, recv, target):
         copy = pltpu.make_async_remote_copy(src_ref=src, dst_ref=dst, send_sem=send, recv_sem=recv, device_id={"sp": target}, device_id_type=MESH)
@@ -202,11 +204,15 @@
             hops[part, h, step] = ring(part, h, step, landed.at[part, h, step - 1], landed.at[part, h, step])
     stores = []
 
+    swaps = []
+
     def store(part, h, shift, n):
-        where = rows(part, shift, h)
-        copy = pltpu.make_async_copy(gathered.at[part, where], outs[part].at[where], out_sem.at[part, h, n])
+        src = gathered.at[part, rows(part, shift, h)]
+        where = pl.ds(pl.multiple_of(wrap(at[1 - part] + sign * shift) * small, small), small)
+        copy = pltpu.make_async_copy(src, own_outs[2 * h + part].at[where], out_sem.at[part, h, n])
         copy.start()
         stores.append(copy)
+        swaps.append(send(src, other_outs[2 * h + part].at[where], swap_send.at[part, h, n], swap_recv.at[part, h, n], partner))
 
     last = side - 1
     for part, h in lanes:
@@ -229,9 +235,11 @@
             copy.wait_send()
     for copy in hops.values():
         copy.wait_send()
-
-
-def place_kernel(side, step, fresh, *refs):
+    for copy in swaps:
+        copy.wait()
+
+
+def place_kernel(side, step, lane, halves, fresh, *refs):
     blocks = refs[:4]
     grads = refs[4 if fresh else 4 + N_GRADS :][:N_GRADS]
     buf, sem_in, sem_out = refs[-3:]
@@ -239,19 +247,18 @@
     core = lax.rem(index, N_CORES)
     col = lax.rem(index // N_CORES, side)
     row = index // (N_CORES * side)
-    height = blocks[0].shape[0]
+    small = blocks[0].shape[0] // side
+    piece = small * halves
     half = grads[0].shape[0] // 2
-    granule = buf.shape[1]
-    per_block = height // granule
     jobs = []
     for k, src in enumerate(blocks):
         own, part = k < 2, k % 2
         at = col if part == 0 else row
         c = core if own else 1 - core
         which = lax.rem(at - (1 - 2 * c) * step + 2 * side, side)
-        start = part * half + c * height
-        for g in range(per_block):
-            jobs.append((src.at[pl.ds(g * granule, granule)], which, pl.multiple_of(start + g * granule, granule)))
+        start = part * half + c * side * piece + lane * small
+        for g in range(side):
+            jobs.append((src.at[pl.ds(g * small, small)], which, pl.multiple_of(start + g * piece, small)))
     for n, (src, which, start) in enumerate(jobs):
         pltpu.make_async_copy(src, buf.at[n], sem_in.at[n]).start()
     for n, (src, which, start) in enumerate(jobs):
@@ -260,10 +267,10 @@
 
             @pl.when(which == m)
             def _():
-                pltpu.make_async_copy(buf.at[n], grads[m].at[pl.ds(start, granule)], sem_out.at[n]).start()
+                pltpu.make_async_copy(buf.at[n], grads[m].at[pl.ds(start, small)], sem_out.at[n]).start()
 
     for n, (src, which, start) in enumerate(jobs):
-        pltpu.make_async_copy(buf.at[n], grads[0].at[pl.ds(0, granule)], sem_out.at[n]).wait()
+        pltpu.make_async_copy(buf.at[n], grads[0].at[pl.ds(0, small)], sem_out.at[n]).wait()
 
 
 def solution(mesh):
@@ -358,8 +365,8 @@
         blocks = pl.pallas_call(
             functools.partial(exchange_kernel, side, halves),
             in_specs=[pl.BlockSpec(memory_space=VMEM)] * 2,
-            out_specs=[pl.BlockSpec(memory_space=pl.ANY)] * 2,
-            out_shape=[jax.ShapeDtypeStruct((block, model_dim), F32)] * 2,
+            out_specs=[pl.BlockSpec(memory_space=pl.ANY)] * (4 * halves),
+            out_shape=[jax.ShapeDtypeStruct((block // halves, model_dim), F32)] * (4 * halves),
             scratch_shapes=[
                 VMEM((2, 3, n_rows, half), BF16),
                 VMEM((2, 3, n_rows, model_dim), BF16),
@@ -375,31 +382,35 @@
                 dma((2, halves, 2 * (side - 1))),
                 dma((2, halves, 2 * (side - 1))),
                 dma((2, halves, side)),
+                dma((2, halves, side)),
+                dma((2, halves, side)),
             ],
             cost_estimate=pl.CostEstimate(flops=2 * 2 * block * model_dim * n_rows * 8, bytes_accessed=2**24, transcendentals=0),
             compiler_params=pltpu.CompilerParams(collective_id=1, has_side_effects=True, vmem_limit_bytes=60 * 2**20),
             name="exchange",
         )(lefts, rights)
-        blocks = list(blocks)
+        own = [list(blocks[2 * h : 2 * h + 2]) for h in range(halves)]
+        others = [list(blocks[2 * (halves + h) : 2 * (halves + h) + 2]) for h in range(halves)]
 
         grads = []
-        granule = 128
-        n_copies = 4 * block // granule
+        n_copies = 4 * side
         for step in range(side):
-            if step:
-                for part, (first, second) in enumerate(axes):
-                    blocks[part] = hop(blocks[part], first, 1)
-            others = [swap_cores(b) for b in blocks]
-            place_blocks = pl.pallas_call(
-                functools.partial(place_kernel, side, step, step == 0),
-                in_specs=[pl.BlockSpec(memory_space=pl.ANY)] * (4 + len(grads)),
-                out_specs=[pl.BlockSpec(memory_space=pl.ANY)] * N_GRADS,
-                out_shape=[jax.ShapeDtypeStruct((model_dim, model_dim), F32)] * N_GRADS,
-                scratch_shapes=[VMEM((n_copies, granule, model_dim), F32), pltpu.SemaphoreType.DMA((n_copies,)), pltpu.SemaphoreType.DMA((n_copies,))],
-                input_output_aliases={} if step == 0 else {4 + m: m for m in range(N_GRADS)},
-                cost_estimate=pl.CostEstimate(flops=5 * 10**9, bytes_accessed=8 * 4 * block * model_dim, transcendentals=0),
-            )
-            grads = place_blocks(*blocks, *others, *grads)
+            for h in range(halves):
+                if step:
+                    for part, (first, second) in enumerate(axes):
+                        own[h][part] = hop(own[h][part], first, 1)
+                    others[h] = [swap_cores(b) for b in own[h]]
+                fresh = not grads
+                place_blocks = pl.pallas_call(
+                    functools.partial(place_kernel, side, step, h, halves, fresh),
+                    in_specs=[pl.BlockSpec(memory_space=pl.ANY)] * (4 + len(grads)),
+                    out_specs=[pl.BlockSpec(memory_space=pl.ANY)] * N_GRADS,
+                    out_shape=[jax.ShapeDtypeStruct((model_dim, model_dim), F32)] * N_GRADS,
+                    scratch_shapes=[VMEM((n_copies, small, model_dim), F32), dma((n_copies,)), dma((n_copies,))],
+                    input_output_aliases={} if fresh else {4 + m: m for m in range(N_GRADS)},
+                    cost_estimate=pl.CostEstimate(flops=3 * 10**9, bytes_accessed=32 * n_copies * small * model_dim, transcendentals=0),
+                )
+                grads = place_blocks(*own[h], *others[h], *grads)
 
         out_y = project(lefts[1], w_o)
         grad_x = (back_proj(rights[0], w_q) + back_proj(rights[1], w_k) + back_proj(rights[2], w_v)).astype(BF16)

time: 488 us -> 465 us (0.953)
  waiting for transfers between devices: 133 us -> 88.6 us
  starting transfers between devices: 19.4 us -> 31.2 us
  Pallas kernels: 237 us -> 245 us
    ppermute x6 -> x12, waiting for transfers between devices: 133 us -> 88.4 us  [hop(): return lax.ppermute(value, 'sp', perm=ring_perm(axis, hops))]
    ppermute x8 -> x12, starting transfers between devices: 7.09 us -> 15.4 us  [swap_cores(): return lax.ppermute(value, 'sp', perm=core_perm)]
    pallas_call x4 -> x8, Pallas kernels: 47.9 us -> 52.5 us  [local_layer(): grads = place_blocks(*own[h], *others[h], *grads)]
    ppermute x6 -> x12, starting transfers between devices: 12.3 us -> 15.8 us  [hop(): return lax.ppermute(value, 'sp', perm=ring_perm(axis, hops))]
  transfers between devices with their start and end apart: 14 -> 24, of which waited for: 3 -> 7; matrix products, arithmetic and copies ran while one was open for 4% -> 5% of each run, Pallas kernels for 7% -> 10%
where the time goes in v3:
time: 465 us; the launch traced here: 464 us
  Pallas kernels  245 us (53%)
  waiting for transfers between devices  88.6 us (19%)
  blocking collectives  69.9 us (15%)
  starting transfers between devices  31.2 us (7%)
  matrix products  22.5 us (5%)
  local copies, waits for them, and re-layouts  6.47 us (1%)
    pallas_call x1, Pallas kernels, local_layer(): pl.pallas_call(functools.partial(exchange_kernel, side, halves), in_specs...  154 us
    ppermute x12, waiting for transfers between devices, hop(): return lax.ppermute(value, 'sp', perm=ring_perm(axis, hops))  88.4 us
    pallas_call x8, Pallas kernels, local_layer(): grads = place_blocks(*own[h], *others[h], *grads)  52.5 us
    all_to_all x1, blocking collectives, local_layer(): parts = lax.all_to_all(totals, 'sp', 0, 0)  37.5 us
    all_to_all x1, blocking collectives, local_layer(): states = lax.all_to_all(prefixes, 'sp', 0, 0)  32.4 us
    pallas_call x1, Pallas kernels, local_layer(): pl.pallas_call(project_kernel, grid=(model_dim // tile,), in_specs=[full,...  19.1 us
    pallas_call x1, Pallas kernels, local_layer(): pl.pallas_call(functools.partial(attend_kernel, att_scale), grid=(n_heads...  16.1 us
    ppermute x12, starting transfers between devices, hop(): return lax.ppermute(value, 'sp', perm=ring_perm(axis, hops))  15.8 us
  transfers between devices with their start and end apart: 24, of which 7 were waited for; matrix products, arithmetic and copies ran while one was open for 5% of the time, Pallas kernels for 10%

profile of v3, /device:TPU:97, one launch (start us, length us, event | category | flops | bytes accessed | tf_op | source)
XLA Modules:
  0.0 464.4 jit_solution(2822068383062045879)
XLA Ops:
  1.9 19.1 %project.1 = (bf16[256,2048]{1,0:T(8,128)(2,1)S(1)}, bf16[256,2048]{1,0:T(8,128)(2,1)S(1)}, bf16[256,2048]{1,0:T(8,128)(2,1)S(1)}, bf16[256,2048]{1,0:T(8,128)(2,1)S(1)}, f32[32,2,64,128]{3,2,1,0:T(8,128)}) custom-call(bf16[256,2048]{1,0:T(8,128)(2,1)S(1)} %copy-done, bf16[256,2048]{1,0:T(8,128)(2,1)} %dy_ref.3, bf16[2048,2048]{1,0:T(8,128)(2,1)} %wq_ref.1, ...), custom_call_target="tpu_custom_call" | custom-call | flops 8589934592 | bytes 33554432 | tf_op jit(solution)/shard_map/project/pallas_call | solution.py:325
  24.8 37.5 %all_to_all.10.parts_ref = f32[32,2,64,128]{3,2,1,0:T(8,128)} all-to-all(f32[32,2,64,128]{3,2,1,0:T(8,128)} %get-tuple-element.57), channel_id=1, replica_groups=mesh['dp'=1,'sp'=32] {'sp'}, dimensions={0} | all-to-all | bytes 4194304 | tf_op jit(solution)/shard_map/all_to_all | solution.py:336
  62.3 3.0 state_prefix.1
  65.4 32.4 %all_to_all.11.state_ref = f32[32,2,64,128]{3,2,1,0:T(8,128)} all-to-all(f32[32,2,64,128]{3,2,1,0:T(8,128)} %state_prefix.1), channel_id=1, replica_groups=mesh['dp'=1,'sp'=32] {'sp'}, dimensions={0} | all-to-all | bytes 4194304 | tf_op jit(solution)/shard_map/all_to_all | solution.py:345
  97.7 16.1 %attend.1 = (bf16[2,256,2048]{2,1,0:T(8,128)(2,1)}, bf16[4,256,2048]{2,1,0:T(8,128)(2,1)}) custom-call(bf16[256,2048]{1,0:T(8,128)(2,1)} %copy-done.1, bf16[256,2048]{1,0:T(8,128)(2,1)} %copy-done.2, bf16[256,2048]{1,0:T(8,128)(2,1)} %copy-done.3, bf16[256,2048]{1,0:T(8,128)(2,1)} %copy-done.4, bf16[256,2048]{1,0:T(8,128)(2,1)} %x_ref.3, ...), custom_call_target="tpu_custom_call" | custom-call | flops 1610612736 | bytes 16777216 | tf_op jit(solution)/shard_map/attend/pallas_call | solution.py:349
  113.8 153.9 %exchange.1 = (f32[256,2048]{1,0:T(8,128)}, f32[256,2048]{1,0:T(8,128)}, f32[256,2048]{1,0:T(8,128)}, f32[256,2048]{1,0:T(8,128)}, f32[256,2048]{1,0:T(8,128)}, ...) custom-call(bf16[2,256,2048]{2,1,0:T(8,128)(2,1)} %get-tuple-element.58.left_ref, ...), custom_call_target="tpu_custom_call" | custom-call | flops 8589934592 | bytes 16777216 | tf_op jit(solution)/shard_map/exchange/pallas_call | solution.py:365
  270.8 22.4 %collective-permute-done.8.refs_0_ = f32[256,2048]{1,0:T(8,128)S(1)} collective-permute-done((f32[256,2048]{1,0:T(8,128)}, f32[256,2048]{1,0:T(8,128)S(1)}, u32[]{:S(2)}, u32[]{:S(2)}) %collective-permute-start.8) | collective-permute-done | bytes 2097184 | tf_op jit(solution)/shard_map/ppermute | solution.py:309
  296.0 19.7 %collective-permute-done.refs_0_ = f32[256,2048]{1,0:T(8,128)S(1)} collective-permute-done((f32[256,2048]{1,0:T(8,128)}, f32[256,2048]{1,0:T(8,128)S(1)}, u32[]{:S(2)}, u32[]{:S(2)}) %collective-permute-start) | collective-permute-done | bytes 2097184 | tf_op jit(solution)/shard_map/ppermute | solution.py:309
  323.9 19.3 %collective-permute-done.9.refs_0_ = f32[256,2048]{1,0:T(8,128)} collective-permute-done((f32[256,2048]{1,0:T(8,128)S(1)}, f32[256,2048]{1,0:T(8,128)}, u32[]{:S(2)}, u32[]{:S(2)}) %collective-permute-start.9) | collective-permute-done | bytes 2097184 | tf_op jit(solution)/shard_map/ppermute | solution.py:309
  348.3 17.4 %collective-permute-done.1.refs_0_ = f32[256,2048]{1,0:T(8,128)} collective-permute-done((f32[256,2048]{1,0:T(8,128)S(1)}, f32[256,2048]{1,0:T(8,128)}, u32[]{:S(2)}, u32[]{:S(2)}) %collective-permute-start.1) | collective-permute-done | bytes 2097184 | tf_op jit(solution)/shard_map/ppermute | solution.py:309
  368.5 6.2 %fusion.3 = f32[256,2048]{1,0:T(8,128)S(1)} fusion(bf16[2048,2048]{1,0:T(8,128)(2,1)} %wq_ref.1, bf16[4,256,2048]{2,1,0:T(8,128)(2,1)} %get-tuple-element.59.right_ref), kind=kOutput, calls=%fused_computation.6 | convolution fusion | flops 2147483648 | bytes 11534336 | tf_op jit(solution)/shard_map/ne,de->nd/dot_general | solution.py:315
  379.0 6.0 %convolution_add_fusion.1 = f32[256,2048]{1,0:T(8,128)S(1)} fusion(f32[256,2048]{1,0:T(8,128)S(1)} %fusion.3, bf16[2048,2048]{1,0:T(8,128)(2,1)} %wk_ref.1, bf16[4,256,2048]{2,1,0:T(8,128)(2,1)S(1)} %copy-done.16), kind=kOutput, calls=%fused_computation.1 | convolution fusion | flops 2148007936 | bytes 13631488 | tf_op jit(solution)/shard_map/ne,de->nd/dot_general | solution.py:315
  385.0 3.4 fusion
  388.4 6.6 %shard_map.109 = (f32[2048,2048]{1,0:T(8,128)}, f32[2048,2048]{1,0:T(8,128)}, f32[2048,2048]{1,0:T(8,128)}, f32[2048,2048]{1,0:T(8,128)}) custom-call(f32[256,2048]{1,0:T(8,128)} %get-tuple-element.62.refs_0_, f32[256,2048]{1,0:T(8,128)} %get-tuple-element.63.refs_1_, f32[256,2048]{1,0:T(8,128)} %get-tuple-element.66.refs_2_, ...), custom_call_target="tpu_custom_call" | custom-call | flops 3000000000 | bytes 67108864 | tf_op jit(solution)/shard_map/pallas_call | solution.py:413
  395.7 6.6 %shard_map.110 = (f32[2048,2048]{1,0:T(8,128)}, f32[2048,2048]{1,0:T(8,128)}, f32[2048,2048]{1,0:T(8,128)}, f32[2048,2048]{1,0:T(8,128)}) custom-call(f32[256,2048]{1,0:T(8,128)} %get-tuple-element.60.refs_0_, f32[256,2048]{1,0:T(8,128)} %get-tuple-element.61.refs_1_, ...), custom_call_target="tpu_custom_call", output_to_operand_aliasing={{0}: (4, {}), {1}: (5, {}), {2}: (6, {}), {3}: (7, {})} | custom-call | flops 3000000000 | bytes 67108864 | tf_op jit(solution)/shard_map/pallas_call | solution.py:413
  402.3 8.4 %collective-permute-done.2.refs_0_ = f32[256,2048]{1,0:T(8,128)S(1)} collective-permute-done((f32[256,2048]{1,0:T(8,128)}, f32[256,2048]{1,0:T(8,128)S(1)}, u32[]{:S(2)}, u32[]{:S(2)}) %collective-permute-start.2) | collective-permute-done | bytes 2097184 | tf_op jit(solution)/shard_map/ppermute | solution.py:309
  413.7 4.1 collective-permute-start.7
  417.8 7.0 %convolution_convert_fusion = bf16[256,2048]{1,0:T(8,128)(2,1)} fusion(bf16[2048,2048]{1,0:T(8,128)(2,1)} %wo_ref.1, bf16[2,256,2048]{2,1,0:T(8,128)(2,1)} %get-tuple-element.58.left_ref), kind=kOutput, calls=%fused_computation.3 | convolution fusion | flops 2148007936 | bytes 10485760 | tf_op jit(solution)/shard_map/dot_general | solution.py:312
  424.8 6.6 %shard_map.111 = (f32[2048,2048]{1,0:T(8,128)}, f32[2048,2048]{1,0:T(8,128)}, f32[2048,2048]{1,0:T(8,128)}, f32[2048,2048]{1,0:T(8,128)}) custom-call(f32[256,2048]{1,0:T(8,128)} %copy-done.7, f32[256,2048]{1,0:T(8,128)} %copy-done.8, f32[256,2048]{1,0:T(8,128)} %copy-done.9, ...), custom_call_target="tpu_custom_call", output_to_operand_aliasing={{0}: (4, {}), {1}: (5, {}), {2}: (6, {}), {3}: (7, {})} | custom-call | flops 3000000000 | bytes 67108864 | tf_op jit(solution)/shard_map/pallas_call | solution.py:413
  431.4 6.6 %shard_map.112 = (f32[2048,2048]{1,0:T(8,128)}, f32[2048,2048]{1,0:T(8,128)}, f32[2048,2048]{1,0:T(8,128)}, f32[2048,2048]{1,0:T(8,128)}) custom-call(f32[256,2048]{1,0:T(8,128)} %copy-done.5, f32[256,2048]{1,0:T(8,128)} %copy-done.6, f32[256,2048]{1,0:T(8,128)} %copy-done.10, ...), custom_call_target="tpu_custom_call", output_to_operand_aliasing={{0}: (4, {}), {1}: (5, {}), {2}: (6, {}), {3}: (7, {})} | custom-call | flops 3000000000 | bytes 67108864 | tf_op jit(solution)/shard_map/pallas_call | solution.py:413
  438.0 6.6 %shard_map.113 = (f32[2048,2048]{1,0:T(8,128)}, f32[2048,2048]{1,0:T(8,128)}, f32[2048,2048]{1,0:T(8,128)}, f32[2048,2048]{1,0:T(8,128)}) custom-call(f32[256,2048]{1,0:T(8,128)} %collective-permute-done.9.refs_0_, f32[256,2048]{1,0:T(8,128)} %collective-permute-done.12.refs_1_, ...), custom_call_target="tpu_custom_call", output_to_operand_aliasing={{0}: (4, {}), {1}: (5, {}), {2}: (6, {}), {3}: (7, {})} | custom-call | flops 3000000000 | bytes 67108864 | tf_op jit(solution)/shard_map/pallas_call | solution.py:413
  444.5 6.6 %shard_map.114 = (f32[2048,2048]{1,0:T(8,128)}, f32[2048,2048]{1,0:T(8,128)}, f32[2048,2048]{1,0:T(8,128)}, f32[2048,2048]{1,0:T(8,128)}) custom-call(f32[256,2048]{1,0:T(8,128)} %collective-permute-done.1.refs_0_, f32[256,2048]{1,0:T(8,128)} %collective-permute-done.4.refs_1_, ...), custom_call_target="tpu_custom_call", output_to_operand_aliasing={{0}: (4, {}), {1}: (5, {}), {2}: (6, {}), {3}: (7, {})} | custom-call | flops 3000000000 | bytes 67108864 | tf_op jit(solution)/shard_map/pallas_call | solution.py:413
  451.1 6.6 %shard_map.115 = (f32[2048,2048]{1,0:T(8,128)}, f32[2048,2048]{1,0:T(8,128)}, f32[2048,2048]{1,0:T(8,128)}, f32[2048,2048]{1,0:T(8,128)}) custom-call(f32[256,2048]{1,0:T(8,128)} %collective-permute-done.10.refs_0_, f32[256,2048]{1,0:T(8,128)} %collective-permute-done.13.refs_1_, ...), custom_call_target="tpu_custom_call", output_to_operand_aliasing={{0}: (4, {}), {1}: (5, {}), {2}: (6, {}), {3}: (7, {})} | custom-call | flops 3000000000 | bytes 67108864 | tf_op jit(solution)/shard_map/pallas_call | solution.py:413
  457.7 6.6 %shard_map.116 = (f32[2048,2048]{1,0:T(8,128)}, f32[2048,2048]{1,0:T(8,128)}, f32[2048,2048]{1,0:T(8,128)}, f32[2048,2048]{1,0:T(8,128)}) custom-call(f32[256,2048]{1,0:T(8,128)} %copy-done.12, f32[256,2048]{1,0:T(8,128)} %collective-permute-done.5.refs_1_, ...), custom_call_target="tpu_custom_call", output_to_operand_aliasing={{0}: (4, {}), {1}: (5, {}), {2}: (6, {}), {3}: (7, {})} | custom-call | flops 3000000000 | bytes 67108864 | tf_op jit(solution)/shard_map/pallas_call | solution.py:413
  (81 shorter events, 34.9 us)
Async XLA Ops:
  267.8 25.5 %collective-permute-start.8 = (f32[256,2048]{1,0:T(8,128)}, f32[256,2048]{1,0:T(8,128)S(1)}, u32[]{:S(2)}, u32[]{:S(2)}) collective-permute-start(f32[256,2048]{1,0:T(8,128)} %get-tuple-element.62.refs_0_), channel_id=1, source_target_pairs={{0,2},{1,7},{2,4},{3,1},{4,6},{5,3},{6,0},{7,5},{8,10},{9,15},{10,... | collective-permute-start | bytes 6291464 | tf_op jit(solution)/shard_map/ppermute | solution.py:309
  269.6 25.8 %collective-permute-start.11 = (f32[256,2048]{1,0:T(8,128)}, f32[256,2048]{1,0:T(8,128)S(1)}, u32[]{:S(2)}, u32[]{:S(2)}) collective-permute-start(f32[256,2048]{1,0:T(8,128)} %get-tuple-element.63.refs_1_), channel_id=1, source_target_pairs={{0,8},{1,25},{2,10},{3,27},{4,12},{5,29},{6,14},{7,31},{8,16},{9,1... | collective-permute-start | bytes 6291464 | tf_op jit(solution)/shard_map/ppermute | solution.py:309
  269.6 46.1 %collective-permute-start = (f32[256,2048]{1,0:T(8,128)}, f32[256,2048]{1,0:T(8,128)S(1)}, u32[]{:S(2)}, u32[]{:S(2)}) collective-permute-start(f32[256,2048]{1,0:T(8,128)} %get-tuple-element.60.refs_0_), channel_id=1, source_target_pairs={{0,2},{1,7},{2,4},{3,1},{4,6},{5,3},{6,0},{7,5},{8,10},{9,15},{10,... | collective-permute-start | bytes 6291464 | tf_op jit(solution)/shard_map/ppermute | solution.py:309
  270.0 48.8 %collective-permute-start.3 = (f32[256,2048]{1,0:T(8,128)}, f32[256,2048]{1,0:T(8,128)S(1)}, u32[]{:S(2)}, u32[]{:S(2)}) collective-permute-start(f32[256,2048]{1,0:T(8,128)} %get-tuple-element.61.refs_1_), channel_id=1, source_target_pairs={{0,8},{1,25},{2,10},{3,27},{4,12},{5,29},{6,14},{7,31},{8,16},{9,1... | collective-permute-start | bytes 6291464 | tf_op jit(solution)/shard_map/ppermute | solution.py:309
  293.3 26.5 %collective-permute-start.22 = (f32[256,2048]{1,0:T(8,128)S(1)}, f32[256,2048]{1,0:T(8,128)S(1)}, u32[]{:S(2)}, u32[]{:S(2)}) collective-permute-start(f32[256,2048]{1,0:T(8,128)S(1)} %collective-permute-done.8.refs_0_), channel_id=1, source_target_pairs={{0,1},{1,0},{2,3},{3,2},{4,5},{5,4},{6,7},{7,6},{8,9},{9,8},{10,11... | collective-permute-start | bytes 6291464 | tf_op jit(solution)/shard_map/ppermute | solution.py:306
  295.5 24.3 %collective-permute-start.23 = (f32[256,2048]{1,0:T(8,128)S(1)}, f32[256,2048]{1,0:T(8,128)S(1)}, u32[]{:S(2)}, u32[]{:S(2)}) collective-permute-start(f32[256,2048]{1,0:T(8,128)S(1)} %collective-permute-done.11.refs_1_), channel_id=1, source_target_pairs={{0,1},{1,0},{2,3},{3,2},{4,5},{5,4},{6,7},{7,6},{8,9},{9,8},{10,11... | collective-permute-start | bytes 6291464 | tf_op jit(solution)/shard_map/ppermute | solution.py:306
  315.7 6.0 %collective-permute-start.20 = (f32[256,2048]{1,0:T(8,128)S(1)}, f32[256,2048]{1,0:T(8,128)S(1)}, u32[]{:S(2)}, u32[]{:S(2)}) collective-permute-start(f32[256,2048]{1,0:T(8,128)S(1)} %collective-permute-done.refs_0_), channel_id=1, source_target_pairs={{0,1},{1,0},{2,3},{3,2},{4,5},{5,4},{6,7},{7,6},{8,9},{9,8},{10,11... | collective-permute-start | bytes 6291464 | tf_op jit(solution)/shard_map/ppermute | solution.py:306
  317.9 25.3 %collective-permute-start.9 = (f32[256,2048]{1,0:T(8,128)S(1)}, f32[256,2048]{1,0:T(8,128)}, u32[]{:S(2)}, u32[]{:S(2)}) collective-permute-start(f32[256,2048]{1,0:T(8,128)S(1)} %collective-permute-done.8.refs_0_), channel_id=1, source_target_pairs={{0,2},{1,7},{2,4},{3,1},{4,6},{5,3},{6,0},{7,5},{8,10},{9,15},{10,... | collective-permute-start | bytes 6291464 | tf_op jit(solution)/shard_map/ppermute | solution.py:309
  318.7 26.6 %collective-permute-start.12 = (f32[256,2048]{1,0:T(8,128)S(1)}, f32[256,2048]{1,0:T(8,128)}, u32[]{:S(2)}, u32[]{:S(2)}) collective-permute-start(f32[256,2048]{1,0:T(8,128)S(1)} %collective-permute-done.11.refs_1_), channel_id=1, source_target_pairs={{0,8},{1,25},{2,10},{3,27},{4,12},{5,29},{6,14},{7,31},{8,16},{9,1... | collective-permute-start | bytes 6291464 | tf_op jit(solution)/shard_map/ppermute | solution.py:309
  319.8 26.1 %collective-permute-start.21 = (f32[256,2048]{1,0:T(8,128)S(1)}, f32[256,2048]{1,0:T(8,128)S(1)}, u32[]{:S(2)}, u32[]{:S(2)}) collective-permute-start(f32[256,2048]{1,0:T(8,128)S(1)} %collective-permute-done.3.refs_1_), channel_id=1, source_target_pairs={{0,1},{1,0},{2,3},{3,2},{4,5},{5,4},{6,7},{7,6},{8,9},{9,8},{10,11... | collective-permute-start | bytes 6291464 | tf_op jit(solution)/shard_map/ppermute | solution.py:306
  319.8 45.9 %collective-permute-start.1 = (f32[256,2048]{1,0:T(8,128)S(1)}, f32[256,2048]{1,0:T(8,128)}, u32[]{:S(2)}, u32[]{:S(2)}) collective-permute-start(f32[256,2048]{1,0:T(8,128)S(1)} %collective-permute-done.refs_0_), channel_id=1, source_target_pairs={{0,2},{1,7},{2,4},{3,1},{4,6},{5,3},{6,0},{7,5},{8,10},{9,15},{10,... | collective-permute-start | bytes 6291464 | tf_op jit(solution)/shard_map/ppermute | solution.py:309
  321.7 45.7 %collective-permute-start.4 = (f32[256,2048]{1,0:T(8,128)S(1)}, f32[256,2048]{1,0:T(8,128)}, u32[]{:S(2)}, u32[]{:S(2)}) collective-permute-start(f32[256,2048]{1,0:T(8,128)S(1)} %collective-permute-done.3.refs_1_), channel_id=1, source_target_pairs={{0,8},{1,25},{2,10},{3,27},{4,12},{5,29},{6,14},{7,31},{8,16},{9,1... | collective-permute-start | bytes 6291464 | tf_op jit(solution)/shard_map/ppermute | solution.py:309
  343.2 31.5 %collective-permute-start.18 = (f32[256,2048]{1,0:T(8,128)}, f32[256,2048]{1,0:T(8,128)S(1)}, u32[]{:S(2)}, u32[]{:S(2)}) collective-permute-start(f32[256,2048]{1,0:T(8,128)} %collective-permute-done.9.refs_0_), channel_id=1, source_target_pairs={{0,1},{1,0},{2,3},{3,2},{4,5},{5,4},{6,7},{7,6},{8,9},{9,8},{10,11... | collective-permute-start | bytes 6291464 | tf_op jit(solution)/shard_map/ppermute | solution.py:306
  345.3 33.2 %collective-permute-start.19 = (f32[256,2048]{1,0:T(8,128)}, f32[256,2048]{1,0:T(8,128)S(1)}, u32[]{:S(2)}, u32[]{:S(2)}) collective-permute-start(f32[256,2048]{1,0:T(8,128)} %collective-permute-done.12.refs_1_), channel_id=1, source_target_pairs={{0,1},{1,0},{2,3},{3,2},{4,5},{5,4},{6,7},{7,6},{8,9},{9,8},{10,11... | collective-permute-start | bytes 6291464 | tf_op jit(solution)/shard_map/ppermute | solution.py:306
  345.8 49.1 %collective-permute-start.10 = (f32[256,2048]{1,0:T(8,128)}, f32[256,2048]{1,0:T(8,128)}, u32[]{:S(2)}, u32[]{:S(2)}) collective-permute-start(f32[256,2048]{1,0:T(8,128)} %collective-permute-done.9.refs_0_), channel_id=1, source_target_pairs={{0,2},{1,7},{2,4},{3,1},{4,6},{5,3},{6,0},{7,5},{8,10},{9,15},{10,... | collective-permute-start | bytes 6291464 | tf_op jit(solution)/shard_map/ppermute | solution.py:309
  365.7 29.9 %collective-permute-start.13 = (f32[256,2048]{1,0:T(8,128)}, f32[256,2048]{1,0:T(8,128)}, u32[]{:S(2)}, u32[]{:S(2)}) collective-permute-start(f32[256,2048]{1,0:T(8,128)} %collective-permute-done.12.refs_1_), channel_id=1, source_target_pairs={{0,8},{1,25},{2,10},{3,27},{4,12},{5,29},{6,14},{7,31},{8,16},{9,1... | collective-permute-start | bytes 6291464 | tf_op jit(solution)/shard_map/ppermute | solution.py:309
  367.5 20.9 %collective-permute-start.16 = (f32[256,2048]{1,0:T(8,128)}, f32[256,2048]{1,0:T(8,128)}, u32[]{:S(2)}, u32[]{:S(2)}) collective-permute-start(f32[256,2048]{1,0:T(8,128)} %collective-permute-done.1.refs_0_), channel_id=1, source_target_pairs={{0,1},{1,0},{2,3},{3,2},{4,5},{5,4},{6,7},{7,6},{8,9},{9,8},{10,11... | collective-permute-start | bytes 6291464 | tf_op jit(solution)/shard_map/ppermute | solution.py:306
  376.1 34.6 %collective-permute-start.2 = (f32[256,2048]{1,0:T(8,128)}, f32[256,2048]{1,0:T(8,128)S(1)}, u32[]{:S(2)}, u32[]{:S(2)}) collective-permute-start(f32[256,2048]{1,0:T(8,128)} %collective-permute-done.1.refs_0_), channel_id=1, source_target_pairs={{0,2},{1,7},{2,4},{3,1},{4,6},{5,3},{6,0},{7,5},{8,10},{9,15},{10,... | collective-permute-start | bytes 6291464 | tf_op jit(solution)/shard_map/ppermute | solution.py:309
  378.5 35.2 %collective-permute-start.5 = (f32[256,2048]{1,0:T(8,128)}, f32[256,2048]{1,0:T(8,128)}, u32[]{:S(2)}, u32[]{:S(2)}) collective-permute-start(f32[256,2048]{1,0:T(8,128)} %collective-permute-done.4.refs_1_), channel_id=1, source_target_pairs={{0,8},{1,25},{2,10},{3,27},{4,12},{5,29},{6,14},{7,31},{8,16},{9,1... | collective-permute-start | bytes 6291464 | tf_op jit(solution)/shard_map/ppermute | solution.py:309
  388.4 56.2 %collective-permute-start.17 = (f32[256,2048]{1,0:T(8,128)}, f32[256,2048]{1,0:T(8,128)}, u32[]{:S(2)}, u32[]{:S(2)}) collective-permute-start(f32[256,2048]{1,0:T(8,128)} %collective-permute-done.4.refs_1_), channel_id=1, source_target_pairs={{0,1},{1,0},{2,3},{3,2},{4,5},{5,4},{6,7},{7,6},{8,9},{9,8},{10,11... | collective-permute-start | bytes 6291464 | tf_op jit(solution)/shard_map/ppermute | solution.py:306
  395.0 56.2 %collective-permute-start.14 = (f32[256,2048]{1,0:T(8,128)}, f32[256,2048]{1,0:T(8,128)}, u32[]{:S(2)}, u32[]{:S(2)}) collective-permute-start(f32[256,2048]{1,0:T(8,128)} %collective-permute-done.10.refs_0_), channel_id=1, source_target_pairs={{0,1},{1,0},{2,3},{3,2},{4,5},{5,4},{6,7},{7,6},{8,9},{9,8},{10,11... | collective-permute-start | bytes 6291464 | tf_op jit(solution)/shard_map/ppermute | solution.py:306
  395.6 55.6 %collective-permute-start.15 = (f32[256,2048]{1,0:T(8,128)}, f32[256,2048]{1,0:T(8,128)}, u32[]{:S(2)}, u32[]{:S(2)}) collective-permute-start(f32[256,2048]{1,0:T(8,128)} %collective-permute-done.13.refs_1_), channel_id=1, source_target_pairs={{0,1},{1,0},{2,3},{3,2},{4,5},{5,4},{6,7},{7,6},{8,9},{9,8},{10,11... | collective-permute-start | bytes 6291464 | tf_op jit(solution)/shard_map/ppermute | solution.py:306
  410.6 47.1 %collective-permute-start.6 = (f32[256,2048]{1,0:T(8,128)S(1)}, f32[256,2048]{1,0:T(8,128)}, u32[]{:S(2)}, u32[]{:S(2)}) collective-permute-start(f32[256,2048]{1,0:T(8,128)S(1)} %collective-permute-done.2.refs_0_), channel_id=1, source_target_pairs={{0,1},{1,0},{2,3},{3,2},{4,5},{5,4},{6,7},{7,6},{8,9},{9,8},{10,11... | collective-permute-start | bytes 6291464 | tf_op jit(solution)/shard_map/ppermute | solution.py:306
  413.7 44.1 %collective-permute-start.7 = (f32[256,2048]{1,0:T(8,128)}, f32[256,2048]{1,0:T(8,128)}, u32[]{:S(2)}, u32[]{:S(2)}) collective-permute-start(f32[256,2048]{1,0:T(8,128)} %collective-permute-done.5.refs_1_), channel_id=1, source_target_pairs={{0,1},{1,0},{2,3},{3,2},{4,5},{5,4},{6,7},{7,6},{8,9},{9,8},{10,11... | collective-permute-start | bytes 6291464 | tf_op jit(solution)/shard_map/ppermute | solution.py:306
  (19 other events, 579.6 us)

commit v4 on v3

--- a/solution.py
+++ b/solution.py
@@ -30,27 +30,145 @@
     k_ref[...] = dot(x, wk_ref[...], (1, 0)).astype(BF16)
     v_ref[...] = dot(x, wv_ref[...], (1, 0)).astype(BF16)
     do_ref[...] = dot(dy_ref[...], wo_ref[...], (1, 1)).astype(BF16)
-    rows = totals_ref.shape[2]
-    per_head = HEAD_DIM // rows
     for head in range(q_ref.shape[1] // HEAD_DIM):
         cols = slice(head * HEAD_DIM, (head + 1) * HEAD_DIM)
         kv = dot(k_ref[:, cols], v_ref[:, cols], (0, 0))
         qdo = dot(q_ref[:, cols], do_ref[:, cols], (0, 0))
-        for part in range(per_head):
-            totals_ref[head * per_head + part, 0] = kv[part * rows : (part + 1) * rows]
-            totals_ref[head * per_head + part, 1] = qdo[part * rows : (part + 1) * rows]
-
-
-def prefix_kernel(parts_ref, out_ref):
-    n_parts = parts_ref.shape[0]
-    before = jnp.zeros_like(parts_ref[0, 0])
-    after = jnp.zeros_like(parts_ref[0, 1])
-    for step in range(n_parts):
-        last = n_parts - 1 - step
-        out_ref[step, 0] = before
-        out_ref[last, 1] = after
-        before = before + parts_ref[step, 0]
-        after = after + parts_ref[last, 1]
+        totals_ref[0, head] = kv
+        totals_ref[1, head] = qdo
+
+
+def chain_kernel(side, totals_ref, out_ref, other, before, stage, above, down, peer, swap_send, swap_recv, row_send, row_recv, above_recv, down_send, cast_send, back_send, back_recv):
+    me = lax.axis_index("sp")
+    core = lax.rem(me, N_CORES)
+    col = lax.rem(me // N_CORES, side)
+    row = me // (N_CORES * side)
+    partner = me + 1 - 2 * core
+    n_group = totals_ref.shape[1] // N_CORES
+    mine, yours = core * n_group, (1 - core) * n_group
+
+    def wrap(value):
+        return lax.rem(value + 2 * side, side)
+
+    def device(r, c):
+        return (wrap(r) * side + wrap(c)) * N_CORES + core
+
+    barrier = pltpu.get_barrier_semaphore()
+    others = [device(row, col + t) for t in range(1, side)] + [device(row + 1, col), device(row - 1, col), partner]
+    for target in others:
+        pl.semaphore_signal(barrier, inc=1, device_id={"sp": target}, device_id_type=MESH)
+    pl.semaphore_wait(barrier, len(others))
+
+    def copy(src, dst, send, recv, target):
+        return pltpu.make_async_remote_copy(src_ref=src, dst_ref=dst, send_sem=send, recv_sem=recv, device_id={"sp": target}, device_id_type=MESH)
+
+    def swap_copy(kind):
+        return copy(totals_ref.at[kind, pl.ds(yours, n_group)], other.at[kind], swap_send.at[kind], swap_recv.at[kind], partner)
+
+    def row_copy(kind, h):
+        return copy(stage.at[kind, h], before.at[kind, h], row_send.at[kind, h], row_recv.at[kind, h], device(row, col + 1 - 2 * kind))
+
+    def down_copy(kind, h):
+        return copy(down.at[kind, h], above.at[kind, h], down_send.at[kind, h], above_recv.at[kind, h], device(row + 1 - 2 * kind, col))
+
+    def cast_copy(kind, h, t):
+        return copy(above.at[kind, h], above.at[kind, h], cast_send.at[kind, h, t - 1], above_recv.at[kind, h], device(row, col + t))
+
+    def back_copy(kind, h):
+        return copy(peer.at[kind, h], out_ref.at[kind, mine + h], back_send.at[kind, h], back_recv.at[kind, h], partner)
+
+    def position(kind, coordinate):
+        return kind * (side - 1) + (1 - 2 * kind) * coordinate
+
+    for kind in range(2):
+        swap_copy(kind).start()
+    for kind in range(2):
+
+        @pl.when(position(kind, col) == 0)
+        def _():
+            before[kind] = jnp.zeros_like(before[kind])
+
+        @pl.when((position(kind, col) == side - 1) & (position(kind, row) == 0))
+        def _():
+            above[kind] = jnp.zeros_like(above[kind])
+
+    for kind in range(2):
+        swap_copy(kind).wait()
+
+    def run(slot, carry):
+        for kind in range(2):
+            along, across = position(kind, col), position(kind, row)
+            h = slot - 2 * along
+
+            @pl.when((h >= 0) & (h < n_group))
+            def _():
+                @pl.when(along > 0)
+                def _():
+                    row_copy(kind, h).wait_recv()
+
+                stage[kind, h] = before[kind, h] + (totals_ref[kind, mine + h] + other[kind, h])
+
+                @pl.when(along < side - 1)
+                def _():
+                    row_copy(kind, h).start()
+
+            g = slot - 2 * (side - 1 + across)
+
+            @pl.when((along == side - 1) & (g >= 0) & (g < n_group))
+            def _():
+                @pl.when(across > 0)
+                def _():
+                    down_copy(kind, g).wait_recv()
+
+                @pl.when(across < side - 1)
+                def _():
+                    down[kind, g] = above[kind, g] + stage[kind, g]
+                    down_copy(kind, g).start()
+
+                for t in range(1, side):
+                    cast_copy(kind, g, t).start()
+
+        return carry
+
+    lax.fori_loop(0, 4 * (side - 1) + n_group, run, 0)
+
+    def finish(h, carry):
+        for kind in range(2):
+
+            @pl.when(position(kind, col) < side - 1)
+            def _():
+                down_copy(kind, h).wait_recv()
+
+            base = above[kind, h] + before[kind, h]
+            own_total, other_total = totals_ref[kind, mine + h], other[kind, h]
+            out_ref[kind, mine + h] = jnp.where(core == kind, base, base + other_total)
+            peer[kind, h] = jnp.where(core == kind, base + own_total, base)
+            back_copy(kind, h).start()
+        return carry
+
+    lax.fori_loop(0, n_group, finish, 0)
+
+    def drain(h, carry):
+        for kind in range(2):
+            along, across = position(kind, col), position(kind, row)
+            back_copy(kind, h).wait()
+
+            @pl.when(along < side - 1)
+            def _():
+                row_copy(kind, h).wait_send()
+
+            @pl.when(along == side - 1)
+            def _():
+                for t in range(1, side):
+                    cast_copy(kind, h, t).wait_send()
+
+                @pl.when(across < side - 1)
+                def _():
+                    down_copy(kind, h).wait_send()
+
+        return carry
+
+    lax.fori_loop(0, n_group, drain, 0)
 
 
 def attend_kernel(scale, q_ref, k_ref, v_ref, do_ref, x_ref, dy_ref, state_ref, left_ref, right_ref):
@@ -58,10 +176,10 @@
     left_ref[0] = x_ref[...]
     right_ref[3] = dy_ref[...]
     rows = [pl.ds(b * BLOCK_LEN, BLOCK_LEN) for b in range(n_blocks)]
-    fwd = [state_ref[:, 0].reshape(HEAD_DIM, HEAD_DIM)]
+    fwd = [state_ref[0, 0]]
     for b in range(n_blocks - 1):
         fwd.append(fwd[-1] + dot(k_ref[rows[b]], v_ref[rows[b]], (0, 0)))
-    rev = [state_ref[:, 1].reshape(HEAD_DIM, HEAD_DIM)]
+    rev = [state_ref[1, 0]]
     for b in range(n_blocks - 1, 0, -1):
         rev.insert(0, rev[0] + dot(q_ref[rows[b]], do_ref[rows[b]], (0, 0)))
     shape = (BLOCK_LEN, BLOCK_LEN)
@@ -315,8 +433,7 @@
             return jnp.einsum("ne,de->nd", rows, weight, preferred_element_type=F32)
 
         tile = 2 * HEAD_DIM
-        slice_rows = n_heads * HEAD_DIM // n_seq
-        per_tile = tile // slice_rows
+        state_shape = (2, n_heads, HEAD_DIM, HEAD_DIM)
         full = pl.BlockSpec((n_rows, model_dim), lambda i: (0, 0))
         in_cols = pl.BlockSpec((model_dim, tile), lambda i: (0, i))
         in_rows = pl.BlockSpec((tile, model_dim), lambda i: (i, 0))
@@ -326,30 +443,35 @@
             project_kernel,
             grid=(model_dim // tile,),
             in_specs=[full, full, in_cols, in_cols, in_cols, in_rows],
-            out_specs=[out_cols] * 4 + [pl.BlockSpec((per_tile, 2, slice_rows, HEAD_DIM), lambda i: (i, 0, 0, 0))],
-            out_shape=[act] * 4 + [jax.ShapeDtypeStruct((n_seq, 2, slice_rows, HEAD_DIM), F32)],
+            out_specs=[out_cols] * 4 + [pl.BlockSpec((2, tile // HEAD_DIM, HEAD_DIM, HEAD_DIM), lambda i: (0, i, 0, 0))],
+            out_shape=[act] * 4 + [jax.ShapeDtypeStruct(state_shape, F32)],
             cost_estimate=pl.CostEstimate(flops=8 * n_rows * model_dim * model_dim, bytes_accessed=8 * model_dim * model_dim, transcendentals=0),
             compiler_params=pltpu.CompilerParams(vmem_limit_bytes=48 * 2**20),
             name="project",
         )(tokens, grad_y, w_q, w_k, w_v, w_o)
 
-        parts = lax.all_to_all(totals, "sp", 0, 0)
-        prefixes = pl.pallas_call(
-            prefix_kernel,
-            out_shape=jax.ShapeDtypeStruct(parts.shape, parts.dtype),
+        dma = pltpu.SemaphoreType.DMA
+        n_group = n_heads // N_CORES
+        states = pl.pallas_call(
+            functools.partial(chain_kernel, side),
             in_specs=[pl.BlockSpec(memory_space=VMEM)],
             out_specs=pl.BlockSpec(memory_space=VMEM),
-            cost_estimate=pl.CostEstimate(flops=2 * parts.size, bytes_accessed=8 * parts.size, transcendentals=0),
-            name="state_prefix",
-        )(parts)
-        states = lax.all_to_all(prefixes, "sp", 0, 0)
+            out_shape=jax.ShapeDtypeStruct(state_shape, F32),
+            scratch_shapes=[VMEM((2, n_group, HEAD_DIM, HEAD_DIM), F32)] * 6
+            + [dma((2,))] * 2
+            + [dma((2, n_group))] * 4
+            + [dma((2, n_group, side - 1))]
+            + [dma((2, n_group))] * 2,
+            cost_estimate=pl.CostEstimate(flops=10**8, bytes_accessed=2**22, transcendentals=0),
+            compiler_params=pltpu.CompilerParams(collective_id=2, has_side_effects=True),
+            name="state_chain",
+        )(totals)
 
         head_cols = pl.BlockSpec((n_rows, HEAD_DIM), lambda h: (0, h))
-        per_head = HEAD_DIM // slice_rows
         lefts, rights = pl.pallas_call(
             functools.partial(attend_kernel, att_scale),
             grid=(n_heads,),
-            in_specs=[head_cols] * 6 + [pl.BlockSpec((per_head, 2, slice_rows, HEAD_DIM), lambda h: (h, 0, 0, 0))],
+            in_specs=[head_cols] * 6 + [pl.BlockSpec((2, 1, HEAD_DIM, HEAD_DIM), lambda h: (0, h, 0, 0))],
             out_specs=[pl.BlockSpec((2, n_rows, HEAD_DIM), lambda h: (0, 0, h)), pl.BlockSpec((4, n_rows, HEAD_DIM), lambda h: (0, 0, h))],
             out_shape=[jax.ShapeDtypeStruct((2, n_rows, model_dim), BF16), jax.ShapeDtypeStruct((4, n_rows, model_dim), BF16)],
             cost_estimate=pl.CostEstimate(flops=n_heads * 24 * 2 * 128**3, bytes_accessed=2**24, transcendentals=0),
@@ -361,7 +483,6 @@
         halves = 2
         small = block // side // halves
         axes = (("x", "y"), ("y", "x"))
-        dma = pltpu.SemaphoreType.DMA
         blocks = pl.pallas_call(
             functools.partial(exchange_kernel, side, halves),
             in_specs=[pl.BlockSpec(memory_space=VMEM)] * 2,
@@ -413,7 +534,9 @@
                 grads = place_blocks(*own[h], *others[h], *grads)
 
         out_y = project(lefts[1], w_o)
-        grad_x = (back_proj(rights[0], w_q) + back_proj(rights[1], w_k) + back_proj(rights[2], w_v)).astype(BF16)
+        grad_x = back_proj(rights[0], w_q)
+        grad_x = grad_x + back_proj(rights[1], w_k)
+        grad_x = (grad_x + back_proj(rights[2], w_v)).astype(BF16)
         return (out_y, grad_x) + tuple(grads)
 
     return jax.shard_map(local_layer, mesh=mesh, in_specs=(row_spec, P(), P(), P(), P(), row_spec), out_specs=(row_spec, row_spec, grad_spec, grad_spec, grad_spec, grad_spec), check_vma=False)

time: 465 us -> 454 us (0.976)
  blocking collectives: 69.9 us -> 0 us
  Pallas kernels: 245 us -> 302 us
    all_to_all x2 -> x0, blocking collectives: 69.9 us -> none  [the longest x1 37.5 us: local_layer(): parts = lax.all_to_all(totals, 'sp', 0, 0)]
    pallas_call x1, Pallas kernels: 3.04 us -> 53.8 us  [local_layer(): pl.pallas_call(functools.partial(chain_kernel, side), in_specs=[pl.BlockS...]
    pallas_call x1, Pallas kernels: 154 us -> 160 us  [local_layer(): pl.pallas_call(functools.partial(exchange_kernel, side, halves), in_specs...]
  transfers between devices with their start and end apart: 24 -> 24, of which waited for: 7 -> 6; matrix products, arithmetic and copies ran while one was open for 5% -> 6% of each run, Pallas kernels for 10% -> 10%
where the time goes in v4:
time: 454 us; the launch traced here: 453 us
  Pallas kernels  302 us (67%)
  waiting for transfers between devices  84.1 us (19%)
  starting transfers between devices  33.4 us (7%)
  matrix products  26.2 us (6%)
  local copies, waits for them, and re-layouts  6.47 us (1%)
    pallas_call x1, Pallas kernels, local_layer(): pl.pallas_call(functools.partial(exchange_kernel, side, halves), in_specs...  160 us
    ppermute x12, waiting for transfers between devices, hop(): return lax.ppermute(value, 'sp', perm=ring_perm(axis, hops))  84.1 us
    pallas_call x1, Pallas kernels, local_layer(): pl.pallas_call(functools.partial(chain_kernel, side), in_specs=[pl.BlockS...  53.8 us
    pallas_call x8, Pallas kernels, local_layer(): grads = place_blocks(*own[h], *others[h], *grads)  52.5 us
    dot_general x3, matrix products, back_proj(): return jnp.einsum('ne,de->nd', rows, weight, preferred_element_type=F32)  19.2 us
    pallas_call x1, Pallas kernels, local_layer(): pl.pallas_call(project_kernel, grid=(model_dim // tile,), in_specs=[full,...  19.1 us
    ppermute x12, starting transfers between devices, swap_cores(): return lax.ppermute(value, 'sp', perm=core_perm)  19 us
    pallas_call x1, Pallas kernels, local_layer(): pl.pallas_call(functools.partial(attend_kernel, att_scale), grid=(n_heads...  16.1 us
  transfers between devices with their start and end apart: 24, of which 6 were waited for; matrix products, arithmetic and copies ran while one was open for 6% of the time, Pallas kernels for 10%

profile of v4, /device:TPU:97, one launch (start us, length us, event | category | flops | bytes accessed | tf_op | source)
XLA Modules:
  0.0 453.2 jit_solution(15827116471971043756)
XLA Ops:
  1.9 19.1 %project.1 = (bf16[256,2048]{1,0:T(8,128)(2,1)S(1)}, bf16[256,2048]{1,0:T(8,128)(2,1)S(1)}, bf16[256,2048]{1,0:T(8,128)(2,1)S(1)}, bf16[256,2048]{1,0:T(8,128)(2,1)S(1)}, f32[2,16,128,128]{3,2,1,0:T(8,128)}) custom-call(bf16[256,2048]{1,0:T(8,128)(2,1)S(1)} %copy-done, bf16[256,2048]{1,0:T(8,128)(2,1)} %dy_ref.3, bf16[2048,2048]{1,0:T(8,128)(2,1)} %wq_ref.1, ...), custom_call_target="tpu_custom_call" | custom-call | flops 8589934592 | bytes 33554432 | tf_op jit(solution)/shard_map/project/pallas_call | solution.py:442
  24.8 53.8 %state_chain.1.state_ref = f32[2,16,128,128]{3,2,1,0:T(8,128)} custom-call(f32[2,16,128,128]{3,2,1,0:T(8,128)} %get-tuple-element.57.totals_ref), custom_call_target="tpu_custom_call" | custom-call | flops 100000000 | bytes 4194304 | tf_op jit(solution)/shard_map/state_chain/pallas_call | solution.py:455
  78.7 16.1 %attend.1 = (bf16[2,256,2048]{2,1,0:T(8,128)(2,1)}, bf16[4,256,2048]{2,1,0:T(8,128)(2,1)}) custom-call(bf16[256,2048]{1,0:T(8,128)(2,1)} %copy-done.1, bf16[256,2048]{1,0:T(8,128)(2,1)} %copy-done.2, bf16[256,2048]{1,0:T(8,128)(2,1)} %copy-done.3, bf16[256,2048]{1,0:T(8,128)(2,1)} %copy-done.4, bf16[256,2048]{1,0:T(8,128)(2,1)} %x_ref.3, ...), custom_call_target="tpu_custom_call" | custom-call | flops 1610612736 | bytes 16777216 | tf_op jit(solution)/shard_map/attend/pallas_call | solution.py:471
  94.8 160.4 %exchange.1 = (f32[256,2048]{1,0:T(8,128)}, f32[256,2048]{1,0:T(8,128)}, f32[256,2048]{1,0:T(8,128)}, f32[256,2048]{1,0:T(8,128)}, f32[256,2048]{1,0:T(8,128)}, ...) custom-call(bf16[2,256,2048]{2,1,0:T(8,128)(2,1)} %get-tuple-element.58.left_ref, ...), custom_call_target="tpu_custom_call" | custom-call | flops 8589934592 | bytes 16777216 | tf_op jit(solution)/shard_map/exchange/pallas_call | solution.py:486
  255.2 2.3 collective-permute-start.8
  258.8 22.3 %collective-permute-done.8.refs_0_ = f32[256,2048]{1,0:T(8,128)S(1)} collective-permute-done((f32[256,2048]{1,0:T(8,128)}, f32[256,2048]{1,0:T(8,128)S(1)}, u32[]{:S(2)}, u32[]{:S(2)}) %collective-permute-start.8) | collective-permute-done | bytes 2097184 | tf_op jit(solution)/shard_map/ppermute | solution.py:427
  285.1 18.5 %collective-permute-done.refs_0_ = f32[256,2048]{1,0:T(8,128)S(1)} collective-permute-done((f32[256,2048]{1,0:T(8,128)}, f32[256,2048]{1,0:T(8,128)S(1)}, u32[]{:S(2)}, u32[]{:S(2)}) %collective-permute-start) | collective-permute-done | bytes 2097184 | tf_op jit(solution)/shard_map/ppermute | solution.py:427
  311.4 19.3 %collective-permute-done.9.refs_0_ = f32[256,2048]{1,0:T(8,128)} collective-permute-done((f32[256,2048]{1,0:T(8,128)S(1)}, f32[256,2048]{1,0:T(8,128)}, u32[]{:S(2)}, u32[]{:S(2)}) %collective-permute-start.9) | collective-permute-done | bytes 2097184 | tf_op jit(solution)/shard_map/ppermute | solution.py:427
  335.7 17.4 %collective-permute-done.1.refs_0_ = f32[256,2048]{1,0:T(8,128)} collective-permute-done((f32[256,2048]{1,0:T(8,128)S(1)}, f32[256,2048]{1,0:T(8,128)}, u32[]{:S(2)}, u32[]{:S(2)}) %collective-permute-start.1) | collective-permute-done | bytes 2097184 | tf_op jit(solution)/shard_map/ppermute | solution.py:427
  353.1 2.2 collective-permute-start.13
  357.5 6.2 %fusion.3 = f32[256,2048]{1,0:T(8,128)S(1)} fusion(bf16[2048,2048]{1,0:T(8,128)(2,1)} %wq_ref.1, bf16[4,256,2048]{2,1,0:T(8,128)(2,1)} %get-tuple-element.59.right_ref), kind=kOutput, calls=%fused_computation.6 | convolution fusion | flops 2147483648 | bytes 11534336 | tf_op jit(solution)/shard_map/ne,de->nd/dot_general | solution.py:433
  365.7 8.0 %convolution_add_fusion.1 = f32[256,2048]{1,0:T(8,128)} fusion(f32[256,2048]{1,0:T(8,128)S(1)} %fusion.3, bf16[2048,2048]{1,0:T(8,128)(2,1)} %wk_ref.1, bf16[4,256,2048]{2,1,0:T(8,128)(2,1)S(1)} %copy-done.16), kind=kOutput, calls=%fused_computation.1 | convolution fusion | flops 2148007936 | bytes 13631488 | tf_op jit(solution)/shard_map/ne,de->nd/dot_general | solution.py:433
  373.7 5.0 %fusion = bf16[256,2048]{1,0:T(8,128)(2,1)} fusion(f32[256,2048]{1,0:T(8,128)} %convolution_add_fusion.1, bf16[2048,2048]{1,0:T(8,128)(2,1)S(1)} %bitcast.17, bf16[4,256,2048]{2,1,0:T(8,128)(2,1)S(1)} %copy-done.16), kind=kOutput, calls=%fused_computation.2 | convolution fusion | flops 2148532224 | bytes 12582912 | tf_op jit(solution)/shard_map/ne,de->nd/dot_general | solution.py:433
  378.6 6.6 %shard_map.109 = (f32[2048,2048]{1,0:T(8,128)}, f32[2048,2048]{1,0:T(8,128)}, f32[2048,2048]{1,0:T(8,128)}, f32[2048,2048]{1,0:T(8,128)}) custom-call(f32[256,2048]{1,0:T(8,128)} %get-tuple-element.62.refs_0_, f32[256,2048]{1,0:T(8,128)} %get-tuple-element.63.refs_1_, f32[256,2048]{1,0:T(8,128)} %get-tuple-element.66.refs_2_, ...), custom_call_target="tpu_custom_call" | custom-call | flops 3000000000 | bytes 67108864 | tf_op jit(solution)/shard_map/pallas_call | solution.py:534
  386.0 6.6 %shard_map.110 = (f32[2048,2048]{1,0:T(8,128)}, f32[2048,2048]{1,0:T(8,128)}, f32[2048,2048]{1,0:T(8,128)}, f32[2048,2048]{1,0:T(8,128)}) custom-call(f32[256,2048]{1,0:T(8,128)} %get-tuple-element.60.refs_0_, f32[256,2048]{1,0:T(8,128)} %get-tuple-element.61.refs_1_, ...), custom_call_target="tpu_custom_call", output_to_operand_aliasing={{0}: (4, {}), {1}: (5, {}), {2}: (6, {}), {3}: (7, {})} | custom-call | flops 3000000000 | bytes 67108864 | tf_op jit(solution)/shard_map/pallas_call | solution.py:534
  392.5 5.5 %collective-permute-done.2.refs_0_ = f32[256,2048]{1,0:T(8,128)} collective-permute-done((f32[256,2048]{1,0:T(8,128)}, f32[256,2048]{1,0:T(8,128)}, u32[]{:S(2)}, u32[]{:S(2)}) %collective-permute-start.2) | collective-permute-done | bytes 2097184 | tf_op jit(solution)/shard_map/ppermute | solution.py:427
  401.1 4.1 collective-permute-start.7
  405.2 7.0 %convolution_convert_fusion = bf16[256,2048]{1,0:T(8,128)(2,1)} fusion(bf16[2048,2048]{1,0:T(8,128)(2,1)} %wo_ref.1, bf16[2,256,2048]{2,1,0:T(8,128)(2,1)} %get-tuple-element.58.left_ref), kind=kOutput, calls=%fused_computation.3 | convolution fusion | flops 2148007936 | bytes 10485760 | tf_op jit(solution)/shard_map/dot_general | solution.py:430
  412.3 6.6 %shard_map.111 = (f32[2048,2048]{1,0:T(8,128)}, f32[2048,2048]{1,0:T(8,128)}, f32[2048,2048]{1,0:T(8,128)}, f32[2048,2048]{1,0:T(8,128)}) custom-call(f32[256,2048]{1,0:T(8,128)} %copy-done.7, f32[256,2048]{1,0:T(8,128)} %copy-done.8, f32[256,2048]{1,0:T(8,128)} %copy-done.9, ...), custom_call_target="tpu_custom_call", output_to_operand_aliasing={{0}: (4, {}), {1}: (5, {}), {2}: (6, {}), {3}: (7, {})} | custom-call | flops 3000000000 | bytes 67108864 | tf_op jit(solution)/shard_map/pallas_call | solution.py:534
  418.8 6.6 %shard_map.112 = (f32[2048,2048]{1,0:T(8,128)}, f32[2048,2048]{1,0:T(8,128)}, f32[2048,2048]{1,0:T(8,128)}, f32[2048,2048]{1,0:T(8,128)}) custom-call(f32[256,2048]{1,0:T(8,128)} %copy-done.5, f32[256,2048]{1,0:T(8,128)} %copy-done.6, f32[256,2048]{1,0:T(8,128)} %copy-done.10, ...), custom_call_target="tpu_custom_call", output_to_operand_aliasing={{0}: (4, {}), {1}: (5, {}), {2}: (6, {}), {3}: (7, {})} | custom-call | flops 3000000000 | bytes 67108864 | tf_op jit(solution)/shard_map/pallas_call | solution.py:534
  425.4 6.6 %shard_map.113 = (f32[2048,2048]{1,0:T(8,128)}, f32[2048,2048]{1,0:T(8,128)}, f32[2048,2048]{1,0:T(8,128)}, f32[2048,2048]{1,0:T(8,128)}) custom-call(f32[256,2048]{1,0:T(8,128)} %collective-permute-done.9.refs_0_, f32[256,2048]{1,0:T(8,128)} %collective-permute-done.12.refs_1_, ...), custom_call_target="tpu_custom_call", output_to_operand_aliasing={{0}: (4, {}), {1}: (5, {}), {2}: (6, {}), {3}: (7, {})} | custom-call | flops 3000000000 | bytes 67108864 | tf_op jit(solution)/shard_map/pallas_call | solution.py:534
  432.0 6.6 %shard_map.114 = (f32[2048,2048]{1,0:T(8,128)}, f32[2048,2048]{1,0:T(8,128)}, f32[2048,2048]{1,0:T(8,128)}, f32[2048,2048]{1,0:T(8,128)}) custom-call(f32[256,2048]{1,0:T(8,128)} %collective-permute-done.1.refs_0_, f32[256,2048]{1,0:T(8,128)} %collective-permute-done.4.refs_1_, ...), custom_call_target="tpu_custom_call", output_to_operand_aliasing={{0}: (4, {}), {1}: (5, {}), {2}: (6, {}), {3}: (7, {})} | custom-call | flops 3000000000 | bytes 67108864 | tf_op jit(solution)/shard_map/pallas_call | solution.py:534
  439.9 6.6 %shard_map.115 = (f32[2048,2048]{1,0:T(8,128)}, f32[2048,2048]{1,0:T(8,128)}, f32[2048,2048]{1,0:T(8,128)}, f32[2048,2048]{1,0:T(8,128)}) custom-call(f32[256,2048]{1,0:T(8,128)} %collective-permute-done.10.refs_0_, f32[256,2048]{1,0:T(8,128)} %collective-permute-done.13.refs_1_, ...), custom_call_target="tpu_custom_call", output_to_operand_aliasing={{0}: (4, {}), {1}: (5, {}), {2}: (6, {}), {3}: (7, {})} | custom-call | flops 3000000000 | bytes 67108864 | tf_op jit(solution)/shard_map/pallas_call | solution.py:534
  446.5 6.6 %shard_map.116 = (f32[2048,2048]{1,0:T(8,128)}, f32[2048,2048]{1,0:T(8,128)}, f32[2048,2048]{1,0:T(8,128)}, f32[2048,2048]{1,0:T(8,128)}) custom-call(f32[256,2048]{1,0:T(8,128)} %collective-permute-done.2.refs_0_, f32[256,2048]{1,0:T(8,128)} %collective-permute-done.5.refs_1_, ...), custom_call_target="tpu_custom_call", output_to_operand_aliasing={{0}: (4, {}), {1}: (5, {}), {2}: (6, {}), {3}: (7, {})} | custom-call | flops 3000000000 | bytes 67108864 | tf_op jit(solution)/shard_map/pallas_call | solution.py:534
  (79 shorter events, 32.3 us)
Async XLA Ops:
  255.2 25.9 %collective-permute-start.8 = (f32[256,2048]{1,0:T(8,128)}, f32[256,2048]{1,0:T(8,128)S(1)}, u32[]{:S(2)}, u32[]{:S(2)}) collective-permute-start(f32[256,2048]{1,0:T(8,128)} %get-tuple-element.62.refs_0_), channel_id=1, source_target_pairs={{0,2},{1,7},{2,4},{3,1},{4,6},{5,3},{6,0},{7,5},{8,10},{9,15},{10,... | collective-permute-start | bytes 6291464 | tf_op jit(solution)/shard_map/ppermute | solution.py:427
  257.5 25.4 %collective-permute-start.11 = (f32[256,2048]{1,0:T(8,128)}, f32[256,2048]{1,0:T(8,128)S(1)}, u32[]{:S(2)}, u32[]{:S(2)}) collective-permute-start(f32[256,2048]{1,0:T(8,128)} %get-tuple-element.63.refs_1_), channel_id=1, source_target_pairs={{0,8},{1,25},{2,10},{3,27},{4,12},{5,29},{6,14},{7,31},{8,16},{9,1... | collective-permute-start | bytes 6291464 | tf_op jit(solution)/shard_map/ppermute | solution.py:427
  257.5 46.1 %collective-permute-start = (f32[256,2048]{1,0:T(8,128)}, f32[256,2048]{1,0:T(8,128)S(1)}, u32[]{:S(2)}, u32[]{:S(2)}) collective-permute-start(f32[256,2048]{1,0:T(8,128)} %get-tuple-element.60.refs_0_), channel_id=1, source_target_pairs={{0,2},{1,7},{2,4},{3,1},{4,6},{5,3},{6,0},{7,5},{8,10},{9,15},{10,... | collective-permute-start | bytes 6291464 | tf_op jit(solution)/shard_map/ppermute | solution.py:427
  258.7 47.9 %collective-permute-start.3 = (f32[256,2048]{1,0:T(8,128)}, f32[256,2048]{1,0:T(8,128)S(1)}, u32[]{:S(2)}, u32[]{:S(2)}) collective-permute-start(f32[256,2048]{1,0:T(8,128)} %get-tuple-element.61.refs_1_), channel_id=1, source_target_pairs={{0,8},{1,25},{2,10},{3,27},{4,12},{5,29},{6,14},{7,31},{8,16},{9,1... | collective-permute-start | bytes 6291464 | tf_op jit(solution)/shard_map/ppermute | solution.py:427
  281.1 26.5 %collective-permute-start.22 = (f32[256,2048]{1,0:T(8,128)S(1)}, f32[256,2048]{1,0:T(8,128)S(1)}, u32[]{:S(2)}, u32[]{:S(2)}) collective-permute-start(f32[256,2048]{1,0:T(8,128)S(1)} %collective-permute-done.8.refs_0_), channel_id=1, source_target_pairs={{0,1},{1,0},{2,3},{3,2},{4,5},{5,4},{6,7},{7,6},{8,9},{9,8},{10,11... | collective-permute-start | bytes 6291464 | tf_op jit(solution)/shard_map/ppermute | solution.py:424
  282.9 24.8 %collective-permute-start.23 = (f32[256,2048]{1,0:T(8,128)S(1)}, f32[256,2048]{1,0:T(8,128)S(1)}, u32[]{:S(2)}, u32[]{:S(2)}) collective-permute-start(f32[256,2048]{1,0:T(8,128)S(1)} %collective-permute-done.11.refs_1_), channel_id=1, source_target_pairs={{0,1},{1,0},{2,3},{3,2},{4,5},{5,4},{6,7},{7,6},{8,9},{9,8},{10,11... | collective-permute-start | bytes 6291464 | tf_op jit(solution)/shard_map/ppermute | solution.py:424
  303.6 6.0 %collective-permute-start.20 = (f32[256,2048]{1,0:T(8,128)S(1)}, f32[256,2048]{1,0:T(8,128)S(1)}, u32[]{:S(2)}, u32[]{:S(2)}) collective-permute-start(f32[256,2048]{1,0:T(8,128)S(1)} %collective-permute-done.refs_0_), channel_id=1, source_target_pairs={{0,1},{1,0},{2,3},{3,2},{4,5},{5,4},{6,7},{7,6},{8,9},{9,8},{10,11... | collective-permute-start | bytes 6291464 | tf_op jit(solution)/shard_map/ppermute | solution.py:424
  305.4 25.3 %collective-permute-start.9 = (f32[256,2048]{1,0:T(8,128)S(1)}, f32[256,2048]{1,0:T(8,128)}, u32[]{:S(2)}, u32[]{:S(2)}) collective-permute-start(f32[256,2048]{1,0:T(8,128)S(1)} %collective-permute-done.8.refs_0_), channel_id=1, source_target_pairs={{0,2},{1,7},{2,4},{3,1},{4,6},{5,3},{6,0},{7,5},{8,10},{9,15},{10,... | collective-permute-start | bytes 6291464 | tf_op jit(solution)/shard_map/ppermute | solution.py:427
  306.6 26.1 %collective-permute-start.12 = (f32[256,2048]{1,0:T(8,128)S(1)}, f32[256,2048]{1,0:T(8,128)}, u32[]{:S(2)}, u32[]{:S(2)}) collective-permute-start(f32[256,2048]{1,0:T(8,128)S(1)} %collective-permute-done.11.refs_1_), channel_id=1, source_target_pairs={{0,8},{1,25},{2,10},{3,27},{4,12},{5,29},{6,14},{7,31},{8,16},{9,1... | collective-permute-start | bytes 6291464 | tf_op jit(solution)/shard_map/ppermute | solution.py:427
  307.7 27.2 %collective-permute-start.21 = (f32[256,2048]{1,0:T(8,128)S(1)}, f32[256,2048]{1,0:T(8,128)S(1)}, u32[]{:S(2)}, u32[]{:S(2)}) collective-permute-start(f32[256,2048]{1,0:T(8,128)S(1)} %collective-permute-done.3.refs_1_), channel_id=1, source_target_pairs={{0,1},{1,0},{2,3},{3,2},{4,5},{5,4},{6,7},{7,6},{8,9},{9,8},{10,11... | collective-permute-start | bytes 6291464 | tf_op jit(solution)/shard_map/ppermute | solution.py:424
  307.7 45.4 %collective-permute-start.1 = (f32[256,2048]{1,0:T(8,128)S(1)}, f32[256,2048]{1,0:T(8,128)}, u32[]{:S(2)}, u32[]{:S(2)}) collective-permute-start(f32[256,2048]{1,0:T(8,128)S(1)} %collective-permute-done.refs_0_), channel_id=1, source_target_pairs={{0,2},{1,7},{2,4},{3,1},{4,6},{5,3},{6,0},{7,5},{8,10},{9,15},{10,... | collective-permute-start | bytes 6291464 | tf_op jit(solution)/shard_map/ppermute | solution.py:427
  309.6 45.7 %collective-permute-start.4 = (f32[256,2048]{1,0:T(8,128)S(1)}, f32[256,2048]{1,0:T(8,128)}, u32[]{:S(2)}, u32[]{:S(2)}) collective-permute-start(f32[256,2048]{1,0:T(8,128)S(1)} %collective-permute-done.3.refs_1_), channel_id=1, source_target_pairs={{0,8},{1,25},{2,10},{3,27},{4,12},{5,29},{6,14},{7,31},{8,16},{9,1... | collective-permute-start | bytes 6291464 | tf_op jit(solution)/shard_map/ppermute | solution.py:427
  330.7 33.1 %collective-permute-start.18 = (f32[256,2048]{1,0:T(8,128)}, f32[256,2048]{1,0:T(8,128)S(1)}, u32[]{:S(2)}, u32[]{:S(2)}) collective-permute-start(f32[256,2048]{1,0:T(8,128)} %collective-permute-done.9.refs_0_), channel_id=1, source_target_pairs={{0,1},{1,0},{2,3},{3,2},{4,5},{5,4},{6,7},{7,6},{8,9},{9,8},{10,11... | collective-permute-start | bytes 6291464 | tf_op jit(solution)/shard_map/ppermute | solution.py:424
  332.7 31.9 %collective-permute-start.19 = (f32[256,2048]{1,0:T(8,128)}, f32[256,2048]{1,0:T(8,128)S(1)}, u32[]{:S(2)}, u32[]{:S(2)}) collective-permute-start(f32[256,2048]{1,0:T(8,128)} %collective-permute-done.12.refs_1_), channel_id=1, source_target_pairs={{0,1},{1,0},{2,3},{3,2},{4,5},{5,4},{6,7},{7,6},{8,9},{9,8},{10,11... | collective-permute-start | bytes 6291464 | tf_op jit(solution)/shard_map/ppermute | solution.py:424
  334.9 50.3 %collective-permute-start.10 = (f32[256,2048]{1,0:T(8,128)}, f32[256,2048]{1,0:T(8,128)}, u32[]{:S(2)}, u32[]{:S(2)}) collective-permute-start(f32[256,2048]{1,0:T(8,128)} %collective-permute-done.9.refs_0_), channel_id=1, source_target_pairs={{0,2},{1,7},{2,4},{3,1},{4,6},{5,3},{6,0},{7,5},{8,10},{9,15},{10,... | collective-permute-start | bytes 6291464 | tf_op jit(solution)/shard_map/ppermute | solution.py:427
  353.1 32.7 %collective-permute-start.13 = (f32[256,2048]{1,0:T(8,128)}, f32[256,2048]{1,0:T(8,128)}, u32[]{:S(2)}, u32[]{:S(2)}) collective-permute-start(f32[256,2048]{1,0:T(8,128)} %collective-permute-done.12.refs_1_), channel_id=1, source_target_pairs={{0,8},{1,25},{2,10},{3,27},{4,12},{5,29},{6,14},{7,31},{8,16},{9,1... | collective-permute-start | bytes 6291464 | tf_op jit(solution)/shard_map/ppermute | solution.py:427
  355.4 23.2 %collective-permute-start.16 = (f32[256,2048]{1,0:T(8,128)}, f32[256,2048]{1,0:T(8,128)}, u32[]{:S(2)}, u32[]{:S(2)}) collective-permute-start(f32[256,2048]{1,0:T(8,128)} %collective-permute-done.1.refs_0_), channel_id=1, source_target_pairs={{0,1},{1,0},{2,3},{3,2},{4,5},{5,4},{6,7},{7,6},{8,9},{9,8},{10,11... | collective-permute-start | bytes 6291464 | tf_op jit(solution)/shard_map/ppermute | solution.py:424
  363.8 34.3 %collective-permute-start.2 = (f32[256,2048]{1,0:T(8,128)}, f32[256,2048]{1,0:T(8,128)}, u32[]{:S(2)}, u32[]{:S(2)}) collective-permute-start(f32[256,2048]{1,0:T(8,128)} %collective-permute-done.1.refs_0_), channel_id=1, source_target_pairs={{0,2},{1,7},{2,4},{3,1},{4,6},{5,3},{6,0},{7,5},{8,10},{9,15},{10,... | collective-permute-start | bytes 6291464 | tf_op jit(solution)/shard_map/ppermute | solution.py:427
  364.7 36.4 %collective-permute-start.5 = (f32[256,2048]{1,0:T(8,128)}, f32[256,2048]{1,0:T(8,128)}, u32[]{:S(2)}, u32[]{:S(2)}) collective-permute-start(f32[256,2048]{1,0:T(8,128)} %collective-permute-done.4.refs_1_), channel_id=1, source_target_pairs={{0,8},{1,25},{2,10},{3,27},{4,12},{5,29},{6,14},{7,31},{8,16},{9,1... | collective-permute-start | bytes 6291464 | tf_op jit(solution)/shard_map/ppermute | solution.py:427
  378.6 53.3 %collective-permute-start.17 = (f32[256,2048]{1,0:T(8,128)}, f32[256,2048]{1,0:T(8,128)}, u32[]{:S(2)}, u32[]{:S(2)}) collective-permute-start(f32[256,2048]{1,0:T(8,128)} %collective-permute-done.4.refs_1_), channel_id=1, source_target_pairs={{0,1},{1,0},{2,3},{3,2},{4,5},{5,4},{6,7},{7,6},{8,9},{9,8},{10,11... | collective-permute-start | bytes 6291464 | tf_op jit(solution)/shard_map/ppermute | solution.py:424
  385.2 53.3 %collective-permute-start.14 = (f32[256,2048]{1,0:T(8,128)}, f32[256,2048]{1,0:T(8,128)S(1)}, u32[]{:S(2)}, u32[]{:S(2)}) collective-permute-start(f32[256,2048]{1,0:T(8,128)} %collective-permute-done.10.refs_0_), channel_id=1, source_target_pairs={{0,1},{1,0},{2,3},{3,2},{4,5},{5,4},{6,7},{7,6},{8,9},{9,8},{10,11... | collective-permute-start | bytes 6291464 | tf_op jit(solution)/shard_map/ppermute | solution.py:424
  385.8 52.7 %collective-permute-start.15 = (f32[256,2048]{1,0:T(8,128)}, f32[256,2048]{1,0:T(8,128)}, u32[]{:S(2)}, u32[]{:S(2)}) collective-permute-start(f32[256,2048]{1,0:T(8,128)} %collective-permute-done.13.refs_1_), channel_id=1, source_target_pairs={{0,1},{1,0},{2,3},{3,2},{4,5},{5,4},{6,7},{7,6},{8,9},{9,8},{10,11... | collective-permute-start | bytes 6291464 | tf_op jit(solution)/shard_map/ppermute | solution.py:424
  398.1 48.4 %collective-permute-start.6 = (f32[256,2048]{1,0:T(8,128)}, f32[256,2048]{1,0:T(8,128)}, u32[]{:S(2)}, u32[]{:S(2)}) collective-permute-start(f32[256,2048]{1,0:T(8,128)} %collective-permute-done.2.refs_0_), channel_id=1, source_target_pairs={{0,1},{1,0},{2,3},{3,2},{4,5},{5,4},{6,7},{7,6},{8,9},{9,8},{10,11... | collective-permute-start | bytes 6291464 | tf_op jit(solution)/shard_map/ppermute | solution.py:424
  401.1 45.4 %collective-permute-start.7 = (f32[256,2048]{1,0:T(8,128)}, f32[256,2048]{1,0:T(8,128)}, u32[]{:S(2)}, u32[]{:S(2)}) collective-permute-start(f32[256,2048]{1,0:T(8,128)} %collective-permute-done.5.refs_1_), channel_id=1, source_target_pairs={{0,1},{1,0},{2,3},{3,2},{4,5},{5,4},{6,7},{7,6},{8,9},{9,8},{10,11... | collective-permute-start | bytes 6291464 | tf_op jit(solution)/shard_map/ppermute | solution.py:424
  (19 other events, 593.5 us)

commit v5 on v4

v5 whole, which is shorter than its diff:
```python
import functools
import math
import jax
import jax.numpy as jnp
from jax import lax
from jax.experimental import pallas as pl
from jax.experimental.pallas import tpu as pltpu
from jax.sharding import PartitionSpec as P


HEAD_DIM = 128
BLOCK_LEN = 128
N_CORES = 2
N_GRADS = 4
RELAY_STEP = 7
SLOTS = 2


F32 = jnp.float32
BF16 = jnp.bfloat16
VMEM = pltpu.VMEM
MESH = pl.DeviceIdType.MESH


def dot(a, b, dims):
    return lax.dot_general(a, b, ((dims[:1], dims[1:]), ((), ())), preferred_element_type=F32)


def neighbours(me, side):
    core = lax.rem(me, N_CORES)
    sign = 1 - 2 * core
    col = lax.rem(me // N_CORES, side)
    row = me // (N_CORES * side)

    def wrap(value):
        return lax.rem(value + 2 * side, side)

    def device(r, c):
        return (r * side + c) * N_CORES + core

    ahead = (device(row, wrap(col + sign)), device(wrap(row + sign), col))
    behind = (device(row, wrap(col - sign)), device(wrap(row - sign), col))
    return core, sign, (col, row), ahead, behind, wrap


def remote(src, dst, send, recv, target):
    return pltpu.make_async_remote_copy(src_ref=src, dst_ref=dst, send_sem=send, recv_sem=recv, device_id={"sp": target}, device_id_type=MESH)


def chain(side, totals_ref, out_ref, other, before, stage, above, down, peer, swap_send, swap_recv, row_send, row_recv, above_recv, down_send, cast_send, back_send, back_recv):
    me = lax.axis_index("sp")
    core = lax.rem(me, N_CORES)
    col = lax.rem(me // N_CORES, side)
    row = me // (N_CORES * side)
    partner = me + 1 - 2 * core
    n_group = totals_ref.shape[1] // N_CORES
    mine, yours = core * n_group, (1 - core) * n_group

    def wrap(value):
        return lax.rem(value + 2 * side, side)

    def device(r, c):
        return (wrap(r) * side + wrap(c)) * N_CORES + core

    def copy(src, dst, send, recv, target):
        return pltpu.make_async_remote_copy(src_ref=src, dst_ref=dst, send_sem=send, recv_sem=recv, device_id={"sp": target}, device_id_type=MESH)

    def swap_copy(kind):
        return copy(totals_ref.at[kind, pl.ds(yours, n_group)], other.at[kind], swap_send.at[kind], swap_recv.at[kind], partner)

    def row_copy(kind, h):
        return copy(stage.at[kind, h], before.at[kind, h], row_send.at[kind, h], row_recv.at[kind, h], device(row, col + 1 - 2 * kind))

    def down_copy(kind, h):
        return copy(down.at[kind, h], above.at[kind, h], down_send.at[kind, h], above_recv.at[kind, h], device(row + 1 - 2 * kind, col))

    def cast_copy(kind, h, t):
        return copy(above.at[kind, h], above.at[kind, h], cast_send.at[kind, h, t - 1], above_recv.at[kind, h], device(row, col + t))

    def back_copy(kind, h):
        return copy(peer.at[kind, h], out_ref.at[kind, mine + h], back_send.at[kind, h], back_recv.at[kind, h], partner)

    def position(kind, coordinate):
        return kind * (side - 1) + (1 - 2 * kind) * coordinate

    for kind in range(2):
        swap_copy(kind).start()
    for kind in range(2):

        @pl.when(position(kind, col) == 0)
        def _():
            before[kind] = jnp.zeros_like(before[kind])

        @pl.when((position(kind, col) == side - 1) & (position(kind, row) == 0))
        def _():
            above[kind] = jnp.zeros_like(above[kind])

    for kind in range(2):
        swap_copy(kind).wait()

    def run(slot, carry):
        for kind in range(2):
            along, across = position(kind, col), position(kind, row)
            h = slot - SLOTS * along

            @pl.when((h >= 0) & (h < n_group))
            def _():
                @pl.when(along > 0)
                def _():
                    row_copy(kind, h).wait_recv()

                stage[kind, h] = before[kind, h] + (totals_ref[kind, mine + h] + other[kind, h])

                @pl.when(along < side - 1)
                def _():
                    row_copy(kind, h).start()

            g = slot - SLOTS * (side - 1 + across)

            @pl.when((along == side - 1) & (g >= 0) & (g < n_group))
            def _():
                @pl.when(across > 0)
                def _():
                    down_copy(kind, g).wait_recv()

                @pl.when(across < side - 1)
                def _():
                    down[kind, g] = above[kind, g] + stage[kind, g]
                    down_copy(kind, g).start()

                for t in range(1, side):
                    cast_copy(kind, g, t).start()

        return carry

    lax.fori_loop(0, 2 * SLOTS * (side - 1) + n_group, run, 0)

    def finish(h, carry):
        for kind in range(2):

            @pl.when(position(kind, col) < side - 1)
            def _():
                down_copy(kind, h).wait_recv()

            base = above[kind, h] + before[kind, h]
            own_total, other_total = totals_ref[kind, mine + h], other[kind, h]
            out_ref[kind, mine + h] = jnp.where(core == kind, base, base + other_total)
            peer[kind, h] = jnp.where(core == kind, base + own_total, base)
            back_copy(kind, h).start()
        return carry

    lax.fori_loop(0, n_group, finish, 0)

    def drain(h, carry):
        for kind in range(2):
            along, across = position(kind, col), position(kind, row)
            back_copy(kind, h).wait()

            @pl.when(along < side - 1)
            def _():
                row_copy(kind, h).wait_send()

            @pl.when(along == side - 1)
            def _():
                for t in range(1, side):
                    cast_copy(kind, h, t).wait_send()

                @pl.when(across < side - 1)
                def _():
                    down_copy(kind, h).wait_send()

        return carry

    lax.fori_loop(0, n_group, drain, 0)


def project_kernel(side, x_ref, dy_ref, wq_ref, wk_ref, wv_ref, wo_ref, x_any, dy_any, q_ref, k_ref, v_ref, do_ref, early_ref, states_ref, totals, states, relay, send_sem, recv_sem, own_sem, *chain_refs):
    core, sign, at, ahead, behind, wrap = neighbours(lax.axis_index("sp"), side)
    half = early_ref.shape[3]
    step = pl.program_id(0)

    def early(part, kind, src):
        dst = relay.at[part] if kind == 3 else early_ref.at[part, kind]
        return remote(src, dst, send_sem.at[part, kind], recv_sem.at[part, kind], behind[part] if kind == 1 else ahead[part])

    def source(part, array):
        return array.at[:, pl.ds(part * half, half)]

    def start_to(part, kind, which):
        @pl.when(which < N_GRADS - 1)
        def _():
            early(part, kind, source(part, x_any)).start()

        @pl.when(which == N_GRADS - 1)
        def _():
            early(part, kind, source(part, dy_any)).start()

    def own(part, array):
        return pltpu.make_async_copy(source(part, array), early_ref.at[part, 3], own_sem.at[part])

    @pl.when(step == 0)
    def _():
        barrier = pltpu.get_barrier_semaphore()
        me = lax.axis_index("sp")
        first_in_row = at[1] * side * N_CORES + core
        peers = [first_in_row + wrap(at[0] + t) * N_CORES for t in range(1, side)] + [ahead[1], behind[1], me + sign]
        for target in peers:
            pl.semaphore_signal(barrier, inc=1, device_id={"sp": target}, device_id_type=MESH)
        pl.semaphore_wait(barrier, len(peers))
        for part in range(2):
            start_to(part, 3, wrap(at[part] + 2))
        for part in range(2):
            start_to(part, 1, wrap(at[part] - sign))
        for part in range(2):
            start_to(part, 0, wrap(at[part] + sign))

            @pl.when(at[part] < N_GRADS - 1)
            def _():
                own(part, x_any).start()

            @pl.when(at[part] == N_GRADS - 1)
            def _():
                own(part, dy_any).start()

    @pl.when(step == RELAY_STEP)
    def _():
        for part in range(2):
            early(part, 3, source(part, x_any)).wait_recv()
            early(part, 2, relay.at[part]).start()

    x = x_ref[...]
    q_ref[...] = dot(x, wq_ref[...], (1, 0)).astype(BF16)
    k_ref[...] = dot(x, wk_ref[...], (1, 0)).astype(BF16)
    v_ref[...] = dot(x, wv_ref[...], (1, 0)).astype(BF16)
    do_ref[...] = dot(dy_ref[...], wo_ref[...], (1, 1)).astype(BF16)
    for head in range(q_ref.shape[1] // HEAD_DIM):
        cols = slice(head * HEAD_DIM, (head + 1) * HEAD_DIM)
        kv = dot(k_ref[:, cols], v_ref[:, cols], (0, 0))
        qdo = dot(q_ref[:, cols], do_ref[:, cols], (0, 0))
        at_head = step * (q_ref.shape[1] // HEAD_DIM) + head
        totals[0, at_head] = kv
        totals[1, at_head] = qdo

    @pl.when(step == pl.num_programs(0) - 1)
    def _():
        chain(side, totals, states, *chain_refs)
        result = pltpu.make_async_copy(states, states_ref, own_sem.at[2])
        result.start()
        result.wait()
        for part in range(2):
            own(part, x_any).wait()
            for kind in range(4):
                copy = early(part, kind, source(part, x_any))
                copy.wait_send()
                if kind != 3:
                    copy.wait_recv()


def attend_kernel(scale, q_ref, k_ref, v_ref, do_ref, dy_ref, state_ref, out_ref, late_ref):
    n_blocks = q_ref.shape[0] // BLOCK_LEN
    rows = [pl.ds(b * BLOCK_LEN, BLOCK_LEN) for b in range(n_blocks)]
    fwd = [state_ref[0, 0]]
    for b in range(n_blocks - 1):
        fwd.append(fwd[-1] + dot(k_ref[rows[b]], v_ref[rows[b]], (0, 0)))
    rev = [state_ref[1, 0]]
    for b in range(n_blocks - 1, 0, -1):
        rev.insert(0, rev[0] + dot(q_ref[rows[b]], do_ref[rows[b]], (0, 0)))
    shape = (BLOCK_LEN, BLOCK_LEN)
    causal = lax.broadcasted_iota(jnp.int32, shape, 0) >= lax.broadcasted_iota(jnp.int32, shape, 1)
    for b in range(n_blocks):
        q, k, v, do = q_ref[rows[b]], k_ref[rows[b]], v_ref[rows[b]], do_ref[rows[b]]
        s = fwd[b].astype(BF16)
        r = rev[b].astype(BF16)
        att = jnp.where(causal, dot(q, k, (1, 1)), 0.0).astype(BF16)
        d_att = jnp.where(causal, dot(do, v, (1, 1)), 0.0).astype(BF16)
        out_ref[rows[b], :] = ((dot(att, v, (1, 0)) + dot(q, s, (1, 0))) * scale).astype(BF16)
        late_ref[0, rows[b]] = ((dot(d_att, k, (1, 0)) + dot(do, s, (1, 1))) * scale).astype(BF16)
        late_ref[1, rows[b]] = ((dot(d_att, q, (0, 0)) + dot(v, r, (1, 1))) * scale).astype(BF16)
        late_ref[2, rows[b]] = ((dot(att, do, (0, 0)) + dot(k, r, (1, 0))) * scale).astype(BF16)
    first_half = pl.program_id(0) < pl.num_programs(0) // 2

    @pl.when(first_half)
    def _():
        late_ref[3] = out_ref[...]
        late_ref[4] = dy_ref[...]

    @pl.when(jnp.logical_not(first_half))
    def _():
        late_ref[3] = dy_ref[...]
        late_ref[4] = out_ref[...]


def exchange_kernel(side, halves, early_ref, late_ref, *refs):
    own_outs, other_outs = refs[: 2 * halves], refs[2 * halves : 4 * halves]
    early, near, far, pair_early, pair_late, total, landed, gathered = refs[4 * halves : -9]
    send_sem, recv_sem, early_sem, ring_send, ring_recv, out_sem, swap_send, swap_recv, load_sem = refs[-9:]
    me = lax.axis_index("sp")
    core, sign, at, ahead, behind, wrap = neighbours(me, side)
    partner = me + sign

    barrier = pltpu.get_barrier_semaphore()
    for other in ahead + behind + (partner,):
        pl.semaphore_signal(barrier, inc=1, device_id={"sp": other}, device_id_type=MESH)
    pl.semaphore_wait(barrier, 5)

    half = early_ref.shape[3]
    block = half // N_CORES

    def send(*args):
        copy = remote(*args)
        copy.start()
        return copy

    def late_of(which, part):
        return late_ref.at[which + part * (which // (N_GRADS - 1))]

    copies = {}

    def start(part, kind, src, dst, target):
        copies[part, kind] = send(src, dst, send_sem.at[part, kind], recv_sem.at[part, kind], target)

    for part in range(2):
        start(part, 3, late_of(wrap(at[part] + 2), part), far.at[part], ahead[part])
    for part in range(2):
        start(part, 1, late_of(wrap(at[part] - sign), part), near.at[part, 1], behind[part])
        start(part, 7, late_of(at[part], part), pair_late.at[part, 3], partner)
    for part in range(2):
        start(part, 0, late_of(wrap(at[part] + sign), part), near.at[part, 0], ahead[part])
    load = pltpu.make_async_copy(early_ref, early, load_sem.at[0])
    load.start()
    shares = [send(early_ref.at[part], pair_early.at[part], early_sem.at[0, part], early_sem.at[1, part], partner) for part in range(2)]

    n_tiles = 2
    width = half // n_tiles

    def my_cols(start):
        return pl.ds(pl.multiple_of(start + core * block, block), block)

    def accumulate(part, early_part, late_part, fresh=False):
        def add(left_value, right, offset, right_offset):
            def tile(t, carry):
                cols = pl.ds(pl.multiple_of(offset + t * width, width), width)
                product = dot(left_value, right[:, pl.ds(pl.multiple_of(right_offset + t * width, width), width)], (0, 0))
                if fresh:
                    total[part, :, cols] = product
                else:
                    total[part, :, cols] += product
                return carry

            return tile

        @pl.when(at[part] < N_GRADS - 1)
        def _():
            lax.fori_loop(0, 2 * n_tiles, add(early_part[:, my_cols(0)], late_part, 0, 0), 0)

        @pl.when(at[part] == N_GRADS - 1)
        def _():
            left_value = late_part[:, my_cols(part * half)]
            lax.fori_loop(0, n_tiles, add(left_value, early_part, part * half, 0), 0)
            lax.fori_loop(0, n_tiles, add(left_value, late_part, (1 - part) * half, (1 - part) * half), 0)

    def take(part, slot):
        copies[part, slot].wait_recv()
        start(part, 4 + slot, near.at[part, slot], pair_late.at[part, slot], partner)
        accumulate(part, early.at[part, slot], near.at[part, slot])

    def take_other(part, slot):
        copies[part, 4 + slot].wait_recv()
        accumulate(part, pair_early.at[part, slot], pair_late.at[part, slot])

    load.wait()
    for part in range(2):
        accumulate(part, early.at[part, 3], late_of(at[part], part), fresh=True)
    for part in range(2):
        shares[part].wait_recv()
        take_other(part, 3)
    for part in range(2):
        copies[part, 3].wait_recv()
        start(part, 2, far.at[part], near.at[part, 2], ahead[part])
    for slot in (1, 0, 2):
        for part in range(2):
            take(part, slot)
        for part in range(2):
            take_other(part, slot)

    piece = block // side
    small = piece // halves

    def rows(part, shift, h):
        return pl.ds(pl.multiple_of(wrap(at[1 - part] + sign * shift) * piece + h * small, small), small)

    def ring(part, h, step, src, dst):
        return send(src, dst, ring_send.at[part, h, step], ring_recv.at[part, h, step], ahead[1 - part])

    lanes = [(part, h) for h in range(halves) for part in range(2)]
    hops = {}
    for part, h in lanes:
        hops[part, h, 0] = ring(part, h, 0, total.at[part, rows(part, -1, h)], landed.at[part, h, 0])
    for step in range(1, side - 1):
        for part, h in lanes:
            hops[part, h, step - 1].wait_recv()
            landed[part, h, step - 1] += total[part, rows(part, -(step + 1), h), :]
            hops[part, h, step] = ring(part, h, step, landed.at[part, h, step - 1], landed.at[part, h, step])
    stores = []

    swaps = []

    def store(part, h, shift, n):
        src = gathered.at[part, rows(part, shift, h)]
        where = pl.ds(pl.multiple_of(wrap(at[1 - part] + sign * shift) * small, small), small)
        copy = pltpu.make_async_copy(src, own_outs[2 * h + part].at[where], out_sem.at[part, h, n])
        copy.start()
        stores.append(copy)
        swaps.append(send(src, other_outs[2 * h + part].at[where], swap_send.at[part, h, n], swap_recv.at[part, h, n], partner))

    last = side - 1
    for part, h in lanes:
        hops[part, h, last - 1].wait_recv()
        mine = rows(part, 0, h)
        gathered[part, mine, :] = landed[part, h, last - 1] + total[part, mine, :]
        hops[part, h, last] = ring(part, h, last, gathered.at[part, mine], gathered.at[part, mine])
        store(part, h, 0, 0)
    for step in range(1, side):
        for part, h in lanes:
            hops[part, h, last + step - 1].wait_recv()
            where = rows(part, -step, h)
            if step < side - 1:
                hops[part, h, last + step] = ring(part, h, last + step, gathered.at[part, where], gathered.at[part, where])
            store(part, h, -step, step)
    for copy in stores:
        copy.wait()
    for copy in list(copies.values()) + shares:
        copy.wait_send()
    for copy in hops.values():
        copy.wait_send()
    for copy in swaps:
        copy.wait()


def place_kernel(side, step, lane, halves, fresh, *refs):
    blocks = refs[:4]
    grads = refs[4 if fresh else 4 + N_GRADS :][:N_GRADS]
    buf, sem_in, sem_out = refs[-3:]
    index = lax.axis_index("sp")
    core = lax.rem(index, N_CORES)
    col = lax.rem(index // N_CORES, side)
    row = index // (N_CORES * side)
    small = blocks[0].shape[0] // side
    piece = small * halves
    half = grads[0].shape[0] // 2
    jobs = []
    for k, src in enumerate(blocks):
        own, part = k < 2, k % 2
        at = col if part == 0 else row
        c = core if own else 1 - core
        which = lax.rem(at - (1 - 2 * c) * step + 2 * side, side)
        start = part * half + c * side * piece + lane * small
        for g in range(side):
            jobs.append((src.at[pl.ds(g * small, small)], which, pl.multiple_of(start + g * piece, small)))
    for n, (src, which, start) in enumerate(jobs):
        pltpu.make_async_copy(src, buf.at[n], sem_in.at[n]).start()
    for n, (src, which, start) in enumerate(jobs):
        pltpu.make_async_copy(src, buf.at[n], sem_in.at[n]).wait()
        for m in range(N_GRADS):

            @pl.when(which == m)
            def _():
                pltpu.make_async_copy(buf.at[n], grads[m].at[pl.ds(start, small)], sem_out.at[n]).start()

    for n, (src, which, start) in enumerate(jobs):
        pltpu.make_async_copy(buf.at[n], grads[0].at[pl.ds(0, small)], sem_out.at[n]).wait()


def solution(mesh):
    n_seq = mesh.shape["sp"]
    side = math.isqrt(n_seq // N_CORES)
    row_spec = P(("dp", "sp"), None)
    grad_spec = P("dp", None)

    def device_at(row, col, core):
        return ((row % side) * side + col % side) * N_CORES + core

    def ring_perm(axis, hops):
        pairs = []
        for row in range(side):
            for col in range(side):
                for core in range(N_CORES):
                    shift = hops * (1 - 2 * core)
                    target = device_at(row, col + shift, core) if axis == "x" else device_at(row + shift, col, core)
                    pairs.append((device_at(row, col, core), target))
        return pairs

    core_perm = [(j, j ^ 1) for j in range(n_seq)]

    def local_layer(tokens, w_q, w_k, w_v, w_o, grad_y):
        n_rows, model_dim = tokens.shape
        n_heads = model_dim // HEAD_DIM
        att_scale = 1.0 / math.sqrt(n_rows * n_seq * HEAD_DIM)
        index = lax.axis_index("sp")
        core = lax.rem(index, N_CORES)
        place = {"x": lax.rem(index // N_CORES, side), "y": index // (N_CORES * side)}

        def swap_cores(value):
            return lax.ppermute(value, "sp", perm=core_perm)

        def hop(value, axis, hops):
            return lax.ppermute(value, "sp", perm=ring_perm(axis, hops))

        def project(operand, weight):
            return jnp.dot(operand, weight, preferred_element_type=F32).astype(BF16)

        def back_proj(rows, weight):
            return jnp.einsum("ne,de->nd", rows, weight, preferred_element_type=F32)

        tile = 2 * HEAD_DIM
        state_shape = (2, n_heads, HEAD_DIM, HEAD_DIM)
        full = pl.BlockSpec((n_rows, model_dim), lambda i: (0, 0))
        in_cols = pl.BlockSpec((model_dim, tile), lambda i: (0, i))
        in_rows = pl.BlockSpec((tile, model_dim), lambda i: (i, 0))
        out_cols = pl.BlockSpec((n_rows, tile), lambda i: (0, i))
        act = jax.ShapeDtypeStruct((n_rows, model_dim), BF16)
        half = model_dim // 2
        dma = pltpu.SemaphoreType.DMA
        anywhere = pl.BlockSpec(memory_space=pl.ANY)
        n_group = n_heads // N_CORES
        q, k, v, do, early, states = pl.pallas_call(
            functools.partial(project_kernel, side),
            grid=(model_dim // tile,),
            in_specs=[full, full, in_cols, in_cols, in_cols, in_rows, anywhere, anywhere],
            out_specs=[out_cols] * 4 + [anywhere] * 2,
            out_shape=[act] * 4 + [jax.ShapeDtypeStruct((2, 4, n_rows, half), BF16), jax.ShapeDtypeStruct(state_shape, F32)],
            scratch_shapes=[VMEM(state_shape, F32)] * 2
            + [VMEM((2, n_rows, half), BF16), dma((2, 4)), dma((2, 4)), dma((3,))]
            + [VMEM((2, n_group, HEAD_DIM, HEAD_DIM), F32)] * 6
            + [dma((2,))] * 2
            + [dma((2, n_group))] * 4
            + [dma((2, n_group, side - 1))]
            + [dma((2, n_group))] * 2,
            cost_estimate=pl.CostEstimate(flops=8 * n_rows * model_dim * model_dim, bytes_accessed=8 * model_dim * model_dim, transcendentals=0),
            compiler_params=pltpu.CompilerParams(collective_id=3, has_side_effects=True, vmem_limit_bytes=48 * 2**20),
            name="project",
        )(tokens, grad_y, w_q, w_k, w_v, w_o, tokens, grad_y)

        head_cols = pl.BlockSpec((n_rows, HEAD_DIM), lambda h: (0, h))
        out_rows, late = pl.pallas_call(
            functools.partial(attend_kernel, att_scale),
            grid=(n_heads,),
            in_specs=[head_cols] * 5 + [pl.BlockSpec((2, 1, HEAD_DIM, HEAD_DIM), lambda h: (0, h, 0, 0))],
            out_specs=[head_cols, pl.BlockSpec((5, n_rows, HEAD_DIM), lambda h: (0, 0, h))],
            out_shape=[act, jax.ShapeDtypeStruct((5, n_rows, model_dim), BF16)],
            cost_estimate=pl.CostEstimate(flops=n_heads * 24 * 2 * 128**3, bytes_accessed=2**24, transcendentals=0),
            compiler_params=pltpu.CompilerParams(vmem_limit_bytes=16 * 2**20),
            name="attend",
        )(q, k, v, do, grad_y, states)

        block = half // N_CORES
        halves = 2
        small = block // side // halves
        axes = (("x", "y"), ("y", "x"))
        blocks = pl.pallas_call(
            functools.partial(exchange_kernel, side, halves),
            in_specs=[anywhere, pl.BlockSpec(memory_space=VMEM)],
            out_specs=[anywhere] * (4 * halves),
            out_shape=[jax.ShapeDtypeStruct((block // halves, model_dim), F32)] * (4 * halves),
            scratch_shapes=[
                VMEM((2, 4, n_rows, half), BF16),
                VMEM((2, 3, n_rows, model_dim), BF16),
                VMEM((2, n_rows, model_dim), BF16),
                VMEM((2, 4, n_rows, half), BF16),
                VMEM((2, 4, n_rows, model_dim), BF16),
                VMEM((2, block, model_dim), F32),
                VMEM((2, halves, side - 1, small, model_dim), F32),
                VMEM((2, block, model_dim), F32),
                dma((2, 8)),
                dma((2, 8)),
                dma((2, 2)),
                dma((2, halves, 2 * (side - 1))),
                dma((2, halves, 2 * (side - 1))),
                dma((2, halves, side)),
                dma((2, halves, side)),
                dma((2, halves, side)),
                dma((1,)),
            ],
            cost_estimate=pl.CostEstimate(flops=2 * 2 * block * model_dim * n_rows * 8, bytes_accessed=2**24, transcendentals=0),
            compiler_params=pltpu.CompilerParams(collective_id=1, has_side_effects=True, vmem_limit_bytes=60 * 2**20),
            name="exchange",
        )(early, late)
        own = [list(blocks[2 * h : 2 * h + 2]) for h in range(halves)]
        others = [list(blocks[2 * (halves + h) : 2 * (halves + h) + 2]) for h in range(halves)]

        grads = []
        n_copies = 4 * side
        for step in range(side):
            for h in range(halves):
                if step:
                    for part, (first, second) in enumerate(axes):
                        own[h][part] = hop(own[h][part], first, 1)
                    others[h] = [swap_cores(b) for b in own[h]]
                fresh = not grads
                place_blocks = pl.pallas_call(
                    functools.partial(place_kernel, side, step, h, halves, fresh),
                    in_specs=[pl.BlockSpec(memory_space=pl.ANY)] * (4 + len(grads)),
                    out_specs=[pl.BlockSpec(memory_space=pl.ANY)] * N_GRADS,
                    out_shape=[jax.ShapeDtypeStruct((model_dim, model_dim), F32)] * N_GRADS,
                    scratch_shapes=[VMEM((n_copies, small, model_dim), F32), dma((n_copies,)), dma((n_copies,))],
                    input_output_aliases={} if fresh else {4 + m: m for m in range(N_GRADS)},
                    cost_estimate=pl.CostEstimate(flops=3 * 10**9, bytes_accessed=32 * n_copies * small * model_dim, transcendentals=0),
                )
                grads = place_blocks(*own[h], *others[h], *grads)

        out_y = project(out_rows, w_o)
        grad_x = back_proj(late[0], w_q)
        grad_x = grad_x + back_proj(late[1], w_k)
        grad_x = (grad_x + back_proj(late[2], w_v)).astype(BF16)
        return (out_y, grad_x) + tuple(grads)

    return jax.shard_map(local_layer, mesh=mesh, in_specs=(row_spec, P(), P(), P(), P(), row_spec), out_specs=(row_spec, row_spec, grad_spec, grad_spec, grad_spec, grad_spec), check_vma=False)
```

time: 454 us -> 430 us (0.947)
  Pallas kernels: 302 us -> 280 us
    pallas_call x1, Pallas kernels: 160 us -> 138 us  [local_layer(): pl.pallas_call(functools.partial(exchange_kernel, side, halves), in_specs...]
    pallas_call x2 -> x1, Pallas kernels: 72.9 us -> 75.6 us  [local_layer(): pl.pallas_call(functools.partial(project_kernel, side), grid=(model_dim /...]
  transfers between devices with their start and end apart: 24 -> 24, of which waited for: 6 -> 7; matrix products, arithmetic and copies ran while one was open for 6% -> 6% of each run, Pallas kernels for 10% -> 11%
where the time goes in v5:
time: 430 us; the launch traced here: 429 us
  Pallas kernels  280 us (65%)
  waiting for transfers between devices  86 us (20%)
  starting transfers between devices  32.3 us (8%)
  matrix products  23.7 us (6%)
  local copies, waits for them, and re-layouts  6.66 us (2%)
    pallas_call x1, Pallas kernels, local_layer(): pl.pallas_call(functools.partial(exchange_kernel, side, halves), in_specs...  138 us
    ppermute x12, waiting for transfers between devices, hop(): return lax.ppermute(value, 'sp', perm=ring_perm(axis, hops))  86 us
    pallas_call x1, Pallas kernels, local_layer(): pl.pallas_call(functools.partial(project_kernel, side), grid=(model_dim /...  75.6 us
    pallas_call x8, Pallas kernels, local_layer(): grads = place_blocks(*own[h], *others[h], *grads)  52.5 us
    ppermute x12, starting transfers between devices, swap_cores(): return lax.ppermute(value, 'sp', perm=core_perm)  17.6 us
    dot_general x3, matrix products, back_proj(): return jnp.einsum('ne,de->nd', rows, weight, preferred_element_type=F32)  17 us
    ppermute x12, starting transfers between devices, hop(): return lax.ppermute(value, 'sp', perm=ring_perm(axis, hops))  14.7 us
    pallas_call x1, Pallas kernels, local_layer(): pl.pallas_call(functools.partial(attend_kernel, att_scale), grid=(n_heads...  13.9 us
  transfers between devices with their start and end apart: 24, of which 7 were waited for; matrix products, arithmetic and copies ran while one was open for 6% of the time, Pallas kernels for 11%

profile of v5, /device:TPU:97, one launch (start us, length us, event | category | flops | bytes accessed | tf_op | source)
XLA Modules:
  0.0 429.3 jit_solution(17768159568849344050)
XLA Ops:
  2.0 75.6 %project.1 = (bf16[256,2048]{1,0:T(8,128)(2,1)S(1)}, bf16[256,2048]{1,0:T(8,128)(2,1)S(1)}, bf16[256,2048]{1,0:T(8,128)(2,1)S(1)}, bf16[256,2048]{1,0:T(8,128)(2...) custom-call(bf16[256,2048]{1,0:T(8,128)(2,1)S(1)} %copy-done.1, bf16[256,2048]{1,0:T(8,128)(2,1)} %dy_ref.3, ...), custom_call_target="tpu_custom_call" | custom-call | flops 8589934592 | bytes 33554432 | tf_op jit(solution)/shard_map/project/pallas_call | solution.py:526
  79.2 13.9 %attend.1 = (bf16[256,2048]{1,0:T(8,128)(2,1)S(1)}, bf16[5,256,2048]{2,1,0:T(8,128)(2,1)S(1)}) custom-call(bf16[256,2048]{1,0:T(8,128)(2,1)S(1)} %get-tuple-element.54.q_ref, bf16[256,2048]{1,0:T(8,128)(2,1)S(1)} %get-tuple-element.55.k_ref, bf16[256,2048]{1,0:T(8,128)(2,1)S(1)} %get-tuple-element.56.v_ref, bf16[256,2048]{1,0:T(8,128)(2,1)S(1)} %get-tuple-element.57.do_ref, ...), custom_call_target="tpu_custom_call" | custom-call | flops 1610612736 | bytes 16777216 | tf_op jit(solution)/shard_map/attend/pallas_call | solution.py:545
  93.1 2.3 copy-done.3
  95.5 137.5 %exchange.1 = (f32[256,2048]{1,0:T(8,128)}, f32[256,2048]{1,0:T(8,128)}, f32[256,2048]{1,0:T(8,128)}, f32[256,2048]{1,0:T(8,128)}, f32[256,2048]{1,0:T(8,128)}, ...) custom-call(bf16[2,4,256,1024]{3,2,1,0:T(8,128)(2,1)} %get-tuple-element.61.early_ref, ...), custom_call_target="tpu_custom_call" | custom-call | flops 8589934592 | bytes 16777216 | tf_op jit(solution)/shard_map/exchange/pallas_call | solution.py:560
  233.0 2.5 collective-permute-start.8
  236.5 22.3 %collective-permute-done.8.refs_0_ = f32[256,2048]{1,0:T(8,128)S(1)} collective-permute-done((f32[256,2048]{1,0:T(8,128)}, f32[256,2048]{1,0:T(8,128)S(1)}, u32[]{:S(2)}, u32[]{:S(2)}) %collective-permute-start.8) | collective-permute-done | bytes 2097184 | tf_op jit(solution)/shard_map/ppermute | solution.py:507
  262.3 19.0 %collective-permute-done.refs_0_ = f32[256,2048]{1,0:T(8,128)S(1)} collective-permute-done((f32[256,2048]{1,0:T(8,128)}, f32[256,2048]{1,0:T(8,128)S(1)}, u32[]{:S(2)}, u32[]{:S(2)}) %collective-permute-start) | collective-permute-done | bytes 2097184 | tf_op jit(solution)/shard_map/ppermute | solution.py:507
  285.2 2.4 collective-permute-start.1
  289.1 19.3 %collective-permute-done.9.refs_0_ = f32[256,2048]{1,0:T(8,128)} collective-permute-done((f32[256,2048]{1,0:T(8,128)S(1)}, f32[256,2048]{1,0:T(8,128)}, u32[]{:S(2)}, u32[]{:S(2)}) %collective-permute-start.9) | collective-permute-done | bytes 2097184 | tf_op jit(solution)/shard_map/ppermute | solution.py:507
  313.5 17.4 %collective-permute-done.1.refs_0_ = f32[256,2048]{1,0:T(8,128)} collective-permute-done((f32[256,2048]{1,0:T(8,128)S(1)}, f32[256,2048]{1,0:T(8,128)}, u32[]{:S(2)}, u32[]{:S(2)}) %collective-permute-start.1) | collective-permute-done | bytes 2097184 | tf_op jit(solution)/shard_map/ppermute | solution.py:507
  334.8 6.2 %fusion.3 = f32[256,2048]{1,0:T(8,128)S(1)} fusion(bf16[2048,2048]{1,0:T(8,128)(2,1)} %wq_ref.1, bf16[5,256,2048]{2,1,0:T(8,128)(2,1)} %copy-done.3), kind=kOutput, calls=%fused_computation.6 | convolution fusion | flops 2147483648 | bytes 11534336 | tf_op jit(solution)/shard_map/ne,de->nd/dot_general | solution.py:513
  344.5 6.1 %convolution_add_fusion.1 = f32[256,2048]{1,0:T(8,128)S(1)} fusion(f32[256,2048]{1,0:T(8,128)S(1)} %fusion.3, bf16[2048,2048]{1,0:T(8,128)(2,1)} %wk_ref.1, bf16[5,256,2048]{2,1,0:T(8,128)(2,1)} %copy-done.3), kind=kOutput, calls=%fused_computation.1 | convolution fusion | flops 2148007936 | bytes 13631488 | tf_op jit(solution)/shard_map/ne,de->nd/dot_general | solution.py:513
  350.6 4.7 %fusion = bf16[256,2048]{1,0:T(8,128)(2,1)} fusion(f32[256,2048]{1,0:T(8,128)S(1)} %convolution_add_fusion.1, bf16[2048,2048]{1,0:T(8,128)(2,1)S(1)} %bitcast.15, bf16[5,256,2048]{2,1,0:T(8,128)(2,1)} %copy-done.3), kind=kOutput, calls=%fused_computation.2 | convolution fusion | flops 2148532224 | bytes 12582912 | tf_op jit(solution)/shard_map/ne,de->nd/dot_general | solution.py:513
  355.3 6.6 %shard_map.109 = (f32[2048,2048]{1,0:T(8,128)}, f32[2048,2048]{1,0:T(8,128)}, f32[2048,2048]{1,0:T(8,128)}, f32[2048,2048]{1,0:T(8,128)}) custom-call(f32[256,2048]{1,0:T(8,128)} %get-tuple-element.64.refs_0_, f32[256,2048]{1,0:T(8,128)} %get-tuple-element.65.refs_1_, f32[256,2048]{1,0:T(8,128)} %get-tuple-element.68.refs_2_, ...), custom_call_target="tpu_custom_call" | custom-call | flops 3000000000 | bytes 67108864 | tf_op jit(solution)/shard_map/pallas_call | solution.py:609
  362.6 6.6 %shard_map.110 = (f32[2048,2048]{1,0:T(8,128)}, f32[2048,2048]{1,0:T(8,128)}, f32[2048,2048]{1,0:T(8,128)}, f32[2048,2048]{1,0:T(8,128)}) custom-call(f32[256,2048]{1,0:T(8,128)} %get-tuple-element.62.refs_0_, f32[256,2048]{1,0:T(8,128)} %get-tuple-element.63.refs_1_, ...), custom_call_target="tpu_custom_call", output_to_operand_aliasing={{0}: (4, {}), {1}: (5, {}), {2}: (6, {}), {3}: (7, {})} | custom-call | flops 3000000000 | bytes 67108864 | tf_op jit(solution)/shard_map/pallas_call | solution.py:609
  369.2 6.7 %collective-permute-done.2.refs_0_ = f32[256,2048]{1,0:T(8,128)S(1)} collective-permute-done((f32[256,2048]{1,0:T(8,128)}, f32[256,2048]{1,0:T(8,128)S(1)}, u32[]{:S(2)}, u32[]{:S(2)}) %collective-permute-start.2) | collective-permute-done | bytes 2097184 | tf_op jit(solution)/shard_map/ppermute | solution.py:507
  378.9 4.1 collective-permute-start.7
  383.0 6.7 %convolution_convert_fusion = bf16[256,2048]{1,0:T(8,128)(2,1)} fusion(bf16[256,2048]{1,0:T(8,128)(2,1)S(1)} %get-tuple-element.59, bf16[2048,2048]{1,0:T(8,128)(2,1)} %wo_ref.1), kind=kOutput, calls=%fused_computation.3 | convolution fusion | flops 2148007936 | bytes 10485760 | tf_op jit(solution)/shard_map/dot_general | solution.py:510
  389.7 6.6 %shard_map.111 = (f32[2048,2048]{1,0:T(8,128)}, f32[2048,2048]{1,0:T(8,128)}, f32[2048,2048]{1,0:T(8,128)}, f32[2048,2048]{1,0:T(8,128)}) custom-call(f32[256,2048]{1,0:T(8,128)} %copy-done.6, f32[256,2048]{1,0:T(8,128)} %copy-done.7, f32[256,2048]{1,0:T(8,128)} %copy-done.8, ...), custom_call_target="tpu_custom_call", output_to_operand_aliasing={{0}: (4, {}), {1}: (5, {}), {2}: (6, {}), {3}: (7, {})} | custom-call | flops 3000000000 | bytes 67108864 | tf_op jit(solution)/shard_map/pallas_call | solution.py:609
  396.3 6.6 %shard_map.112 = (f32[2048,2048]{1,0:T(8,128)}, f32[2048,2048]{1,0:T(8,128)}, f32[2048,2048]{1,0:T(8,128)}, f32[2048,2048]{1,0:T(8,128)}) custom-call(f32[256,2048]{1,0:T(8,128)} %copy-done.4, f32[256,2048]{1,0:T(8,128)} %copy-done.5, f32[256,2048]{1,0:T(8,128)} %copy-done.9, ...), custom_call_target="tpu_custom_call", output_to_operand_aliasing={{0}: (4, {}), {1}: (5, {}), {2}: (6, {}), {3}: (7, {})} | custom-call | flops 3000000000 | bytes 67108864 | tf_op jit(solution)/shard_map/pallas_call | solution.py:609
  402.8 6.6 %shard_map.113 = (f32[2048,2048]{1,0:T(8,128)}, f32[2048,2048]{1,0:T(8,128)}, f32[2048,2048]{1,0:T(8,128)}, f32[2048,2048]{1,0:T(8,128)}) custom-call(f32[256,2048]{1,0:T(8,128)} %collective-permute-done.9.refs_0_, f32[256,2048]{1,0:T(8,128)} %collective-permute-done.12.refs_1_, ...), custom_call_target="tpu_custom_call", output_to_operand_aliasing={{0}: (4, {}), {1}: (5, {}), {2}: (6, {}), {3}: (7, {})} | custom-call | flops 3000000000 | bytes 67108864 | tf_op jit(solution)/shard_map/pallas_call | solution.py:609
  409.4 6.6 %shard_map.114 = (f32[2048,2048]{1,0:T(8,128)}, f32[2048,2048]{1,0:T(8,128)}, f32[2048,2048]{1,0:T(8,128)}, f32[2048,2048]{1,0:T(8,128)}) custom-call(f32[256,2048]{1,0:T(8,128)} %collective-permute-done.1.refs_0_, f32[256,2048]{1,0:T(8,128)} %collective-permute-done.4.refs_1_, ...), custom_call_target="tpu_custom_call", output_to_operand_aliasing={{0}: (4, {}), {1}: (5, {}), {2}: (6, {}), {3}: (7, {})} | custom-call | flops 3000000000 | bytes 67108864 | tf_op jit(solution)/shard_map/pallas_call | solution.py:609
  416.0 6.6 %shard_map.115 = (f32[2048,2048]{1,0:T(8,128)}, f32[2048,2048]{1,0:T(8,128)}, f32[2048,2048]{1,0:T(8,128)}, f32[2048,2048]{1,0:T(8,128)}) custom-call(f32[256,2048]{1,0:T(8,128)} %collective-permute-done.10.refs_0_, f32[256,2048]{1,0:T(8,128)} %collective-permute-done.13.refs_1_, ...), custom_call_target="tpu_custom_call", output_to_operand_aliasing={{0}: (4, {}), {1}: (5, {}), {2}: (6, {}), {3}: (7, {})} | custom-call | flops 3000000000 | bytes 67108864 | tf_op jit(solution)/shard_map/pallas_call | solution.py:609
  422.6 6.6 %shard_map.116 = (f32[2048,2048]{1,0:T(8,128)}, f32[2048,2048]{1,0:T(8,128)}, f32[2048,2048]{1,0:T(8,128)}, f32[2048,2048]{1,0:T(8,128)}) custom-call(f32[256,2048]{1,0:T(8,128)} %copy-done.11, f32[256,2048]{1,0:T(8,128)} %collective-permute-done.5.refs_1_, ...), custom_call_target="tpu_custom_call", output_to_operand_aliasing={{0}: (4, {}), {1}: (5, {}), {2}: (6, {}), {3}: (7, {})} | custom-call | flops 3000000000 | bytes 67108864 | tf_op jit(solution)/shard_map/pallas_call | solution.py:609
  (74 shorter events, 28.9 us)
Async XLA Ops:
  233.0 25.8 %collective-permute-start.8 = (f32[256,2048]{1,0:T(8,128)}, f32[256,2048]{1,0:T(8,128)S(1)}, u32[]{:S(2)}, u32[]{:S(2)}) collective-permute-start(f32[256,2048]{1,0:T(8,128)} %get-tuple-element.64.refs_0_), channel_id=1, source_target_pairs={{0,2},{1,7},{2,4},{3,1},{4,6},{5,3},{6,0},{7,5},{8,10},{9,15},{10,... | collective-permute-start | bytes 6291464 | tf_op jit(solution)/shard_map/ppermute | solution.py:507
  235.5 25.4 %collective-permute-start.11 = (f32[256,2048]{1,0:T(8,128)}, f32[256,2048]{1,0:T(8,128)S(1)}, u32[]{:S(2)}, u32[]{:S(2)}) collective-permute-start(f32[256,2048]{1,0:T(8,128)} %get-tuple-element.65.refs_1_), channel_id=1, source_target_pairs={{0,8},{1,25},{2,10},{3,27},{4,12},{5,29},{6,14},{7,31},{8,16},{9,1... | collective-permute-start | bytes 6291464 | tf_op jit(solution)/shard_map/ppermute | solution.py:507
  235.5 45.8 %collective-permute-start = (f32[256,2048]{1,0:T(8,128)}, f32[256,2048]{1,0:T(8,128)S(1)}, u32[]{:S(2)}, u32[]{:S(2)}) collective-permute-start(f32[256,2048]{1,0:T(8,128)} %get-tuple-element.62.refs_0_), channel_id=1, source_target_pairs={{0,2},{1,7},{2,4},{3,1},{4,6},{5,3},{6,0},{7,5},{8,10},{9,15},{10,... | collective-permute-start | bytes 6291464 | tf_op jit(solution)/shard_map/ppermute | solution.py:507
  236.0 48.6 %collective-permute-start.3 = (f32[256,2048]{1,0:T(8,128)}, f32[256,2048]{1,0:T(8,128)S(1)}, u32[]{:S(2)}, u32[]{:S(2)}) collective-permute-start(f32[256,2048]{1,0:T(8,128)} %get-tuple-element.63.refs_1_), channel_id=1, source_target_pairs={{0,8},{1,25},{2,10},{3,27},{4,12},{5,29},{6,14},{7,31},{8,16},{9,1... | collective-permute-start | bytes 6291464 | tf_op jit(solution)/shard_map/ppermute | solution.py:507
  258.8 26.4 %collective-permute-start.22 = (f32[256,2048]{1,0:T(8,128)S(1)}, f32[256,2048]{1,0:T(8,128)S(1)}, u32[]{:S(2)}, u32[]{:S(2)}) collective-permute-start(f32[256,2048]{1,0:T(8,128)S(1)} %collective-permute-done.8.refs_0_), channel_id=1, source_target_pairs={{0,1},{1,0},{2,3},{3,2},{4,5},{5,4},{6,7},{7,6},{8,9},{9,8},{10,11... | collective-permute-start | bytes 6291464 | tf_op jit(solution)/shard_map/ppermute | solution.py:504
  260.9 24.3 %collective-permute-start.23 = (f32[256,2048]{1,0:T(8,128)S(1)}, f32[256,2048]{1,0:T(8,128)S(1)}, u32[]{:S(2)}, u32[]{:S(2)}) collective-permute-start(f32[256,2048]{1,0:T(8,128)S(1)} %collective-permute-done.11.refs_1_), channel_id=1, source_target_pairs={{0,1},{1,0},{2,3},{3,2},{4,5},{5,4},{6,7},{7,6},{8,9},{9,8},{10,11... | collective-permute-start | bytes 6291464 | tf_op jit(solution)/shard_map/ppermute | solution.py:504
  281.3 6.4 %collective-permute-start.20 = (f32[256,2048]{1,0:T(8,128)S(1)}, f32[256,2048]{1,0:T(8,128)S(1)}, u32[]{:S(2)}, u32[]{:S(2)}) collective-permute-start(f32[256,2048]{1,0:T(8,128)S(1)} %collective-permute-done.refs_0_), channel_id=1, source_target_pairs={{0,1},{1,0},{2,3},{3,2},{4,5},{5,4},{6,7},{7,6},{8,9},{9,8},{10,11... | collective-permute-start | bytes 6291464 | tf_op jit(solution)/shard_map/ppermute | solution.py:504
  283.2 25.3 %collective-permute-start.9 = (f32[256,2048]{1,0:T(8,128)S(1)}, f32[256,2048]{1,0:T(8,128)}, u32[]{:S(2)}, u32[]{:S(2)}) collective-permute-start(f32[256,2048]{1,0:T(8,128)S(1)} %collective-permute-done.8.refs_0_), channel_id=1, source_target_pairs={{0,2},{1,7},{2,4},{3,1},{4,6},{5,3},{6,0},{7,5},{8,10},{9,15},{10,... | collective-permute-start | bytes 6291464 | tf_op jit(solution)/shard_map/ppermute | solution.py:507
  284.6 25.9 %collective-permute-start.12 = (f32[256,2048]{1,0:T(8,128)S(1)}, f32[256,2048]{1,0:T(8,128)}, u32[]{:S(2)}, u32[]{:S(2)}) collective-permute-start(f32[256,2048]{1,0:T(8,128)S(1)} %collective-permute-done.11.refs_1_), channel_id=1, source_target_pairs={{0,8},{1,25},{2,10},{3,27},{4,12},{5,29},{6,14},{7,31},{8,16},{9,1... | collective-permute-start | bytes 6291464 | tf_op jit(solution)/shard_map/ppermute | solution.py:507
  285.2 26.9 %collective-permute-start.21 = (f32[256,2048]{1,0:T(8,128)S(1)}, f32[256,2048]{1,0:T(8,128)S(1)}, u32[]{:S(2)}, u32[]{:S(2)}) collective-permute-start(f32[256,2048]{1,0:T(8,128)S(1)} %collective-permute-done.3.refs_1_), channel_id=1, source_target_pairs={{0,1},{1,0},{2,3},{3,2},{4,5},{5,4},{6,7},{7,6},{8,9},{9,8},{10,11... | collective-permute-start | bytes 6291464 | tf_op jit(solution)/shard_map/ppermute | solution.py:504
  285.2 45.7 %collective-permute-start.1 = (f32[256,2048]{1,0:T(8,128)S(1)}, f32[256,2048]{1,0:T(8,128)}, u32[]{:S(2)}, u32[]{:S(2)}) collective-permute-start(f32[256,2048]{1,0:T(8,128)S(1)} %collective-permute-done.refs_0_), channel_id=1, source_target_pairs={{0,2},{1,7},{2,4},{3,1},{4,6},{5,3},{6,0},{7,5},{8,10},{9,15},{10,... | collective-permute-start | bytes 6291464 | tf_op jit(solution)/shard_map/ppermute | solution.py:507
  287.6 45.2 %collective-permute-start.4 = (f32[256,2048]{1,0:T(8,128)S(1)}, f32[256,2048]{1,0:T(8,128)}, u32[]{:S(2)}, u32[]{:S(2)}) collective-permute-start(f32[256,2048]{1,0:T(8,128)S(1)} %collective-permute-done.3.refs_1_), channel_id=1, source_target_pairs={{0,8},{1,25},{2,10},{3,27},{4,12},{5,29},{6,14},{7,31},{8,16},{9,1... | collective-permute-start | bytes 6291464 | tf_op jit(solution)/shard_map/ppermute | solution.py:507
  308.4 32.6 %collective-permute-start.18 = (f32[256,2048]{1,0:T(8,128)}, f32[256,2048]{1,0:T(8,128)S(1)}, u32[]{:S(2)}, u32[]{:S(2)}) collective-permute-start(f32[256,2048]{1,0:T(8,128)} %collective-permute-done.9.refs_0_), channel_id=1, source_target_pairs={{0,1},{1,0},{2,3},{3,2},{4,5},{5,4},{6,7},{7,6},{8,9},{9,8},{10,11... | collective-permute-start | bytes 6291464 | tf_op jit(solution)/shard_map/ppermute | solution.py:504
  310.5 33.2 %collective-permute-start.19 = (f32[256,2048]{1,0:T(8,128)}, f32[256,2048]{1,0:T(8,128)S(1)}, u32[]{:S(2)}, u32[]{:S(2)}) collective-permute-start(f32[256,2048]{1,0:T(8,128)} %collective-permute-done.12.refs_1_), channel_id=1, source_target_pairs={{0,1},{1,0},{2,3},{3,2},{4,5},{5,4},{6,7},{7,6},{8,9},{9,8},{10,11... | collective-permute-start | bytes 6291464 | tf_op jit(solution)/shard_map/ppermute | solution.py:504
  312.1 49.7 %collective-permute-start.10 = (f32[256,2048]{1,0:T(8,128)}, f32[256,2048]{1,0:T(8,128)}, u32[]{:S(2)}, u32[]{:S(2)}) collective-permute-start(f32[256,2048]{1,0:T(8,128)} %collective-permute-done.9.refs_0_), channel_id=1, source_target_pairs={{0,2},{1,7},{2,4},{3,1},{4,6},{5,3},{6,0},{7,5},{8,10},{9,15},{10,... | collective-permute-start | bytes 6291464 | tf_op jit(solution)/shard_map/ppermute | solution.py:507
  330.9 31.6 %collective-permute-start.13 = (f32[256,2048]{1,0:T(8,128)}, f32[256,2048]{1,0:T(8,128)}, u32[]{:S(2)}, u32[]{:S(2)}) collective-permute-start(f32[256,2048]{1,0:T(8,128)} %collective-permute-done.12.refs_1_), channel_id=1, source_target_pairs={{0,8},{1,25},{2,10},{3,27},{4,12},{5,29},{6,14},{7,31},{8,16},{9,1... | collective-permute-start | bytes 6291464 | tf_op jit(solution)/shard_map/ppermute | solution.py:507
  332.9 22.4 %collective-permute-start.16 = (f32[256,2048]{1,0:T(8,128)}, f32[256,2048]{1,0:T(8,128)}, u32[]{:S(2)}, u32[]{:S(2)}) collective-permute-start(f32[256,2048]{1,0:T(8,128)} %collective-permute-done.1.refs_0_), channel_id=1, source_target_pairs={{0,1},{1,0},{2,3},{3,2},{4,5},{5,4},{6,7},{7,6},{8,9},{9,8},{10,11... | collective-permute-start | bytes 6291464 | tf_op jit(solution)/shard_map/ppermute | solution.py:504
  342.4 33.5 %collective-permute-start.2 = (f32[256,2048]{1,0:T(8,128)}, f32[256,2048]{1,0:T(8,128)S(1)}, u32[]{:S(2)}, u32[]{:S(2)}) collective-permute-start(f32[256,2048]{1,0:T(8,128)} %collective-permute-done.1.refs_0_), channel_id=1, source_target_pairs={{0,2},{1,7},{2,4},{3,1},{4,6},{5,3},{6,0},{7,5},{8,10},{9,15},{10,... | collective-permute-start | bytes 6291464 | tf_op jit(solution)/shard_map/ppermute | solution.py:507
  343.7 35.2 %collective-permute-start.5 = (f32[256,2048]{1,0:T(8,128)}, f32[256,2048]{1,0:T(8,128)}, u32[]{:S(2)}, u32[]{:S(2)}) collective-permute-start(f32[256,2048]{1,0:T(8,128)} %collective-permute-done.4.refs_1_), channel_id=1, source_target_pairs={{0,8},{1,25},{2,10},{3,27},{4,12},{5,29},{6,14},{7,31},{8,16},{9,1... | collective-permute-start | bytes 6291464 | tf_op jit(solution)/shard_map/ppermute | solution.py:507
  355.3 54.1 %collective-permute-start.17 = (f32[256,2048]{1,0:T(8,128)}, f32[256,2048]{1,0:T(8,128)}, u32[]{:S(2)}, u32[]{:S(2)}) collective-permute-start(f32[256,2048]{1,0:T(8,128)} %collective-permute-done.4.refs_1_), channel_id=1, source_target_pairs={{0,1},{1,0},{2,3},{3,2},{4,5},{5,4},{6,7},{7,6},{8,9},{9,8},{10,11... | collective-permute-start | bytes 6291464 | tf_op jit(solution)/shard_map/ppermute | solution.py:504
  361.9 54.1 %collective-permute-start.14 = (f32[256,2048]{1,0:T(8,128)}, f32[256,2048]{1,0:T(8,128)}, u32[]{:S(2)}, u32[]{:S(2)}) collective-permute-start(f32[256,2048]{1,0:T(8,128)} %collective-permute-done.10.refs_0_), channel_id=1, source_target_pairs={{0,1},{1,0},{2,3},{3,2},{4,5},{5,4},{6,7},{7,6},{8,9},{9,8},{10,11... | collective-permute-start | bytes 6291464 | tf_op jit(solution)/shard_map/ppermute | solution.py:504
  362.5 53.5 %collective-permute-start.15 = (f32[256,2048]{1,0:T(8,128)}, f32[256,2048]{1,0:T(8,128)}, u32[]{:S(2)}, u32[]{:S(2)}) collective-permute-start(f32[256,2048]{1,0:T(8,128)} %collective-permute-done.13.refs_1_), channel_id=1, source_target_pairs={{0,1},{1,0},{2,3},{3,2},{4,5},{5,4},{6,7},{7,6},{8,9},{9,8},{10,11... | collective-permute-start | bytes 6291464 | tf_op jit(solution)/shard_map/ppermute | solution.py:504
  375.9 46.7 %collective-permute-start.6 = (f32[256,2048]{1,0:T(8,128)S(1)}, f32[256,2048]{1,0:T(8,128)}, u32[]{:S(2)}, u32[]{:S(2)}) collective-permute-start(f32[256,2048]{1,0:T(8,128)S(1)} %collective-permute-done.2.refs_0_), channel_id=1, source_target_pairs={{0,1},{1,0},{2,3},{3,2},{4,5},{5,4},{6,7},{7,6},{8,9},{9,8},{10,11... | collective-permute-start | bytes 6291464 | tf_op jit(solution)/shard_map/ppermute | solution.py:504
  378.9 43.7 %collective-permute-start.7 = (f32[256,2048]{1,0:T(8,128)}, f32[256,2048]{1,0:T(8,128)}, u32[]{:S(2)}, u32[]{:S(2)}) collective-permute-start(f32[256,2048]{1,0:T(8,128)} %collective-permute-done.5.refs_1_), channel_id=1, source_target_pairs={{0,1},{1,0},{2,3},{3,2},{4,5},{5,4},{6,7},{7,6},{8,9},{9,8},{10,11... | collective-permute-start | bytes 6291464 | tf_op jit(solution)/shard_map/ppermute | solution.py:504
  (17 other events, 545.1 us)

commit v6 on v5

--- a/solution.py
+++ b/solution.py
@@ -13,7 +13,7 @@
 N_CORES = 2
 N_GRADS = 4
 RELAY_STEP = 7
-SLOTS = 2
+SLOTS = 3
 
 
 F32 = jnp.float32
@@ -259,24 +259,29 @@
 def attend_kernel(scale, q_ref, k_ref, v_ref, do_ref, dy_ref, state_ref, out_ref, late_ref):
     n_blocks = q_ref.shape[0] // BLOCK_LEN
     rows = [pl.ds(b * BLOCK_LEN, BLOCK_LEN) for b in range(n_blocks)]
-    fwd = [state_ref[0, 0]]
-    for b in range(n_blocks - 1):
-        fwd.append(fwd[-1] + dot(k_ref[rows[b]], v_ref[rows[b]], (0, 0)))
-    rev = [state_ref[1, 0]]
-    for b in range(n_blocks - 1, 0, -1):
-        rev.insert(0, rev[0] + dot(q_ref[rows[b]], do_ref[rows[b]], (0, 0)))
     shape = (BLOCK_LEN, BLOCK_LEN)
     causal = lax.broadcasted_iota(jnp.int32, shape, 0) >= lax.broadcasted_iota(jnp.int32, shape, 1)
-    for b in range(n_blocks):
-        q, k, v, do = q_ref[rows[b]], k_ref[rows[b]], v_ref[rows[b]], do_ref[rows[b]]
-        s = fwd[b].astype(BF16)
-        r = rev[b].astype(BF16)
-        att = jnp.where(causal, dot(q, k, (1, 1)), 0.0).astype(BF16)
-        d_att = jnp.where(causal, dot(do, v, (1, 1)), 0.0).astype(BF16)
-        out_ref[rows[b], :] = ((dot(att, v, (1, 0)) + dot(q, s, (1, 0))) * scale).astype(BF16)
-        late_ref[0, rows[b]] = ((dot(d_att, k, (1, 0)) + dot(do, s, (1, 1))) * scale).astype(BF16)
-        late_ref[1, rows[b]] = ((dot(d_att, q, (0, 0)) + dot(v, r, (1, 1))) * scale).astype(BF16)
-        late_ref[2, rows[b]] = ((dot(att, do, (0, 0)) + dot(k, r, (1, 0))) * scale).astype(BF16)
+    work = []
+    for head in range(state_ref.shape[1]):
+        cols = pl.ds(head * HEAD_DIM, HEAD_DIM)
+        fwd = [state_ref[0, head]]
+        for b in range(n_blocks - 1):
+            fwd.append(fwd[-1] + dot(k_ref[rows[b], cols], v_ref[rows[b], cols], (0, 0)))
+        rev = [state_ref[1, head]]
+        for b in range(n_blocks - 1, 0, -1):
+            rev.insert(0, rev[0] + dot(q_ref[rows[b], cols], do_ref[rows[b], cols], (0, 0)))
+        work += [(rows[b], cols, fwd[b].astype(BF16), rev[b].astype(BF16)) for b in range(n_blocks)]
+    scores = []
+    for at, cols, s, r in work:
+        att = jnp.where(causal, dot(q_ref[at, cols], k_ref[at, cols], (1, 1)), 0.0).astype(BF16)
+        d_att = jnp.where(causal, dot(do_ref[at, cols], v_ref[at, cols], (1, 1)), 0.0).astype(BF16)
+        scores.append((att, d_att))
+    for (at, cols, s, r), (att, d_att) in zip(work, scores):
+        q, k, v, do = q_ref[at, cols], k_ref[at, cols], v_ref[at, cols], do_ref[at, cols]
+        out_ref[at, cols] = ((dot(att, v, (1, 0)) + dot(q, s, (1, 0))) * scale).astype(BF16)
+        late_ref[0, at, cols] = ((dot(d_att, k, (1, 0)) + dot(do, s, (1, 1))) * scale).astype(BF16)
+        late_ref[1, at, cols] = ((dot(d_att, q, (0, 0)) + dot(v, r, (1, 1))) * scale).astype(BF16)
+        late_ref[2, at, cols] = ((dot(att, do, (0, 0)) + dot(k, r, (1, 0))) * scale).astype(BF16)
     first_half = pl.program_id(0) < pl.num_programs(0) // 2
 
     @pl.when(first_half)
@@ -437,9 +442,10 @@
         copy.wait()
 
 
-def place_kernel(side, step, lane, halves, fresh, *refs):
-    blocks = refs[:4]
-    grads = refs[4 if fresh else 4 + N_GRADS :][:N_GRADS]
+def place_kernel(side, step, lane, halves, kinds, fresh, *refs):
+    n_blocks = len(kinds)
+    blocks = refs[:n_blocks]
+    grads = refs[n_blocks if fresh else n_blocks + N_GRADS :][:N_GRADS]
     buf, sem_in, sem_out = refs[-3:]
     index = lax.axis_index("sp")
     core = lax.rem(index, N_CORES)
@@ -449,8 +455,7 @@
     piece = small * halves
     half = grads[0].shape[0] // 2
     jobs = []
-    for k, src in enumerate(blocks):
-        own, part = k < 2, k % 2
+    for (own, part), src in zip(kinds, blocks):
         at = col if part == 0 else row
         c = core if own else 1 - core
         which = lax.rem(at - (1 - 2 * c) * step + 2 * side, side)
@@ -541,12 +546,11 @@
             name="project",
         )(tokens, grad_y, w_q, w_k, w_v, w_o, tokens, grad_y)
 
-        head_cols = pl.BlockSpec((n_rows, HEAD_DIM), lambda h: (0, h))
         out_rows, late = pl.pallas_call(
             functools.partial(attend_kernel, att_scale),
-            grid=(n_heads,),
-            in_specs=[head_cols] * 5 + [pl.BlockSpec((2, 1, HEAD_DIM, HEAD_DIM), lambda h: (0, h, 0, 0))],
-            out_specs=[head_cols, pl.BlockSpec((5, n_rows, HEAD_DIM), lambda h: (0, 0, h))],
+            grid=(model_dim // tile,),
+            in_specs=[out_cols] * 5 + [pl.BlockSpec((2, tile // HEAD_DIM, HEAD_DIM, HEAD_DIM), lambda i: (0, i, 0, 0))],
+            out_specs=[out_cols, pl.BlockSpec((5, n_rows, tile), lambda i: (0, 0, i))],
             out_shape=[act, jax.ShapeDtypeStruct((5, n_rows, model_dim), BF16)],
             cost_estimate=pl.CostEstimate(flops=n_heads * 24 * 2 * 128**3, bytes_accessed=2**24, transcendentals=0),
             compiler_params=pltpu.CompilerParams(vmem_limit_bytes=16 * 2**20),
@@ -589,24 +593,32 @@
         others = [list(blocks[2 * (halves + h) : 2 * (halves + h) + 2]) for h in range(halves)]
 
         grads = []
-        n_copies = 4 * side
+
+        def put(kinds, sources, step, h):
+            n_copies = len(kinds) * side
+            return pl.pallas_call(
+                functools.partial(place_kernel, side, step, h, halves, kinds, not grads),
+                in_specs=[anywhere] * (len(kinds) + len(grads)),
+                out_specs=[anywhere] * N_GRADS,
+                out_shape=[jax.ShapeDtypeStruct((model_dim, model_dim), F32)] * N_GRADS,
+                scratch_shapes=[VMEM((n_copies, small, model_dim), F32), dma((n_copies,)), dma((n_copies,))],
+                input_output_aliases={len(kinds) + m: m for m in range(len(grads))},
+                cost_estimate=pl.CostEstimate(flops=3 * 10**9, bytes_accessed=8 * n_copies * small * model_dim, transcendentals=0),
+            )(*sources, *grads)
+
+        own_kinds, other_kinds = ((True, 0), (True, 1)), ((False, 0), (False, 1))
         for step in range(side):
             for h in range(halves):
                 if step:
                     for part, (first, second) in enumerate(axes):
                         own[h][part] = hop(own[h][part], first, 1)
-                    others[h] = [swap_cores(b) for b in own[h]]
-                fresh = not grads
-                place_blocks = pl.pallas_call(
-                    functools.partial(place_kernel, side, step, h, halves, fresh),
-                    in_specs=[pl.BlockSpec(memory_space=pl.ANY)] * (4 + len(grads)),
-                    out_specs=[pl.BlockSpec(memory_space=pl.ANY)] * N_GRADS,
-                    out_shape=[jax.ShapeDtypeStruct((model_dim, model_dim), F32)] * N_GRADS,
-                    scratch_shapes=[VMEM((n_copies, small, model_dim), F32), dma((n_copies,)), dma((n_copies,))],
-                    input_output_aliases={} if fresh else {4 + m: m for m in range(N_GRADS)},
-                    cost_estimate=pl.CostEstimate(flops=3 * 10**9, bytes_accessed=32 * n_copies * small * model_dim, transcendentals=0),
-                )
-                grads = place_blocks(*own[h], *others[h], *grads)
+                    for part in range(2):
+                        others[h][part] = swap_cores(own[h][part])
+                if (step, h) == (side - 1, halves - 1):
+                    grads = put(own_kinds, own[h], step, h)
+                    grads = put(other_kinds, others[h], step, h)
+                else:
+                    grads = put(own_kinds + other_kinds, own[h] + others[h], step, h)
 
         out_y = project(out_rows, w_o)
         grad_x = back_proj(late[0], w_q)

time: 430 us -> 435 us (1.012)
  waiting for transfers between devices: 86 us -> 91.6 us
    pallas_call x1, Pallas kernels: 75.6 us -> 84.8 us  [local_layer(): pl.pallas_call(functools.partial(project_kernel, side), grid=(model_dim /...]
    pallas_call x1, Pallas kernels: 138 us -> 131 us  [local_layer(): pl.pallas_call(functools.partial(exchange_kernel, side, halves), in_specs...]
    ppermute x12, waiting for transfers between devices: 86 us -> 91.5 us  [hop(): return lax.ppermute(value, 'sp', perm=ring_perm(axis, hops))]
    pallas_call x9 -> x10, Pallas kernels: 66.4 us -> 61.3 us  [the longest x9 53.1 us: put(): pl.pallas_call(functools.partial(place_kernel, side, step, h, halves, kin...]
  transfers between devices with their start and end apart: 24 -> 24, of which waited for: 7 -> 7; matrix products, arithmetic and copies ran while one was open for 6% -> 5% of each run, Pallas kernels for 11% -> 11%
where the time goes in v6:
time: 435 us
  Pallas kernels  277 us (64%)
  waiting for transfers between devices  91.6 us (21%)
  starting transfers between devices  35.2 us (8%)
  matrix products  22.7 us (5%)
  local copies, waits for them, and re-layouts  7 us (2%)
    pallas_call x1, Pallas kernels, local_layer(): pl.pallas_call(functools.partial(exchange_kernel, side, halves), in_specs...  131 us
    ppermute x12, waiting for transfers between devices, hop(): return lax.ppermute(value, 'sp', perm=ring_perm(axis, hops))  91.5 us
    pallas_call x1, Pallas kernels, local_layer(): pl.pallas_call(functools.partial(project_kernel, side), grid=(model_dim /...  84.8 us
    pallas_call x9, Pallas kernels, put(): pl.pallas_call(functools.partial(place_kernel, side, step, h, halves, kin...  53.1 us
    ppermute x12, starting transfers between devices, swap_cores(): return lax.ppermute(value, 'sp', perm=core_perm)  19.5 us
    dot_general x3, matrix products, back_proj(): return jnp.einsum('ne,de->nd', rows, weight, preferred_element_type=F32)  19.3 us
    ppermute x12, starting transfers between devices, hop(): return lax.ppermute(value, 'sp', perm=ring_perm(axis, hops))  15.7 us
  transfers between devices with their start and end apart: 24, of which 7 were waited for; matrix products, arithmetic and copies ran while one was open for 5% of the time, Pallas kernels for 11%

profile of v6, /device:TPU:97, one launch (start us, length us, event | category | flops | bytes accessed | tf_op | source)
XLA Modules:
  0.0 435.1 jit_solution(15594895858823083246)
XLA Ops:
  2.0 84.8 %project.1 = (bf16[256,2048]{1,0:T(8,128)(2,1)S(1)}, bf16[256,2048]{1,0:T(8,128)(2,1)S(1)}, bf16[256,2048]{1,0:T(8,128)(2,1)S(1)}, bf16[256,2048]{1,0:T(8,128)(2...) custom-call(bf16[256,2048]{1,0:T(8,128)(2,1)S(1)} %copy-done.1, bf16[256,2048]{1,0:T(8,128)(2,1)} %dy_ref.3, ...), custom_call_target="tpu_custom_call" | custom-call | flops 8589934592 | bytes 33554432 | tf_op jit(solution)/shard_map/project/pallas_call | solution.py:531
  88.3 8.3 %attend.1 = (bf16[256,2048]{1,0:T(8,128)(2,1)S(1)}, bf16[5,256,2048]{2,1,0:T(8,128)(2,1)S(1)}) custom-call(bf16[256,2048]{1,0:T(8,128)(2,1)S(1)} %get-tuple-element.58.q_ref, bf16[256,2048]{1,0:T(8,128)(2,1)S(1)} %get-tuple-element.59.k_ref, bf16[256,2048]{1,0:T(8,128)(2,1)S(1)} %get-tuple-element.60.v_ref, bf16[256,2048]{1,0:T(8,128)(2,1)S(1)} %get-tuple-element.61.do_ref, ...), custom_call_target="tpu_custom_call" | custom-call | flops 1610612736 | bytes 16777216 | tf_op jit(solution)/shard_map/attend/pallas_call | solution.py:549
  99.0 131.3 %exchange.1 = (f32[256,2048]{1,0:T(8,128)}, f32[256,2048]{1,0:T(8,128)}, f32[256,2048]{1,0:T(8,128)}, f32[256,2048]{1,0:T(8,128)}, f32[256,2048]{1,0:T(8,128)}, ...) custom-call(bf16[2,4,256,1024]{3,2,1,0:T(8,128)(2,1)} %get-tuple-element.65.early_ref, ...), custom_call_target="tpu_custom_call" | custom-call | flops 8589934592 | bytes 16777216 | tf_op jit(solution)/shard_map/exchange/pallas_call | solution.py:564
  230.3 3.1 collective-permute-start.8
  234.3 22.3 %collective-permute-done.8.refs_0_ = f32[256,2048]{1,0:T(8,128)S(1)} collective-permute-done((f32[256,2048]{1,0:T(8,128)}, f32[256,2048]{1,0:T(8,128)S(1)}, u32[]{:S(2)}, u32[]{:S(2)}) %collective-permute-start.8) | collective-permute-done | bytes 2097184 | tf_op jit(solution)/shard_map/ppermute | solution.py:512
  260.2 19.0 %collective-permute-done.refs_0_ = f32[256,2048]{1,0:T(8,128)S(1)} collective-permute-done((f32[256,2048]{1,0:T(8,128)}, f32[256,2048]{1,0:T(8,128)S(1)}, u32[]{:S(2)}, u32[]{:S(2)}) %collective-permute-start) | collective-permute-done | bytes 2097184 | tf_op jit(solution)/shard_map/ppermute | solution.py:512
  286.8 19.0 %collective-permute-done.9.refs_0_ = f32[256,2048]{1,0:T(8,128)S(1)} collective-permute-done((f32[256,2048]{1,0:T(8,128)S(1)}, f32[256,2048]{1,0:T(8,128)S(1)}, u32[]{:S(2)}, u32[]{:S(2)}) %collective-permute-start.9) | collective-permute-done | bytes 2097184 | tf_op jit(solution)/shard_map/ppermute | solution.py:512
  310.9 17.3 %collective-permute-done.1.refs_0_ = f32[256,2048]{1,0:T(8,128)} collective-permute-done((f32[256,2048]{1,0:T(8,128)S(1)}, f32[256,2048]{1,0:T(8,128)}, u32[]{:S(2)}, u32[]{:S(2)}) %collective-permute-start.1) | collective-permute-done | bytes 2097184 | tf_op jit(solution)/shard_map/ppermute | solution.py:512
  332.6 6.2 %fusion.3 = f32[256,2048]{1,0:T(8,128)S(1)} fusion(bf16[2048,2048]{1,0:T(8,128)(2,1)} %wq_ref.1, bf16[5,256,2048]{2,1,0:T(8,128)(2,1)} %copy-done.3), kind=kOutput, calls=%fused_computation.6 | convolution fusion | flops 2147483648 | bytes 11534336 | tf_op jit(solution)/shard_map/ne,de->nd/dot_general | solution.py:518
  341.3 7.6 %convolution_add_fusion.1 = f32[256,2048]{1,0:T(8,128)} fusion(f32[256,2048]{1,0:T(8,128)S(1)} %fusion.3, bf16[2048,2048]{1,0:T(8,128)(2,1)} %wk_ref.1, bf16[5,256,2048]{2,1,0:T(8,128)(2,1)} %copy-done.3), kind=kOutput, calls=%fused_computation.1 | convolution fusion | flops 2148007936 | bytes 13631488 | tf_op jit(solution)/shard_map/ne,de->nd/dot_general | solution.py:518
  348.9 5.5 %fusion = bf16[256,2048]{1,0:T(8,128)(2,1)} fusion(f32[256,2048]{1,0:T(8,128)} %convolution_add_fusion.1, bf16[2048,2048]{1,0:T(8,128)(2,1)S(1)} %bitcast.15, bf16[5,256,2048]{2,1,0:T(8,128)(2,1)} %copy-done.3), kind=kOutput, calls=%fused_computation.2 | convolution fusion | flops 2148532224 | bytes 12582912 | tf_op jit(solution)/shard_map/ne,de->nd/dot_general | solution.py:518
  355.0 2.9 collective-permute-start.15
  357.9 3.4 convolution_convert_fusion
  361.3 11.9 %collective-permute-done.2.refs_0_ = f32[256,2048]{1,0:T(8,128)} collective-permute-done((f32[256,2048]{1,0:T(8,128)}, f32[256,2048]{1,0:T(8,128)}, u32[]{:S(2)}, u32[]{:S(2)}) %collective-permute-start.2) | collective-permute-done | bytes 2097184 | tf_op jit(solution)/shard_map/ppermute | solution.py:512
  376.5 3.8 collective-permute-start.7
  380.4 6.6 %shard_map.109 = (f32[2048,2048]{1,0:T(8,128)}, f32[2048,2048]{1,0:T(8,128)}, f32[2048,2048]{1,0:T(8,128)}, f32[2048,2048]{1,0:T(8,128)}) custom-call(f32[256,2048]{1,0:T(8,128)} %get-tuple-element.68.refs_0_, f32[256,2048]{1,0:T(8,128)} %get-tuple-element.69.refs_1_, f32[256,2048]{1,0:T(8,128)} %get-tuple-element.72.refs_2_, ...), custom_call_target="tpu_custom_call" | custom-call | flops 3000000000 | bytes 16777216 | tf_op jit(solution)/shard_map/pallas_call | solution.py:599
  386.9 6.6 %shard_map.110 = (f32[2048,2048]{1,0:T(8,128)}, f32[2048,2048]{1,0:T(8,128)}, f32[2048,2048]{1,0:T(8,128)}, f32[2048,2048]{1,0:T(8,128)}) custom-call(f32[256,2048]{1,0:T(8,128)} %get-tuple-element.66.refs_0_, f32[256,2048]{1,0:T(8,128)} %get-tuple-element.67.refs_1_, ...), custom_call_target="tpu_custom_call", output_to_operand_aliasing={{0}: (4, {}), {1}: (5, {}), {2}: (6, {}), {3}: (7, {})} | custom-call | flops 3000000000 | bytes 16777216 | tf_op jit(solution)/shard_map/pallas_call | solution.py:599
  393.5 6.6 %shard_map.111 = (f32[2048,2048]{1,0:T(8,128)}, f32[2048,2048]{1,0:T(8,128)}, f32[2048,2048]{1,0:T(8,128)}, f32[2048,2048]{1,0:T(8,128)}) custom-call(f32[256,2048]{1,0:T(8,128)} %copy-done.6, f32[256,2048]{1,0:T(8,128)} %copy-done.7, f32[256,2048]{1,0:T(8,128)} %copy-done.9, ...), custom_call_target="tpu_custom_call", output_to_operand_aliasing={{0}: (4, {}), {1}: (5, {}), {2}: (6, {}), {3}: (7, {})} | custom-call | flops 3000000000 | bytes 16777216 | tf_op jit(solution)/shard_map/pallas_call | solution.py:599
  400.1 6.6 %shard_map.112 = (f32[2048,2048]{1,0:T(8,128)}, f32[2048,2048]{1,0:T(8,128)}, f32[2048,2048]{1,0:T(8,128)}, f32[2048,2048]{1,0:T(8,128)}) custom-call(f32[256,2048]{1,0:T(8,128)} %copy-done.4, f32[256,2048]{1,0:T(8,128)} %copy-done.5, f32[256,2048]{1,0:T(8,128)} %copy-done.10, ...), custom_call_target="tpu_custom_call", output_to_operand_aliasing={{0}: (4, {}), {1}: (5, {}), {2}: (6, {}), {3}: (7, {})} | custom-call | flops 3000000000 | bytes 16777216 | tf_op jit(solution)/shard_map/pallas_call | solution.py:599
  406.6 6.6 %shard_map.113 = (f32[2048,2048]{1,0:T(8,128)}, f32[2048,2048]{1,0:T(8,128)}, f32[2048,2048]{1,0:T(8,128)}, f32[2048,2048]{1,0:T(8,128)}) custom-call(f32[256,2048]{1,0:T(8,128)} %copy-done.8, f32[256,2048]{1,0:T(8,128)} %collective-permute-done.12.refs_1_, ...), custom_call_target="tpu_custom_call", output_to_operand_aliasing={{0}: (4, {}), {1}: (5, {}), {2}: (6, {}), {3}: (7, {})} | custom-call | flops 3000000000 | bytes 16777216 | tf_op jit(solution)/shard_map/pallas_call | solution.py:599
  413.2 6.6 %shard_map.114 = (f32[2048,2048]{1,0:T(8,128)}, f32[2048,2048]{1,0:T(8,128)}, f32[2048,2048]{1,0:T(8,128)}, f32[2048,2048]{1,0:T(8,128)}) custom-call(f32[256,2048]{1,0:T(8,128)} %collective-permute-done.1.refs_0_, f32[256,2048]{1,0:T(8,128)} %collective-permute-done.5.refs_1_, ...), custom_call_target="tpu_custom_call", output_to_operand_aliasing={{0}: (4, {}), {1}: (5, {}), {2}: (6, {}), {3}: (7, {})} | custom-call | flops 3000000000 | bytes 16777216 | tf_op jit(solution)/shard_map/pallas_call | solution.py:599
  419.8 6.6 %shard_map.115 = (f32[2048,2048]{1,0:T(8,128)}, f32[2048,2048]{1,0:T(8,128)}, f32[2048,2048]{1,0:T(8,128)}, f32[2048,2048]{1,0:T(8,128)}) custom-call(f32[256,2048]{1,0:T(8,128)} %collective-permute-done.10.refs_0_, f32[256,2048]{1,0:T(8,128)} %collective-permute-done.13.refs_1_, ...), custom_call_target="tpu_custom_call", output_to_operand_aliasing={{0}: (4, {}), {1}: (5, {}), {2}: (6, {}), {3}: (7, {})} | custom-call | flops 3000000000 | bytes 16777216 | tf_op jit(solution)/shard_map/pallas_call | solution.py:599
  426.4 3.6 shard_map.116
  431.3 3.6 shard_map.117
  (80 shorter events, 34.4 us)
Async XLA Ops:
  230.3 26.4 %collective-permute-start.8 = (f32[256,2048]{1,0:T(8,128)}, f32[256,2048]{1,0:T(8,128)S(1)}, u32[]{:S(2)}, u32[]{:S(2)}) collective-permute-start(f32[256,2048]{1,0:T(8,128)} %get-tuple-element.68.refs_0_), channel_id=1, source_target_pairs={{0,2},{1,7},{2,4},{3,1},{4,6},{5,3},{6,0},{7,5},{8,10},{9,15},{10,... | collective-permute-start | bytes 6291464 | tf_op jit(solution)/shard_map/ppermute | solution.py:512
  233.4 25.4 %collective-permute-start.11 = (f32[256,2048]{1,0:T(8,128)}, f32[256,2048]{1,0:T(8,128)S(1)}, u32[]{:S(2)}, u32[]{:S(2)}) collective-permute-start(f32[256,2048]{1,0:T(8,128)} %get-tuple-element.69.refs_1_), channel_id=1, source_target_pairs={{0,8},{1,25},{2,10},{3,27},{4,12},{5,29},{6,14},{7,31},{8,16},{9,1... | collective-permute-start | bytes 6291464 | tf_op jit(solution)/shard_map/ppermute | solution.py:512
  233.4 45.8 %collective-permute-start = (f32[256,2048]{1,0:T(8,128)}, f32[256,2048]{1,0:T(8,128)S(1)}, u32[]{:S(2)}, u32[]{:S(2)}) collective-permute-start(f32[256,2048]{1,0:T(8,128)} %get-tuple-element.66.refs_0_), channel_id=1, source_target_pairs={{0,2},{1,7},{2,4},{3,1},{4,6},{5,3},{6,0},{7,5},{8,10},{9,15},{10,... | collective-permute-start | bytes 6291464 | tf_op jit(solution)/shard_map/ppermute | solution.py:512
  233.8 48.6 %collective-permute-start.4 = (f32[256,2048]{1,0:T(8,128)}, f32[256,2048]{1,0:T(8,128)S(1)}, u32[]{:S(2)}, u32[]{:S(2)}) collective-permute-start(f32[256,2048]{1,0:T(8,128)} %get-tuple-element.67.refs_1_), channel_id=1, source_target_pairs={{0,8},{1,25},{2,10},{3,27},{4,12},{5,29},{6,14},{7,31},{8,16},{9,1... | collective-permute-start | bytes 6291464 | tf_op jit(solution)/shard_map/ppermute | solution.py:512
  256.7 26.4 %collective-permute-start.22 = (f32[256,2048]{1,0:T(8,128)S(1)}, f32[256,2048]{1,0:T(8,128)S(1)}, u32[]{:S(2)}, u32[]{:S(2)}) collective-permute-start(f32[256,2048]{1,0:T(8,128)S(1)} %collective-permute-done.8.refs_0_), channel_id=1, source_target_pairs={{0,1},{1,0},{2,3},{3,2},{4,5},{5,4},{6,7},{7,6},{8,9},{9,8},{10,11... | collective-permute-start | bytes 6291464 | tf_op jit(solution)/shard_map/ppermute | solution.py:509
  258.8 24.3 %collective-permute-start.23 = (f32[256,2048]{1,0:T(8,128)S(1)}, f32[256,2048]{1,0:T(8,128)S(1)}, u32[]{:S(2)}, u32[]{:S(2)}) collective-permute-start(f32[256,2048]{1,0:T(8,128)S(1)} %collective-permute-done.11.refs_1_), channel_id=1, source_target_pairs={{0,1},{1,0},{2,3},{3,2},{4,5},{5,4},{6,7},{7,6},{8,9},{9,8},{10,11... | collective-permute-start | bytes 6291464 | tf_op jit(solution)/shard_map/ppermute | solution.py:509
  279.1 6.4 %collective-permute-start.20 = (f32[256,2048]{1,0:T(8,128)S(1)}, f32[256,2048]{1,0:T(8,128)S(1)}, u32[]{:S(2)}, u32[]{:S(2)}) collective-permute-start(f32[256,2048]{1,0:T(8,128)S(1)} %collective-permute-done.refs_0_), channel_id=1, source_target_pairs={{0,1},{1,0},{2,3},{3,2},{4,5},{5,4},{6,7},{7,6},{8,9},{9,8},{10,11... | collective-permute-start | bytes 6291464 | tf_op jit(solution)/shard_map/ppermute | solution.py:509
  280.5 25.3 %collective-permute-start.9 = (f32[256,2048]{1,0:T(8,128)S(1)}, f32[256,2048]{1,0:T(8,128)S(1)}, u32[]{:S(2)}, u32[]{:S(2)}) collective-permute-start(f32[256,2048]{1,0:T(8,128)S(1)} %collective-permute-done.8.refs_0_), channel_id=1, source_target_pairs={{0,2},{1,7},{2,4},{3,1},{4,6},{5,3},{6,0},{7,5},{8,10},{9,15},{10,... | collective-permute-start | bytes 6291464 | tf_op jit(solution)/shard_map/ppermute | solution.py:512
  282.5 25.3 %collective-permute-start.12 = (f32[256,2048]{1,0:T(8,128)S(1)}, f32[256,2048]{1,0:T(8,128)}, u32[]{:S(2)}, u32[]{:S(2)}) collective-permute-start(f32[256,2048]{1,0:T(8,128)S(1)} %collective-permute-done.11.refs_1_), channel_id=1, source_target_pairs={{0,8},{1,25},{2,10},{3,27},{4,12},{5,29},{6,14},{7,31},{8,16},{9,1... | collective-permute-start | bytes 6291464 | tf_op jit(solution)/shard_map/ppermute | solution.py:512
  283.1 26.9 %collective-permute-start.21 = (f32[256,2048]{1,0:T(8,128)S(1)}, f32[256,2048]{1,0:T(8,128)S(1)}, u32[]{:S(2)}, u32[]{:S(2)}) collective-permute-start(f32[256,2048]{1,0:T(8,128)S(1)} %collective-permute-done.4.refs_1_), channel_id=1, source_target_pairs={{0,1},{1,0},{2,3},{3,2},{4,5},{5,4},{6,7},{7,6},{8,9},{9,8},{10,11... | collective-permute-start | bytes 6291464 | tf_op jit(solution)/shard_map/ppermute | solution.py:509
  283.1 45.2 %collective-permute-start.1 = (f32[256,2048]{1,0:T(8,128)S(1)}, f32[256,2048]{1,0:T(8,128)}, u32[]{:S(2)}, u32[]{:S(2)}) collective-permute-start(f32[256,2048]{1,0:T(8,128)S(1)} %collective-permute-done.refs_0_), channel_id=1, source_target_pairs={{0,2},{1,7},{2,4},{3,1},{4,6},{5,3},{6,0},{7,5},{8,10},{9,15},{10,... | collective-permute-start | bytes 6291464 | tf_op jit(solution)/shard_map/ppermute | solution.py:512
  285.5 45.2 %collective-permute-start.5 = (f32[256,2048]{1,0:T(8,128)S(1)}, f32[256,2048]{1,0:T(8,128)}, u32[]{:S(2)}, u32[]{:S(2)}) collective-permute-start(f32[256,2048]{1,0:T(8,128)S(1)} %collective-permute-done.4.refs_1_), channel_id=1, source_target_pairs={{0,8},{1,25},{2,10},{3,27},{4,12},{5,29},{6,14},{7,31},{8,16},{9,1... | collective-permute-start | bytes 6291464 | tf_op jit(solution)/shard_map/ppermute | solution.py:512
  305.8 33.0 %collective-permute-start.18 = (f32[256,2048]{1,0:T(8,128)S(1)}, f32[256,2048]{1,0:T(8,128)S(1)}, u32[]{:S(2)}, u32[]{:S(2)}) collective-permute-start(f32[256,2048]{1,0:T(8,128)S(1)} %collective-permute-done.9.refs_0_), channel_id=1, source_target_pairs={{0,1},{1,0},{2,3},{3,2},{4,5},{5,4},{6,7},{7,6},{8,9},{9,8},{10,11... | collective-permute-start | bytes 6291464 | tf_op jit(solution)/shard_map/ppermute | solution.py:509
  307.8 32.1 %collective-permute-start.19 = (f32[256,2048]{1,0:T(8,128)}, f32[256,2048]{1,0:T(8,128)}, u32[]{:S(2)}, u32[]{:S(2)}) collective-permute-start(f32[256,2048]{1,0:T(8,128)} %collective-permute-done.12.refs_1_), channel_id=1, source_target_pairs={{0,1},{1,0},{2,3},{3,2},{4,5},{5,4},{6,7},{7,6},{8,9},{9,8},{10,11... | collective-permute-start | bytes 6291464 | tf_op jit(solution)/shard_map/ppermute | solution.py:509
  310.0 44.5 %collective-permute-start.10 = (f32[256,2048]{1,0:T(8,128)S(1)}, f32[256,2048]{1,0:T(8,128)}, u32[]{:S(2)}, u32[]{:S(2)}) collective-permute-start(f32[256,2048]{1,0:T(8,128)S(1)} %collective-permute-done.9.refs_0_), channel_id=1, source_target_pairs={{0,2},{1,7},{2,4},{3,1},{4,6},{5,3},{6,0},{7,5},{8,10},{9,15},{10,... | collective-permute-start | bytes 6291464 | tf_op jit(solution)/shard_map/ppermute | solution.py:512
  328.3 26.7 %collective-permute-start.13 = (f32[256,2048]{1,0:T(8,128)}, f32[256,2048]{1,0:T(8,128)}, u32[]{:S(2)}, u32[]{:S(2)}) collective-permute-start(f32[256,2048]{1,0:T(8,128)} %collective-permute-done.12.refs_1_), channel_id=1, source_target_pairs={{0,8},{1,25},{2,10},{3,27},{4,12},{5,29},{6,14},{7,31},{8,16},{9,1... | collective-permute-start | bytes 6291464 | tf_op jit(solution)/shard_map/ppermute | solution.py:512
  330.8 23.7 %collective-permute-start.16 = (f32[256,2048]{1,0:T(8,128)}, f32[256,2048]{1,0:T(8,128)}, u32[]{:S(2)}, u32[]{:S(2)}) collective-permute-start(f32[256,2048]{1,0:T(8,128)} %collective-permute-done.1.refs_0_), channel_id=1, source_target_pairs={{0,1},{1,0},{2,3},{3,2},{4,5},{5,4},{6,7},{7,6},{8,9},{9,8},{10,11... | collective-permute-start | bytes 6291464 | tf_op jit(solution)/shard_map/ppermute | solution.py:509
  338.9 34.3 %collective-permute-start.2 = (f32[256,2048]{1,0:T(8,128)}, f32[256,2048]{1,0:T(8,128)}, u32[]{:S(2)}, u32[]{:S(2)}) collective-permute-start(f32[256,2048]{1,0:T(8,128)} %collective-permute-done.1.refs_0_), channel_id=1, source_target_pairs={{0,2},{1,7},{2,4},{3,1},{4,6},{5,3},{6,0},{7,5},{8,10},{9,15},{10,... | collective-permute-start | bytes 6291464 | tf_op jit(solution)/shard_map/ppermute | solution.py:512
  340.2 36.3 %collective-permute-start.6 = (f32[256,2048]{1,0:T(8,128)}, f32[256,2048]{1,0:T(8,128)}, u32[]{:S(2)}, u32[]{:S(2)}) collective-permute-start(f32[256,2048]{1,0:T(8,128)} %collective-permute-done.5.refs_1_), channel_id=1, source_target_pairs={{0,8},{1,25},{2,10},{3,27},{4,12},{5,29},{6,14},{7,31},{8,16},{9,1... | collective-permute-start | bytes 6291464 | tf_op jit(solution)/shard_map/ppermute | solution.py:512
  354.5 58.7 %collective-permute-start.17 = (f32[256,2048]{1,0:T(8,128)}, f32[256,2048]{1,0:T(8,128)}, u32[]{:S(2)}, u32[]{:S(2)}) collective-permute-start(f32[256,2048]{1,0:T(8,128)} %collective-permute-done.5.refs_1_), channel_id=1, source_target_pairs={{0,1},{1,0},{2,3},{3,2},{4,5},{5,4},{6,7},{7,6},{8,9},{9,8},{10,11... | collective-permute-start | bytes 6291464 | tf_op jit(solution)/shard_map/ppermute | solution.py:509
  354.5 65.3 %collective-permute-start.14 = (f32[256,2048]{1,0:T(8,128)}, f32[256,2048]{1,0:T(8,128)}, u32[]{:S(2)}, u32[]{:S(2)}) collective-permute-start(f32[256,2048]{1,0:T(8,128)} %collective-permute-done.10.refs_0_), channel_id=1, source_target_pairs={{0,1},{1,0},{2,3},{3,2},{4,5},{5,4},{6,7},{7,6},{8,9},{9,8},{10,11... | collective-permute-start | bytes 6291464 | tf_op jit(solution)/shard_map/ppermute | solution.py:509
  355.0 64.8 %collective-permute-start.15 = (f32[256,2048]{1,0:T(8,128)}, f32[256,2048]{1,0:T(8,128)}, u32[]{:S(2)}, u32[]{:S(2)}) collective-permute-start(f32[256,2048]{1,0:T(8,128)} %collective-permute-done.13.refs_1_), channel_id=1, source_target_pairs={{0,1},{1,0},{2,3},{3,2},{4,5},{5,4},{6,7},{7,6},{8,9},{9,8},{10,11... | collective-permute-start | bytes 6291464 | tf_op jit(solution)/shard_map/ppermute | solution.py:509
  373.2 56.8 %collective-permute-start.3 = (f32[256,2048]{1,0:T(8,128)}, f32[256,2048]{1,0:T(8,128)S(1)}, u32[]{:S(2)}, u32[]{:S(2)}) collective-permute-start(f32[256,2048]{1,0:T(8,128)} %collective-permute-done.2.refs_0_), channel_id=1, source_target_pairs={{0,1},{1,0},{2,3},{3,2},{4,5},{5,4},{6,7},{7,6},{8,9},{9,8},{10,11... | collective-permute-start | bytes 6291464 | tf_op jit(solution)/shard_map/ppermute | solution.py:509
  376.5 53.5 %collective-permute-start.7 = (f32[256,2048]{1,0:T(8,128)}, f32[256,2048]{1,0:T(8,128)}, u32[]{:S(2)}, u32[]{:S(2)}) collective-permute-start(f32[256,2048]{1,0:T(8,128)} %collective-permute-done.6.refs_1_), channel_id=1, source_target_pairs={{0,1},{1,0},{2,3},{3,2},{4,5},{5,4},{6,7},{7,6},{8,9},{9,8},{10,11... | collective-permute-start | bytes 6291464 | tf_op jit(solution)/shard_map/ppermute | solution.py:509
  (19 other events, 625.5 us)

commit v7 on v6

--- a/solution.py
+++ b/solution.py
@@ -13,7 +13,7 @@
 N_CORES = 2
 N_GRADS = 4
 RELAY_STEP = 7
-SLOTS = 3
+SLOTS = 2
 
 
 F32 = jnp.float32
@@ -74,8 +74,9 @@
     def down_copy(kind, h):
         return copy(down.at[kind, h], above.at[kind, h], down_send.at[kind, h], above_recv.at[kind, h], device(row + 1 - 2 * kind, col))
 
-    def cast_copy(kind, h, t):
-        return copy(above.at[kind, h], above.at[kind, h], cast_send.at[kind, h, t - 1], above_recv.at[kind, h], device(row, col + t))
+    def cast_copy(kind, h, n):
+        along = (1 - 2 * kind) * (1, -1, 1 - 2 * core)[n]
+        return copy(above.at[kind, h], above.at[kind, h], cast_send.at[kind, h, n], above_recv.at[kind, h], device(row, col + along))
 
     def back_copy(kind, h):
         return copy(peer.at[kind, h], out_ref.at[kind, mine + h], back_send.at[kind, h], back_recv.at[kind, h], partner)
@@ -128,20 +129,27 @@
                     down[kind, g] = above[kind, g] + stage[kind, g]
                     down_copy(kind, g).start()
 
-                for t in range(1, side):
-                    cast_copy(kind, g, t).start()
+                for n in range(2):
+                    cast_copy(kind, g, n).start()
 
         return carry
 
     lax.fori_loop(0, 2 * SLOTS * (side - 1) + n_group, run, 0)
 
     def finish(h, carry):
+        for i in range(2):
+            kind = lax.rem(1 - col // (side // 2) + i, 2)
+            along = position(kind, col)
+
+            @pl.when(along < side - 1)
+            def _():
+                down_copy(kind, h).wait_recv()
+
+            @pl.when(along == 2 * core)
+            def _():
+                cast_copy(kind, h, 2).start()
+
         for kind in range(2):
-
-            @pl.when(position(kind, col) < side - 1)
-            def _():
-                down_copy(kind, h).wait_recv()
-
             base = above[kind, h] + before[kind, h]
             own_total, other_total = totals_ref[kind, mine + h], other[kind, h]
             out_ref[kind, mine + h] = jnp.where(core == kind, base, base + other_total)
@@ -156,14 +164,18 @@
             along, across = position(kind, col), position(kind, row)
             back_copy(kind, h).wait()
 
+            @pl.when(along == 2 * core)
+            def _():
+                cast_copy(kind, h, 2).wait_send()
+
             @pl.when(along < side - 1)
             def _():
                 row_copy(kind, h).wait_send()
 
             @pl.when(along == side - 1)
             def _():
-                for t in range(1, side):
-                    cast_copy(kind, h, t).wait_send()
+                for n in range(2):
+                    cast_copy(kind, h, n).wait_send()
 
                 @pl.when(across < side - 1)
                 def _():
@@ -479,6 +491,7 @@
 def solution(mesh):
     n_seq = mesh.shape["sp"]
     side = math.isqrt(n_seq // N_CORES)
+    assert side == N_GRADS
     row_spec = P(("dp", "sp"), None)
     grad_spec = P("dp", None)
 

time: 435 us -> 430 us (0.989)
  Pallas kernels: 277 us -> 272 us
    pallas_call x1, Pallas kernels: 84.8 us -> 73.5 us  [local_layer(): pl.pallas_call(functools.partial(project_kernel, side), grid=(model_dim /...]
    pallas_call x1, Pallas kernels: 131 us -> 138 us  [local_layer(): pl.pallas_call(functools.partial(exchange_kernel, side, halves), in_specs...]
  transfers between devices with their start and end apart: 24 -> 24, of which waited for: 7 -> 8; matrix products, arithmetic and copies ran while one was open for 5% -> 5% of each run, Pallas kernels for 11% -> 12%
where the time goes in v7:
time: 430 us
  Pallas kernels  272 us (63%)
  waiting for transfers between devices  92.6 us (22%)
  starting transfers between devices  34.6 us (8%)
  matrix products  22.7 us (5%)
  local copies, waits for them, and re-layouts  6.63 us (2%)
    pallas_call x1, Pallas kernels, local_layer(): pl.pallas_call(functools.partial(exchange_kernel, side, halves), in_specs...  138 us
    ppermute x12, waiting for transfers between devices, hop(): return lax.ppermute(value, 'sp', perm=ring_perm(axis, hops))  91.9 us
    pallas_call x1, Pallas kernels, local_layer(): pl.pallas_call(functools.partial(project_kernel, side), grid=(model_dim /...  73.5 us
    pallas_call x9, Pallas kernels, put(): pl.pallas_call(functools.partial(place_kernel, side, step, h, halves, kin...  53.1 us
    dot_general x3, matrix products, back_proj(): return jnp.einsum('ne,de->nd', rows, weight, preferred_element_type=F32)  19.3 us
    ppermute x12, starting transfers between devices, swap_cores(): return lax.ppermute(value, 'sp', perm=core_perm)  18.8 us
    ppermute x12, starting transfers between devices, hop(): return lax.ppermute(value, 'sp', perm=ring_perm(axis, hops))  15.8 us
  transfers between devices with their start and end apart: 24, of which 8 were waited for; matrix products, arithmetic and copies ran while one was open for 5% of the time, Pallas kernels for 12%

profile of v7, /device:TPU:97, one launch (start us, length us, event | category | flops | bytes accessed | tf_op | source)
XLA Modules:
  0.0 430.0 jit_solution(129028987806990180)
XLA Ops:
  2.0 73.5 %project.1 = (bf16[256,2048]{1,0:T(8,128)(2,1)S(1)}, bf16[256,2048]{1,0:T(8,128)(2,1)S(1)}, bf16[256,2048]{1,0:T(8,128)(2,1)S(1)}, bf16[256,2048]{1,0:T(8,128)(2...) custom-call(bf16[256,2048]{1,0:T(8,128)(2,1)S(1)} %copy-done.1, bf16[256,2048]{1,0:T(8,128)(2,1)} %dy_ref.3, ...), custom_call_target="tpu_custom_call" | custom-call | flops 8589934592 | bytes 33554432 | tf_op jit(solution)/shard_map/project/pallas_call | solution.py:544
  77.1 8.2 %attend.1 = (bf16[256,2048]{1,0:T(8,128)(2,1)S(1)}, bf16[5,256,2048]{2,1,0:T(8,128)(2,1)S(1)}) custom-call(bf16[256,2048]{1,0:T(8,128)(2,1)S(1)} %get-tuple-element.58.q_ref, bf16[256,2048]{1,0:T(8,128)(2,1)S(1)} %get-tuple-element.59.k_ref, bf16[256,2048]{1,0:T(8,128)(2,1)S(1)} %get-tuple-element.60.v_ref, bf16[256,2048]{1,0:T(8,128)(2,1)S(1)} %get-tuple-element.61.do_ref, ...), custom_call_target="tpu_custom_call" | custom-call | flops 1610612736 | bytes 16777216 | tf_op jit(solution)/shard_map/attend/pallas_call | solution.py:562
  87.7 137.5 %exchange.1 = (f32[256,2048]{1,0:T(8,128)}, f32[256,2048]{1,0:T(8,128)}, f32[256,2048]{1,0:T(8,128)}, f32[256,2048]{1,0:T(8,128)}, f32[256,2048]{1,0:T(8,128)}, ...) custom-call(bf16[2,4,256,1024]{3,2,1,0:T(8,128)(2,1)} %get-tuple-element.65.early_ref, ...), custom_call_target="tpu_custom_call" | custom-call | flops 8589934592 | bytes 16777216 | tf_op jit(solution)/shard_map/exchange/pallas_call | solution.py:577
  228.8 22.0 %collective-permute-done.8.refs_0_ = f32[256,2048]{1,0:T(8,128)S(1)} collective-permute-done((f32[256,2048]{1,0:T(8,128)}, f32[256,2048]{1,0:T(8,128)S(1)}, u32[]{:S(2)}, u32[]{:S(2)}) %collective-permute-start.8) | collective-permute-done | bytes 2097184 | tf_op jit(solution)/shard_map/ppermute | solution.py:525
  253.1 20.1 %collective-permute-done.refs_0_ = f32[256,2048]{1,0:T(8,128)S(1)} collective-permute-done((f32[256,2048]{1,0:T(8,128)}, f32[256,2048]{1,0:T(8,128)S(1)}, u32[]{:S(2)}, u32[]{:S(2)}) %collective-permute-start) | collective-permute-done | bytes 2097184 | tf_op jit(solution)/shard_map/ppermute | solution.py:525
  281.4 19.3 %collective-permute-done.9.refs_0_ = f32[256,2048]{1,0:T(8,128)S(1)} collective-permute-done((f32[256,2048]{1,0:T(8,128)S(1)}, f32[256,2048]{1,0:T(8,128)S(1)}, u32[]{:S(2)}, u32[]{:S(2)}) %collective-permute-start.9) | collective-permute-done | bytes 2097184 | tf_op jit(solution)/shard_map/ppermute | solution.py:525
  305.7 17.4 %collective-permute-done.1.refs_0_ = f32[256,2048]{1,0:T(8,128)} collective-permute-done((f32[256,2048]{1,0:T(8,128)S(1)}, f32[256,2048]{1,0:T(8,128)}, u32[]{:S(2)}, u32[]{:S(2)}) %collective-permute-start.1) | collective-permute-done | bytes 2097184 | tf_op jit(solution)/shard_map/ppermute | solution.py:525
  325.5 6.2 %fusion.3 = f32[256,2048]{1,0:T(8,128)S(1)} fusion(bf16[2048,2048]{1,0:T(8,128)(2,1)} %wq_ref.1, bf16[5,256,2048]{2,1,0:T(8,128)(2,1)} %copy-done.3), kind=kOutput, calls=%fused_computation.6 | convolution fusion | flops 2147483648 | bytes 11534336 | tf_op jit(solution)/shard_map/ne,de->nd/dot_general | solution.py:531
  331.7 2.9 collective-permute-start.2
  336.0 7.6 %convolution_add_fusion.1 = f32[256,2048]{1,0:T(8,128)} fusion(f32[256,2048]{1,0:T(8,128)S(1)} %fusion.3, bf16[2048,2048]{1,0:T(8,128)(2,1)} %wk_ref.1, bf16[5,256,2048]{2,1,0:T(8,128)(2,1)} %copy-done.3), kind=kOutput, calls=%fused_computation.1 | convolution fusion | flops 2148007936 | bytes 13631488 | tf_op jit(solution)/shard_map/ne,de->nd/dot_general | solution.py:531
  343.6 5.5 %fusion = bf16[256,2048]{1,0:T(8,128)(2,1)} fusion(f32[256,2048]{1,0:T(8,128)} %convolution_add_fusion.1, bf16[2048,2048]{1,0:T(8,128)(2,1)S(1)} %bitcast.15, bf16[5,256,2048]{2,1,0:T(8,128)(2,1)} %copy-done.3), kind=kOutput, calls=%fused_computation.2 | convolution fusion | flops 2148532224 | bytes 12582912 | tf_op jit(solution)/shard_map/ne,de->nd/dot_general | solution.py:531
  349.6 3.2 collective-permute-start.15
  352.8 3.4 convolution_convert_fusion
  356.2 11.9 %collective-permute-done.2.refs_0_ = f32[256,2048]{1,0:T(8,128)} collective-permute-done((f32[256,2048]{1,0:T(8,128)}, f32[256,2048]{1,0:T(8,128)}, u32[]{:S(2)}, u32[]{:S(2)}) %collective-permute-start.2) | collective-permute-done | bytes 2097184 | tf_op jit(solution)/shard_map/ppermute | solution.py:525
  371.1 4.1 collective-permute-start.7
  375.3 6.6 %shard_map.109 = (f32[2048,2048]{1,0:T(8,128)}, f32[2048,2048]{1,0:T(8,128)}, f32[2048,2048]{1,0:T(8,128)}, f32[2048,2048]{1,0:T(8,128)}) custom-call(f32[256,2048]{1,0:T(8,128)} %get-tuple-element.68.refs_0_, f32[256,2048]{1,0:T(8,128)} %get-tuple-element.69.refs_1_, f32[256,2048]{1,0:T(8,128)} %get-tuple-element.72.refs_2_, ...), custom_call_target="tpu_custom_call" | custom-call | flops 3000000000 | bytes 16777216 | tf_op jit(solution)/shard_map/pallas_call | solution.py:612
  381.8 6.6 %shard_map.110 = (f32[2048,2048]{1,0:T(8,128)}, f32[2048,2048]{1,0:T(8,128)}, f32[2048,2048]{1,0:T(8,128)}, f32[2048,2048]{1,0:T(8,128)}) custom-call(f32[256,2048]{1,0:T(8,128)} %get-tuple-element.66.refs_0_, f32[256,2048]{1,0:T(8,128)} %get-tuple-element.67.refs_1_, ...), custom_call_target="tpu_custom_call", output_to_operand_aliasing={{0}: (4, {}), {1}: (5, {}), {2}: (6, {}), {3}: (7, {})} | custom-call | flops 3000000000 | bytes 16777216 | tf_op jit(solution)/shard_map/pallas_call | solution.py:612
  388.4 6.6 %shard_map.111 = (f32[2048,2048]{1,0:T(8,128)}, f32[2048,2048]{1,0:T(8,128)}, f32[2048,2048]{1,0:T(8,128)}, f32[2048,2048]{1,0:T(8,128)}) custom-call(f32[256,2048]{1,0:T(8,128)} %copy-done.6, f32[256,2048]{1,0:T(8,128)} %copy-done.7, f32[256,2048]{1,0:T(8,128)} %copy-done.9, ...), custom_call_target="tpu_custom_call", output_to_operand_aliasing={{0}: (4, {}), {1}: (5, {}), {2}: (6, {}), {3}: (7, {})} | custom-call | flops 3000000000 | bytes 16777216 | tf_op jit(solution)/shard_map/pallas_call | solution.py:612
  395.0 6.6 %shard_map.112 = (f32[2048,2048]{1,0:T(8,128)}, f32[2048,2048]{1,0:T(8,128)}, f32[2048,2048]{1,0:T(8,128)}, f32[2048,2048]{1,0:T(8,128)}) custom-call(f32[256,2048]{1,0:T(8,128)} %copy-done.4, f32[256,2048]{1,0:T(8,128)} %copy-done.5, f32[256,2048]{1,0:T(8,128)} %copy-done.10, ...), custom_call_target="tpu_custom_call", output_to_operand_aliasing={{0}: (4, {}), {1}: (5, {}), {2}: (6, {}), {3}: (7, {})} | custom-call | flops 3000000000 | bytes 16777216 | tf_op jit(solution)/shard_map/pallas_call | solution.py:612
  401.5 6.6 %shard_map.113 = (f32[2048,2048]{1,0:T(8,128)}, f32[2048,2048]{1,0:T(8,128)}, f32[2048,2048]{1,0:T(8,128)}, f32[2048,2048]{1,0:T(8,128)}) custom-call(f32[256,2048]{1,0:T(8,128)} %copy-done.8, f32[256,2048]{1,0:T(8,128)} %collective-permute-done.12.refs_1_, ...), custom_call_target="tpu_custom_call", output_to_operand_aliasing={{0}: (4, {}), {1}: (5, {}), {2}: (6, {}), {3}: (7, {})} | custom-call | flops 3000000000 | bytes 16777216 | tf_op jit(solution)/shard_map/pallas_call | solution.py:612
  408.1 6.6 %shard_map.114 = (f32[2048,2048]{1,0:T(8,128)}, f32[2048,2048]{1,0:T(8,128)}, f32[2048,2048]{1,0:T(8,128)}, f32[2048,2048]{1,0:T(8,128)}) custom-call(f32[256,2048]{1,0:T(8,128)} %collective-permute-done.1.refs_0_, f32[256,2048]{1,0:T(8,128)} %collective-permute-done.5.refs_1_, ...), custom_call_target="tpu_custom_call", output_to_operand_aliasing={{0}: (4, {}), {1}: (5, {}), {2}: (6, {}), {3}: (7, {})} | custom-call | flops 3000000000 | bytes 16777216 | tf_op jit(solution)/shard_map/pallas_call | solution.py:612
  414.7 6.6 %shard_map.115 = (f32[2048,2048]{1,0:T(8,128)}, f32[2048,2048]{1,0:T(8,128)}, f32[2048,2048]{1,0:T(8,128)}, f32[2048,2048]{1,0:T(8,128)}) custom-call(f32[256,2048]{1,0:T(8,128)} %collective-permute-done.10.refs_0_, f32[256,2048]{1,0:T(8,128)} %collective-permute-done.13.refs_1_, ...), custom_call_target="tpu_custom_call", output_to_operand_aliasing={{0}: (4, {}), {1}: (5, {}), {2}: (6, {}), {3}: (7, {})} | custom-call | flops 3000000000 | bytes 16777216 | tf_op jit(solution)/shard_map/pallas_call | solution.py:612
  421.3 3.6 shard_map.116
  426.2 3.6 shard_map.117
  (80 shorter events, 32.7 us)
Async XLA Ops:
  225.3 25.5 %collective-permute-start.8 = (f32[256,2048]{1,0:T(8,128)}, f32[256,2048]{1,0:T(8,128)S(1)}, u32[]{:S(2)}, u32[]{:S(2)}) collective-permute-start(f32[256,2048]{1,0:T(8,128)} %get-tuple-element.68.refs_0_), channel_id=1, source_target_pairs={{0,2},{1,7},{2,4},{3,1},{4,6},{5,3},{6,0},{7,5},{8,10},{9,15},{10,... | collective-permute-start | bytes 6291464 | tf_op jit(solution)/shard_map/ppermute | solution.py:525
  225.4 27.6 %collective-permute-start.11 = (f32[256,2048]{1,0:T(8,128)}, f32[256,2048]{1,0:T(8,128)S(1)}, u32[]{:S(2)}, u32[]{:S(2)}) collective-permute-start(f32[256,2048]{1,0:T(8,128)} %get-tuple-element.69.refs_1_), channel_id=1, source_target_pairs={{0,8},{1,25},{2,10},{3,27},{4,12},{5,29},{6,14},{7,31},{8,16},{9,1... | collective-permute-start | bytes 6291464 | tf_op jit(solution)/shard_map/ppermute | solution.py:525
  227.2 46.0 %collective-permute-start = (f32[256,2048]{1,0:T(8,128)}, f32[256,2048]{1,0:T(8,128)S(1)}, u32[]{:S(2)}, u32[]{:S(2)}) collective-permute-start(f32[256,2048]{1,0:T(8,128)} %get-tuple-element.66.refs_0_), channel_id=1, source_target_pairs={{0,2},{1,7},{2,4},{3,1},{4,6},{5,3},{6,0},{7,5},{8,10},{9,15},{10,... | collective-permute-start | bytes 6291464 | tf_op jit(solution)/shard_map/ppermute | solution.py:525
  227.9 47.5 %collective-permute-start.4 = (f32[256,2048]{1,0:T(8,128)}, f32[256,2048]{1,0:T(8,128)S(1)}, u32[]{:S(2)}, u32[]{:S(2)}) collective-permute-start(f32[256,2048]{1,0:T(8,128)} %get-tuple-element.67.refs_1_), channel_id=1, source_target_pairs={{0,8},{1,25},{2,10},{3,27},{4,12},{5,29},{6,14},{7,31},{8,16},{9,1... | collective-permute-start | bytes 6291464 | tf_op jit(solution)/shard_map/ppermute | solution.py:525
  250.7 25.4 %collective-permute-start.22 = (f32[256,2048]{1,0:T(8,128)S(1)}, f32[256,2048]{1,0:T(8,128)S(1)}, u32[]{:S(2)}, u32[]{:S(2)}) collective-permute-start(f32[256,2048]{1,0:T(8,128)S(1)} %collective-permute-done.8.refs_0_), channel_id=1, source_target_pairs={{0,1},{1,0},{2,3},{3,2},{4,5},{5,4},{6,7},{7,6},{8,9},{9,8},{10,11... | collective-permute-start | bytes 6291464 | tf_op jit(solution)/shard_map/ppermute | solution.py:522
  252.9 23.2 %collective-permute-start.23 = (f32[256,2048]{1,0:T(8,128)S(1)}, f32[256,2048]{1,0:T(8,128)S(1)}, u32[]{:S(2)}, u32[]{:S(2)}) collective-permute-start(f32[256,2048]{1,0:T(8,128)S(1)} %collective-permute-done.11.refs_1_), channel_id=1, source_target_pairs={{0,1},{1,0},{2,3},{3,2},{4,5},{5,4},{6,7},{7,6},{8,9},{9,8},{10,11... | collective-permute-start | bytes 6291464 | tf_op jit(solution)/shard_map/ppermute | solution.py:522
  273.2 6.0 %collective-permute-start.20 = (f32[256,2048]{1,0:T(8,128)S(1)}, f32[256,2048]{1,0:T(8,128)S(1)}, u32[]{:S(2)}, u32[]{:S(2)}) collective-permute-start(f32[256,2048]{1,0:T(8,128)S(1)} %collective-permute-done.refs_0_), channel_id=1, source_target_pairs={{0,1},{1,0},{2,3},{3,2},{4,5},{5,4},{6,7},{7,6},{8,9},{9,8},{10,11... | collective-permute-start | bytes 6291464 | tf_op jit(solution)/shard_map/ppermute | solution.py:522
  275.4 25.3 %collective-permute-start.9 = (f32[256,2048]{1,0:T(8,128)S(1)}, f32[256,2048]{1,0:T(8,128)S(1)}, u32[]{:S(2)}, u32[]{:S(2)}) collective-permute-start(f32[256,2048]{1,0:T(8,128)S(1)} %collective-permute-done.8.refs_0_), channel_id=1, source_target_pairs={{0,2},{1,7},{2,4},{3,1},{4,6},{5,3},{6,0},{7,5},{8,10},{9,15},{10,... | collective-permute-start | bytes 6291464 | tf_op jit(solution)/shard_map/ppermute | solution.py:525
  275.4 27.2 %collective-permute-start.12 = (f32[256,2048]{1,0:T(8,128)S(1)}, f32[256,2048]{1,0:T(8,128)}, u32[]{:S(2)}, u32[]{:S(2)}) collective-permute-start(f32[256,2048]{1,0:T(8,128)S(1)} %collective-permute-done.11.refs_1_), channel_id=1, source_target_pairs={{0,8},{1,25},{2,10},{3,27},{4,12},{5,29},{6,14},{7,31},{8,16},{9,1... | collective-permute-start | bytes 6291464 | tf_op jit(solution)/shard_map/ppermute | solution.py:525
  276.2 26.7 %collective-permute-start.21 = (f32[256,2048]{1,0:T(8,128)S(1)}, f32[256,2048]{1,0:T(8,128)S(1)}, u32[]{:S(2)}, u32[]{:S(2)}) collective-permute-start(f32[256,2048]{1,0:T(8,128)S(1)} %collective-permute-done.4.refs_1_), channel_id=1, source_target_pairs={{0,1},{1,0},{2,3},{3,2},{4,5},{5,4},{6,7},{7,6},{8,9},{9,8},{10,11... | collective-permute-start | bytes 6291464 | tf_op jit(solution)/shard_map/ppermute | solution.py:522
  276.2 47.0 %collective-permute-start.1 = (f32[256,2048]{1,0:T(8,128)S(1)}, f32[256,2048]{1,0:T(8,128)}, u32[]{:S(2)}, u32[]{:S(2)}) collective-permute-start(f32[256,2048]{1,0:T(8,128)S(1)} %collective-permute-done.refs_0_), channel_id=1, source_target_pairs={{0,2},{1,7},{2,4},{3,1},{4,6},{5,3},{6,0},{7,5},{8,10},{9,15},{10,... | collective-permute-start | bytes 6291464 | tf_op jit(solution)/shard_map/ppermute | solution.py:525
  279.2 44.1 %collective-permute-start.5 = (f32[256,2048]{1,0:T(8,128)S(1)}, f32[256,2048]{1,0:T(8,128)}, u32[]{:S(2)}, u32[]{:S(2)}) collective-permute-start(f32[256,2048]{1,0:T(8,128)S(1)} %collective-permute-done.4.refs_1_), channel_id=1, source_target_pairs={{0,8},{1,25},{2,10},{3,27},{4,12},{5,29},{6,14},{7,31},{8,16},{9,1... | collective-permute-start | bytes 6291464 | tf_op jit(solution)/shard_map/ppermute | solution.py:525
  300.7 31.0 %collective-permute-start.18 = (f32[256,2048]{1,0:T(8,128)S(1)}, f32[256,2048]{1,0:T(8,128)S(1)}, u32[]{:S(2)}, u32[]{:S(2)}) collective-permute-start(f32[256,2048]{1,0:T(8,128)S(1)} %collective-permute-done.9.refs_0_), channel_id=1, source_target_pairs={{0,1},{1,0},{2,3},{3,2},{4,5},{5,4},{6,7},{7,6},{8,9},{9,8},{10,11... | collective-permute-start | bytes 6291464 | tf_op jit(solution)/shard_map/ppermute | solution.py:522
  302.7 32.0 %collective-permute-start.19 = (f32[256,2048]{1,0:T(8,128)}, f32[256,2048]{1,0:T(8,128)}, u32[]{:S(2)}, u32[]{:S(2)}) collective-permute-start(f32[256,2048]{1,0:T(8,128)} %collective-permute-done.12.refs_1_), channel_id=1, source_target_pairs={{0,1},{1,0},{2,3},{3,2},{4,5},{5,4},{6,7},{7,6},{8,9},{9,8},{10,11... | collective-permute-start | bytes 6291464 | tf_op jit(solution)/shard_map/ppermute | solution.py:522
  302.9 46.2 %collective-permute-start.10 = (f32[256,2048]{1,0:T(8,128)S(1)}, f32[256,2048]{1,0:T(8,128)}, u32[]{:S(2)}, u32[]{:S(2)}) collective-permute-start(f32[256,2048]{1,0:T(8,128)S(1)} %collective-permute-done.9.refs_0_), channel_id=1, source_target_pairs={{0,2},{1,7},{2,4},{3,1},{4,6},{5,3},{6,0},{7,5},{8,10},{9,15},{10,... | collective-permute-start | bytes 6291464 | tf_op jit(solution)/shard_map/ppermute | solution.py:525
  323.2 26.4 %collective-permute-start.13 = (f32[256,2048]{1,0:T(8,128)}, f32[256,2048]{1,0:T(8,128)}, u32[]{:S(2)}, u32[]{:S(2)}) collective-permute-start(f32[256,2048]{1,0:T(8,128)} %collective-permute-done.12.refs_1_), channel_id=1, source_target_pairs={{0,8},{1,25},{2,10},{3,27},{4,12},{5,29},{6,14},{7,31},{8,16},{9,1... | collective-permute-start | bytes 6291464 | tf_op jit(solution)/shard_map/ppermute | solution.py:525
  323.3 25.8 %collective-permute-start.16 = (f32[256,2048]{1,0:T(8,128)}, f32[256,2048]{1,0:T(8,128)}, u32[]{:S(2)}, u32[]{:S(2)}) collective-permute-start(f32[256,2048]{1,0:T(8,128)} %collective-permute-done.1.refs_0_), channel_id=1, source_target_pairs={{0,1},{1,0},{2,3},{3,2},{4,5},{5,4},{6,7},{7,6},{8,9},{9,8},{10,11... | collective-permute-start | bytes 6291464 | tf_op jit(solution)/shard_map/ppermute | solution.py:522
  331.7 36.4 %collective-permute-start.2 = (f32[256,2048]{1,0:T(8,128)}, f32[256,2048]{1,0:T(8,128)}, u32[]{:S(2)}, u32[]{:S(2)}) collective-permute-start(f32[256,2048]{1,0:T(8,128)} %collective-permute-done.1.refs_0_), channel_id=1, source_target_pairs={{0,2},{1,7},{2,4},{3,1},{4,6},{5,3},{6,0},{7,5},{8,10},{9,15},{10,... | collective-permute-start | bytes 6291464 | tf_op jit(solution)/shard_map/ppermute | solution.py:525
  334.7 36.5 %collective-permute-start.6 = (f32[256,2048]{1,0:T(8,128)}, f32[256,2048]{1,0:T(8,128)}, u32[]{:S(2)}, u32[]{:S(2)}) collective-permute-start(f32[256,2048]{1,0:T(8,128)} %collective-permute-done.5.refs_1_), channel_id=1, source_target_pairs={{0,8},{1,25},{2,10},{3,27},{4,12},{5,29},{6,14},{7,31},{8,16},{9,1... | collective-permute-start | bytes 6291464 | tf_op jit(solution)/shard_map/ppermute | solution.py:525
  349.1 59.0 %collective-permute-start.17 = (f32[256,2048]{1,0:T(8,128)}, f32[256,2048]{1,0:T(8,128)}, u32[]{:S(2)}, u32[]{:S(2)}) collective-permute-start(f32[256,2048]{1,0:T(8,128)} %collective-permute-done.5.refs_1_), channel_id=1, source_target_pairs={{0,1},{1,0},{2,3},{3,2},{4,5},{5,4},{6,7},{7,6},{8,9},{9,8},{10,11... | collective-permute-start | bytes 6291464 | tf_op jit(solution)/shard_map/ppermute | solution.py:522
  349.1 65.6 %collective-permute-start.14 = (f32[256,2048]{1,0:T(8,128)}, f32[256,2048]{1,0:T(8,128)}, u32[]{:S(2)}, u32[]{:S(2)}) collective-permute-start(f32[256,2048]{1,0:T(8,128)} %collective-permute-done.10.refs_0_), channel_id=1, source_target_pairs={{0,1},{1,0},{2,3},{3,2},{4,5},{5,4},{6,7},{7,6},{8,9},{9,8},{10,11... | collective-permute-start | bytes 6291464 | tf_op jit(solution)/shard_map/ppermute | solution.py:522
  349.6 65.1 %collective-permute-start.15 = (f32[256,2048]{1,0:T(8,128)}, f32[256,2048]{1,0:T(8,128)}, u32[]{:S(2)}, u32[]{:S(2)}) collective-permute-start(f32[256,2048]{1,0:T(8,128)} %collective-permute-done.13.refs_1_), channel_id=1, source_target_pairs={{0,1},{1,0},{2,3},{3,2},{4,5},{5,4},{6,7},{7,6},{8,9},{9,8},{10,11... | collective-permute-start | bytes 6291464 | tf_op jit(solution)/shard_map/ppermute | solution.py:522
  368.1 56.8 %collective-permute-start.3 = (f32[256,2048]{1,0:T(8,128)}, f32[256,2048]{1,0:T(8,128)S(1)}, u32[]{:S(2)}, u32[]{:S(2)}) collective-permute-start(f32[256,2048]{1,0:T(8,128)} %collective-permute-done.2.refs_0_), channel_id=1, source_target_pairs={{0,1},{1,0},{2,3},{3,2},{4,5},{5,4},{6,7},{7,6},{8,9},{9,8},{10,11... | collective-permute-start | bytes 6291464 | tf_op jit(solution)/shard_map/ppermute | solution.py:522
  371.1 53.8 %collective-permute-start.7 = (f32[256,2048]{1,0:T(8,128)}, f32[256,2048]{1,0:T(8,128)}, u32[]{:S(2)}, u32[]{:S(2)}) collective-permute-start(f32[256,2048]{1,0:T(8,128)} %collective-permute-done.6.refs_1_), channel_id=1, source_target_pairs={{0,1},{1,0},{2,3},{3,2},{4,5},{5,4},{6,7},{7,6},{8,9},{9,8},{10,11... | collective-permute-start | bytes 6291464 | tf_op jit(solution)/shard_map/ppermute | solution.py:522
  (19 other events, 616.6 us)

commit v8 on v7

--- a/solution.py
+++ b/solution.py
@@ -309,7 +309,7 @@
 
 def exchange_kernel(side, halves, early_ref, late_ref, *refs):
     own_outs, other_outs = refs[: 2 * halves], refs[2 * halves : 4 * halves]
-    early, near, far, pair_early, pair_late, total, landed, gathered = refs[4 * halves : -9]
+    early, own_late, near, far, pair_early, pair_late, total, landed, gathered = refs[4 * halves : -9]
     send_sem, recv_sem, early_sem, ring_send, ring_recv, out_sem, swap_send, swap_recv, load_sem = refs[-9:]
     me = lax.axis_index("sp")
     core, sign, at, ahead, behind, wrap = neighbours(me, side)
@@ -345,6 +345,9 @@
         start(part, 0, late_of(wrap(at[part] + sign), part), near.at[part, 0], ahead[part])
     load = pltpu.make_async_copy(early_ref, early, load_sem.at[0])
     load.start()
+    own_loads = [pltpu.make_async_copy(late_of(at[part], part), own_late.at[part], load_sem.at[1 + part]) for part in range(2)]
+    for own_load in own_loads:
+        own_load.start()
     shares = [send(early_ref.at[part], pair_early.at[part], early_sem.at[0, part], early_sem.at[1, part], partner) for part in range(2)]
 
     n_tiles = 2
@@ -387,7 +390,8 @@
 
     load.wait()
     for part in range(2):
-        accumulate(part, early.at[part, 3], late_of(at[part], part), fresh=True)
+        own_loads[part].wait()
+        accumulate(part, early.at[part, 3], own_late.at[part], fresh=True)
     for part in range(2):
         shares[part].wait_recv()
         take_other(part, 3)
@@ -576,11 +580,12 @@
         axes = (("x", "y"), ("y", "x"))
         blocks = pl.pallas_call(
             functools.partial(exchange_kernel, side, halves),
-            in_specs=[anywhere, pl.BlockSpec(memory_space=VMEM)],
+            in_specs=[anywhere, anywhere],
             out_specs=[anywhere] * (4 * halves),
             out_shape=[jax.ShapeDtypeStruct((block // halves, model_dim), F32)] * (4 * halves),
             scratch_shapes=[
                 VMEM((2, 4, n_rows, half), BF16),
+                VMEM((2, n_rows, model_dim), BF16),
                 VMEM((2, 3, n_rows, model_dim), BF16),
                 VMEM((2, n_rows, model_dim), BF16),
                 VMEM((2, 4, n_rows, half), BF16),
@@ -596,7 +601,7 @@
                 dma((2, halves, side)),
                 dma((2, halves, side)),
                 dma((2, halves, side)),
-                dma((1,)),
+                dma((3,)),
             ],
             cost_estimate=pl.CostEstimate(flops=2 * 2 * block * model_dim * n_rows * 8, bytes_accessed=2**24, transcendentals=0),
             compiler_params=pltpu.CompilerParams(collective_id=1, has_side_effects=True, vmem_limit_bytes=60 * 2**20),

time: 430 us -> 428 us (level)
  no operation moved by 1% of the time
where the time goes in v8:
time: 428 us
  Pallas kernels  270 us (63%)
  waiting for transfers between devices  92.6 us (22%)
  starting transfers between devices  34.6 us (8%)
  matrix products  22.7 us (5%)
  local copies, waits for them, and re-layouts  6.63 us (2%)
    pallas_call x1, Pallas kernels, local_layer(): pl.pallas_call(functools.partial(exchange_kernel, side, halves), in_specs...  135 us
    ppermute x12, waiting for transfers between devices, hop(): return lax.ppermute(value, 'sp', perm=ring_perm(axis, hops))  91.9 us
    pallas_call x1, Pallas kernels, local_layer(): pl.pallas_call(functools.partial(project_kernel, side), grid=(model_dim /...  73.5 us
    pallas_call x9, Pallas kernels, put(): pl.pallas_call(functools.partial(place_kernel, side, step, h, halves, kin...  53.1 us
    dot_general x3, matrix products, back_proj(): return jnp.einsum('ne,de->nd', rows, weight, preferred_element_type=F32)  19.3 us
    ppermute x12, starting transfers between devices, swap_cores(): return lax.ppermute(value, 'sp', perm=core_perm)  18.8 us
    ppermute x12, starting transfers between devices, hop(): return lax.ppermute(value, 'sp', perm=ring_perm(axis, hops))  15.8 us
  transfers between devices with their start and end apart: 24, of which 8 were waited for; matrix products, arithmetic and copies ran while one was open for 5% of the time, Pallas kernels for 12%

profile of v8, /device:TPU:97, one launch (start us, length us, event | category | flops | bytes accessed | tf_op | source)
XLA Modules:
  0.0 427.7 jit_solution(10225218594421065554)
XLA Ops:
  2.0 73.5 %project.1 = (bf16[256,2048]{1,0:T(8,128)(2,1)S(1)}, bf16[256,2048]{1,0:T(8,128)(2,1)S(1)}, bf16[256,2048]{1,0:T(8,128)(2,1)S(1)}, bf16[256,2048]{1,0:T(8,128)(2...) custom-call(bf16[256,2048]{1,0:T(8,128)(2,1)S(1)} %copy-done.1, bf16[256,2048]{1,0:T(8,128)(2,1)} %dy_ref.3, ...), custom_call_target="tpu_custom_call" | custom-call | flops 8589934592 | bytes 33554432 | tf_op jit(solution)/shard_map/project/pallas_call | solution.py:548
  77.1 8.2 %attend.1 = (bf16[256,2048]{1,0:T(8,128)(2,1)S(1)}, bf16[5,256,2048]{2,1,0:T(8,128)(2,1)S(1)}) custom-call(bf16[256,2048]{1,0:T(8,128)(2,1)S(1)} %get-tuple-element.58.q_ref, bf16[256,2048]{1,0:T(8,128)(2,1)S(1)} %get-tuple-element.59.k_ref, bf16[256,2048]{1,0:T(8,128)(2,1)S(1)} %get-tuple-element.60.v_ref, bf16[256,2048]{1,0:T(8,128)(2,1)S(1)} %get-tuple-element.61.do_ref, ...), custom_call_target="tpu_custom_call" | custom-call | flops 1610612736 | bytes 16777216 | tf_op jit(solution)/shard_map/attend/pallas_call | solution.py:566
  87.7 135.3 %exchange.1 = (f32[256,2048]{1,0:T(8,128)}, f32[256,2048]{1,0:T(8,128)}, f32[256,2048]{1,0:T(8,128)}, f32[256,2048]{1,0:T(8,128)}, f32[256,2048]{1,0:T(8,128)}, ...) custom-call(bf16[2,4,256,1024]{3,2,1,0:T(8,128)(2,1)} %get-tuple-element.65.early_ref, ...), custom_call_target="tpu_custom_call" | custom-call | flops 8589934592 | bytes 16777216 | tf_op jit(solution)/shard_map/exchange/pallas_call | solution.py:581
  226.5 22.0 %collective-permute-done.8.refs_0_ = f32[256,2048]{1,0:T(8,128)S(1)} collective-permute-done((f32[256,2048]{1,0:T(8,128)}, f32[256,2048]{1,0:T(8,128)S(1)}, u32[]{:S(2)}, u32[]{:S(2)}) %collective-permute-start.8) | collective-permute-done | bytes 2097184 | tf_op jit(solution)/shard_map/ppermute | solution.py:529
  250.8 20.1 %collective-permute-done.refs_0_ = f32[256,2048]{1,0:T(8,128)S(1)} collective-permute-done((f32[256,2048]{1,0:T(8,128)}, f32[256,2048]{1,0:T(8,128)S(1)}, u32[]{:S(2)}, u32[]{:S(2)}) %collective-permute-start) | collective-permute-done | bytes 2097184 | tf_op jit(solution)/shard_map/ppermute | solution.py:529
  279.1 19.3 %collective-permute-done.9.refs_0_ = f32[256,2048]{1,0:T(8,128)S(1)} collective-permute-done((f32[256,2048]{1,0:T(8,128)S(1)}, f32[256,2048]{1,0:T(8,128)S(1)}, u32[]{:S(2)}, u32[]{:S(2)}) %collective-permute-start.9) | collective-permute-done | bytes 2097184 | tf_op jit(solution)/shard_map/ppermute | solution.py:529
  303.5 17.4 %collective-permute-done.1.refs_0_ = f32[256,2048]{1,0:T(8,128)} collective-permute-done((f32[256,2048]{1,0:T(8,128)S(1)}, f32[256,2048]{1,0:T(8,128)}, u32[]{:S(2)}, u32[]{:S(2)}) %collective-permute-start.1) | collective-permute-done | bytes 2097184 | tf_op jit(solution)/shard_map/ppermute | solution.py:529
  323.2 6.2 %fusion.3 = f32[256,2048]{1,0:T(8,128)S(1)} fusion(bf16[2048,2048]{1,0:T(8,128)(2,1)} %wq_ref.1, bf16[5,256,2048]{2,1,0:T(8,128)(2,1)} %copy-done.3), kind=kOutput, calls=%fused_computation.6 | convolution fusion | flops 2147483648 | bytes 11534336 | tf_op jit(solution)/shard_map/ne,de->nd/dot_general | solution.py:535
  329.5 2.9 collective-permute-start.2
  333.7 7.6 %convolution_add_fusion.1 = f32[256,2048]{1,0:T(8,128)} fusion(f32[256,2048]{1,0:T(8,128)S(1)} %fusion.3, bf16[2048,2048]{1,0:T(8,128)(2,1)} %wk_ref.1, bf16[5,256,2048]{2,1,0:T(8,128)(2,1)} %copy-done.3), kind=kOutput, calls=%fused_computation.1 | convolution fusion | flops 2148007936 | bytes 13631488 | tf_op jit(solution)/shard_map/ne,de->nd/dot_general | solution.py:535
  341.3 5.5 %fusion = bf16[256,2048]{1,0:T(8,128)(2,1)} fusion(f32[256,2048]{1,0:T(8,128)} %convolution_add_fusion.1, bf16[2048,2048]{1,0:T(8,128)(2,1)S(1)} %bitcast.15, bf16[5,256,2048]{2,1,0:T(8,128)(2,1)} %copy-done.3), kind=kOutput, calls=%fused_computation.2 | convolution fusion | flops 2148532224 | bytes 12582912 | tf_op jit(solution)/shard_map/ne,de->nd/dot_general | solution.py:535
  347.3 3.2 collective-permute-start.15
  350.5 3.4 convolution_convert_fusion
  353.9 11.9 %collective-permute-done.2.refs_0_ = f32[256,2048]{1,0:T(8,128)} collective-permute-done((f32[256,2048]{1,0:T(8,128)}, f32[256,2048]{1,0:T(8,128)}, u32[]{:S(2)}, u32[]{:S(2)}) %collective-permute-start.2) | collective-permute-done | bytes 2097184 | tf_op jit(solution)/shard_map/ppermute | solution.py:529
  368.9 4.1 collective-permute-start.7
  373.0 6.6 %shard_map.109 = (f32[2048,2048]{1,0:T(8,128)}, f32[2048,2048]{1,0:T(8,128)}, f32[2048,2048]{1,0:T(8,128)}, f32[2048,2048]{1,0:T(8,128)}) custom-call(f32[256,2048]{1,0:T(8,128)} %get-tuple-element.68.refs_0_, f32[256,2048]{1,0:T(8,128)} %get-tuple-element.69.refs_1_, f32[256,2048]{1,0:T(8,128)} %get-tuple-element.72.refs_2_, ...), custom_call_target="tpu_custom_call" | custom-call | flops 3000000000 | bytes 16777216 | tf_op jit(solution)/shard_map/pallas_call | solution.py:617
  379.6 6.6 %shard_map.110 = (f32[2048,2048]{1,0:T(8,128)}, f32[2048,2048]{1,0:T(8,128)}, f32[2048,2048]{1,0:T(8,128)}, f32[2048,2048]{1,0:T(8,128)}) custom-call(f32[256,2048]{1,0:T(8,128)} %get-tuple-element.66.refs_0_, f32[256,2048]{1,0:T(8,128)} %get-tuple-element.67.refs_1_, ...), custom_call_target="tpu_custom_call", output_to_operand_aliasing={{0}: (4, {}), {1}: (5, {}), {2}: (6, {}), {3}: (7, {})} | custom-call | flops 3000000000 | bytes 16777216 | tf_op jit(solution)/shard_map/pallas_call | solution.py:617
  386.2 6.6 %shard_map.111 = (f32[2048,2048]{1,0:T(8,128)}, f32[2048,2048]{1,0:T(8,128)}, f32[2048,2048]{1,0:T(8,128)}, f32[2048,2048]{1,0:T(8,128)}) custom-call(f32[256,2048]{1,0:T(8,128)} %copy-done.6, f32[256,2048]{1,0:T(8,128)} %copy-done.7, f32[256,2048]{1,0:T(8,128)} %copy-done.9, ...), custom_call_target="tpu_custom_call", output_to_operand_aliasing={{0}: (4, {}), {1}: (5, {}), {2}: (6, {}), {3}: (7, {})} | custom-call | flops 3000000000 | bytes 16777216 | tf_op jit(solution)/shard_map/pallas_call | solution.py:617
  392.7 6.6 %shard_map.112 = (f32[2048,2048]{1,0:T(8,128)}, f32[2048,2048]{1,0:T(8,128)}, f32[2048,2048]{1,0:T(8,128)}, f32[2048,2048]{1,0:T(8,128)}) custom-call(f32[256,2048]{1,0:T(8,128)} %copy-done.4, f32[256,2048]{1,0:T(8,128)} %copy-done.5, f32[256,2048]{1,0:T(8,128)} %copy-done.10, ...), custom_call_target="tpu_custom_call", output_to_operand_aliasing={{0}: (4, {}), {1}: (5, {}), {2}: (6, {}), {3}: (7, {})} | custom-call | flops 3000000000 | bytes 16777216 | tf_op jit(solution)/shard_map/pallas_call | solution.py:617
  399.3 6.6 %shard_map.113 = (f32[2048,2048]{1,0:T(8,128)}, f32[2048,2048]{1,0:T(8,128)}, f32[2048,2048]{1,0:T(8,128)}, f32[2048,2048]{1,0:T(8,128)}) custom-call(f32[256,2048]{1,0:T(8,128)} %copy-done.8, f32[256,2048]{1,0:T(8,128)} %collective-permute-done.12.refs_1_, ...), custom_call_target="tpu_custom_call", output_to_operand_aliasing={{0}: (4, {}), {1}: (5, {}), {2}: (6, {}), {3}: (7, {})} | custom-call | flops 3000000000 | bytes 16777216 | tf_op jit(solution)/shard_map/pallas_call | solution.py:617
  405.9 6.6 %shard_map.114 = (f32[2048,2048]{1,0:T(8,128)}, f32[2048,2048]{1,0:T(8,128)}, f32[2048,2048]{1,0:T(8,128)}, f32[2048,2048]{1,0:T(8,128)}) custom-call(f32[256,2048]{1,0:T(8,128)} %collective-permute-done.1.refs_0_, f32[256,2048]{1,0:T(8,128)} %collective-permute-done.5.refs_1_, ...), custom_call_target="tpu_custom_call", output_to_operand_aliasing={{0}: (4, {}), {1}: (5, {}), {2}: (6, {}), {3}: (7, {})} | custom-call | flops 3000000000 | bytes 16777216 | tf_op jit(solution)/shard_map/pallas_call | solution.py:617
  412.5 6.6 %shard_map.115 = (f32[2048,2048]{1,0:T(8,128)}, f32[2048,2048]{1,0:T(8,128)}, f32[2048,2048]{1,0:T(8,128)}, f32[2048,2048]{1,0:T(8,128)}) custom-call(f32[256,2048]{1,0:T(8,128)} %collective-permute-done.10.refs_0_, f32[256,2048]{1,0:T(8,128)} %collective-permute-done.13.refs_1_, ...), custom_call_target="tpu_custom_call", output_to_operand_aliasing={{0}: (4, {}), {1}: (5, {}), {2}: (6, {}), {3}: (7, {})} | custom-call | flops 3000000000 | bytes 16777216 | tf_op jit(solution)/shard_map/pallas_call | solution.py:617
  419.0 3.6 shard_map.116
  424.0 3.6 shard_map.117
  (80 shorter events, 32.7 us)
Async XLA Ops:
  223.0 25.5 %collective-permute-start.8 = (f32[256,2048]{1,0:T(8,128)}, f32[256,2048]{1,0:T(8,128)S(1)}, u32[]{:S(2)}, u32[]{:S(2)}) collective-permute-start(f32[256,2048]{1,0:T(8,128)} %get-tuple-element.68.refs_0_), channel_id=1, source_target_pairs={{0,2},{1,7},{2,4},{3,1},{4,6},{5,3},{6,0},{7,5},{8,10},{9,15},{10,... | collective-permute-start | bytes 6291464 | tf_op jit(solution)/shard_map/ppermute | solution.py:529
  223.1 27.6 %collective-permute-start.11 = (f32[256,2048]{1,0:T(8,128)}, f32[256,2048]{1,0:T(8,128)S(1)}, u32[]{:S(2)}, u32[]{:S(2)}) collective-permute-start(f32[256,2048]{1,0:T(8,128)} %get-tuple-element.69.refs_1_), channel_id=1, source_target_pairs={{0,8},{1,25},{2,10},{3,27},{4,12},{5,29},{6,14},{7,31},{8,16},{9,1... | collective-permute-start | bytes 6291464 | tf_op jit(solution)/shard_map/ppermute | solution.py:529
  224.9 46.0 %collective-permute-start = (f32[256,2048]{1,0:T(8,128)}, f32[256,2048]{1,0:T(8,128)S(1)}, u32[]{:S(2)}, u32[]{:S(2)}) collective-permute-start(f32[256,2048]{1,0:T(8,128)} %get-tuple-element.66.refs_0_), channel_id=1, source_target_pairs={{0,2},{1,7},{2,4},{3,1},{4,6},{5,3},{6,0},{7,5},{8,10},{9,15},{10,... | collective-permute-start | bytes 6291464 | tf_op jit(solution)/shard_map/ppermute | solution.py:529
  225.6 47.5 %collective-permute-start.4 = (f32[256,2048]{1,0:T(8,128)}, f32[256,2048]{1,0:T(8,128)S(1)}, u32[]{:S(2)}, u32[]{:S(2)}) collective-permute-start(f32[256,2048]{1,0:T(8,128)} %get-tuple-element.67.refs_1_), channel_id=1, source_target_pairs={{0,8},{1,25},{2,10},{3,27},{4,12},{5,29},{6,14},{7,31},{8,16},{9,1... | collective-permute-start | bytes 6291464 | tf_op jit(solution)/shard_map/ppermute | solution.py:529
  248.5 25.4 %collective-permute-start.22 = (f32[256,2048]{1,0:T(8,128)S(1)}, f32[256,2048]{1,0:T(8,128)S(1)}, u32[]{:S(2)}, u32[]{:S(2)}) collective-permute-start(f32[256,2048]{1,0:T(8,128)S(1)} %collective-permute-done.8.refs_0_), channel_id=1, source_target_pairs={{0,1},{1,0},{2,3},{3,2},{4,5},{5,4},{6,7},{7,6},{8,9},{9,8},{10,11... | collective-permute-start | bytes 6291464 | tf_op jit(solution)/shard_map/ppermute | solution.py:526
  250.7 23.2 %collective-permute-start.23 = (f32[256,2048]{1,0:T(8,128)S(1)}, f32[256,2048]{1,0:T(8,128)S(1)}, u32[]{:S(2)}, u32[]{:S(2)}) collective-permute-start(f32[256,2048]{1,0:T(8,128)S(1)} %collective-permute-done.11.refs_1_), channel_id=1, source_target_pairs={{0,1},{1,0},{2,3},{3,2},{4,5},{5,4},{6,7},{7,6},{8,9},{9,8},{10,11... | collective-permute-start | bytes 6291464 | tf_op jit(solution)/shard_map/ppermute | solution.py:526
  270.9 6.0 %collective-permute-start.20 = (f32[256,2048]{1,0:T(8,128)S(1)}, f32[256,2048]{1,0:T(8,128)S(1)}, u32[]{:S(2)}, u32[]{:S(2)}) collective-permute-start(f32[256,2048]{1,0:T(8,128)S(1)} %collective-permute-done.refs_0_), channel_id=1, source_target_pairs={{0,1},{1,0},{2,3},{3,2},{4,5},{5,4},{6,7},{7,6},{8,9},{9,8},{10,11... | collective-permute-start | bytes 6291464 | tf_op jit(solution)/shard_map/ppermute | solution.py:526
  273.2 25.3 %collective-permute-start.9 = (f32[256,2048]{1,0:T(8,128)S(1)}, f32[256,2048]{1,0:T(8,128)S(1)}, u32[]{:S(2)}, u32[]{:S(2)}) collective-permute-start(f32[256,2048]{1,0:T(8,128)S(1)} %collective-permute-done.8.refs_0_), channel_id=1, source_target_pairs={{0,2},{1,7},{2,4},{3,1},{4,6},{5,3},{6,0},{7,5},{8,10},{9,15},{10,... | collective-permute-start | bytes 6291464 | tf_op jit(solution)/shard_map/ppermute | solution.py:529
  273.2 27.2 %collective-permute-start.12 = (f32[256,2048]{1,0:T(8,128)S(1)}, f32[256,2048]{1,0:T(8,128)}, u32[]{:S(2)}, u32[]{:S(2)}) collective-permute-start(f32[256,2048]{1,0:T(8,128)S(1)} %collective-permute-done.11.refs_1_), channel_id=1, source_target_pairs={{0,8},{1,25},{2,10},{3,27},{4,12},{5,29},{6,14},{7,31},{8,16},{9,1... | collective-permute-start | bytes 6291464 | tf_op jit(solution)/shard_map/ppermute | solution.py:529
  273.9 26.7 %collective-permute-start.21 = (f32[256,2048]{1,0:T(8,128)S(1)}, f32[256,2048]{1,0:T(8,128)S(1)}, u32[]{:S(2)}, u32[]{:S(2)}) collective-permute-start(f32[256,2048]{1,0:T(8,128)S(1)} %collective-permute-done.4.refs_1_), channel_id=1, source_target_pairs={{0,1},{1,0},{2,3},{3,2},{4,5},{5,4},{6,7},{7,6},{8,9},{9,8},{10,11... | collective-permute-start | bytes 6291464 | tf_op jit(solution)/shard_map/ppermute | solution.py:526
  273.9 47.0 %collective-permute-start.1 = (f32[256,2048]{1,0:T(8,128)S(1)}, f32[256,2048]{1,0:T(8,128)}, u32[]{:S(2)}, u32[]{:S(2)}) collective-permute-start(f32[256,2048]{1,0:T(8,128)S(1)} %collective-permute-done.refs_0_), channel_id=1, source_target_pairs={{0,2},{1,7},{2,4},{3,1},{4,6},{5,3},{6,0},{7,5},{8,10},{9,15},{10,... | collective-permute-start | bytes 6291464 | tf_op jit(solution)/shard_map/ppermute | solution.py:529
  276.9 44.1 %collective-permute-start.5 = (f32[256,2048]{1,0:T(8,128)S(1)}, f32[256,2048]{1,0:T(8,128)}, u32[]{:S(2)}, u32[]{:S(2)}) collective-permute-start(f32[256,2048]{1,0:T(8,128)S(1)} %collective-permute-done.4.refs_1_), channel_id=1, source_target_pairs={{0,8},{1,25},{2,10},{3,27},{4,12},{5,29},{6,14},{7,31},{8,16},{9,1... | collective-permute-start | bytes 6291464 | tf_op jit(solution)/shard_map/ppermute | solution.py:529
  298.4 31.0 %collective-permute-start.18 = (f32[256,2048]{1,0:T(8,128)S(1)}, f32[256,2048]{1,0:T(8,128)S(1)}, u32[]{:S(2)}, u32[]{:S(2)}) collective-permute-start(f32[256,2048]{1,0:T(8,128)S(1)} %collective-permute-done.9.refs_0_), channel_id=1, source_target_pairs={{0,1},{1,0},{2,3},{3,2},{4,5},{5,4},{6,7},{7,6},{8,9},{9,8},{10,11... | collective-permute-start | bytes 6291464 | tf_op jit(solution)/shard_map/ppermute | solution.py:526
  300.4 32.0 %collective-permute-start.19 = (f32[256,2048]{1,0:T(8,128)}, f32[256,2048]{1,0:T(8,128)}, u32[]{:S(2)}, u32[]{:S(2)}) collective-permute-start(f32[256,2048]{1,0:T(8,128)} %collective-permute-done.12.refs_1_), channel_id=1, source_target_pairs={{0,1},{1,0},{2,3},{3,2},{4,5},{5,4},{6,7},{7,6},{8,9},{9,8},{10,11... | collective-permute-start | bytes 6291464 | tf_op jit(solution)/shard_map/ppermute | solution.py:526
  300.6 46.2 %collective-permute-start.10 = (f32[256,2048]{1,0:T(8,128)S(1)}, f32[256,2048]{1,0:T(8,128)}, u32[]{:S(2)}, u32[]{:S(2)}) collective-permute-start(f32[256,2048]{1,0:T(8,128)S(1)} %collective-permute-done.9.refs_0_), channel_id=1, source_target_pairs={{0,2},{1,7},{2,4},{3,1},{4,6},{5,3},{6,0},{7,5},{8,10},{9,15},{10,... | collective-permute-start | bytes 6291464 | tf_op jit(solution)/shard_map/ppermute | solution.py:529
  320.9 26.4 %collective-permute-start.13 = (f32[256,2048]{1,0:T(8,128)}, f32[256,2048]{1,0:T(8,128)}, u32[]{:S(2)}, u32[]{:S(2)}) collective-permute-start(f32[256,2048]{1,0:T(8,128)} %collective-permute-done.12.refs_1_), channel_id=1, source_target_pairs={{0,8},{1,25},{2,10},{3,27},{4,12},{5,29},{6,14},{7,31},{8,16},{9,1... | collective-permute-start | bytes 6291464 | tf_op jit(solution)/shard_map/ppermute | solution.py:529
  321.0 25.8 %collective-permute-start.16 = (f32[256,2048]{1,0:T(8,128)}, f32[256,2048]{1,0:T(8,128)}, u32[]{:S(2)}, u32[]{:S(2)}) collective-permute-start(f32[256,2048]{1,0:T(8,128)} %collective-permute-done.1.refs_0_), channel_id=1, source_target_pairs={{0,1},{1,0},{2,3},{3,2},{4,5},{5,4},{6,7},{7,6},{8,9},{9,8},{10,11... | collective-permute-start | bytes 6291464 | tf_op jit(solution)/shard_map/ppermute | solution.py:526
  329.5 36.4 %collective-permute-start.2 = (f32[256,2048]{1,0:T(8,128)}, f32[256,2048]{1,0:T(8,128)}, u32[]{:S(2)}, u32[]{:S(2)}) collective-permute-start(f32[256,2048]{1,0:T(8,128)} %collective-permute-done.1.refs_0_), channel_id=1, source_target_pairs={{0,2},{1,7},{2,4},{3,1},{4,6},{5,3},{6,0},{7,5},{8,10},{9,15},{10,... | collective-permute-start | bytes 6291464 | tf_op jit(solution)/shard_map/ppermute | solution.py:529
  332.4 36.5 %collective-permute-start.6 = (f32[256,2048]{1,0:T(8,128)}, f32[256,2048]{1,0:T(8,128)}, u32[]{:S(2)}, u32[]{:S(2)}) collective-permute-start(f32[256,2048]{1,0:T(8,128)} %collective-permute-done.5.refs_1_), channel_id=1, source_target_pairs={{0,8},{1,25},{2,10},{3,27},{4,12},{5,29},{6,14},{7,31},{8,16},{9,1... | collective-permute-start | bytes 6291464 | tf_op jit(solution)/shard_map/ppermute | solution.py:529
  346.8 59.0 %collective-permute-start.17 = (f32[256,2048]{1,0:T(8,128)}, f32[256,2048]{1,0:T(8,128)}, u32[]{:S(2)}, u32[]{:S(2)}) collective-permute-start(f32[256,2048]{1,0:T(8,128)} %collective-permute-done.5.refs_1_), channel_id=1, source_target_pairs={{0,1},{1,0},{2,3},{3,2},{4,5},{5,4},{6,7},{7,6},{8,9},{9,8},{10,11... | collective-permute-start | bytes 6291464 | tf_op jit(solution)/shard_map/ppermute | solution.py:526
  346.8 65.6 %collective-permute-start.14 = (f32[256,2048]{1,0:T(8,128)}, f32[256,2048]{1,0:T(8,128)}, u32[]{:S(2)}, u32[]{:S(2)}) collective-permute-start(f32[256,2048]{1,0:T(8,128)} %collective-permute-done.10.refs_0_), channel_id=1, source_target_pairs={{0,1},{1,0},{2,3},{3,2},{4,5},{5,4},{6,7},{7,6},{8,9},{9,8},{10,11... | collective-permute-start | bytes 6291464 | tf_op jit(solution)/shard_map/ppermute | solution.py:526
  347.3 65.1 %collective-permute-start.15 = (f32[256,2048]{1,0:T(8,128)}, f32[256,2048]{1,0:T(8,128)}, u32[]{:S(2)}, u32[]{:S(2)}) collective-permute-start(f32[256,2048]{1,0:T(8,128)} %collective-permute-done.13.refs_1_), channel_id=1, source_target_pairs={{0,1},{1,0},{2,3},{3,2},{4,5},{5,4},{6,7},{7,6},{8,9},{9,8},{10,11... | collective-permute-start | bytes 6291464 | tf_op jit(solution)/shard_map/ppermute | solution.py:526
  365.9 56.8 %collective-permute-start.3 = (f32[256,2048]{1,0:T(8,128)}, f32[256,2048]{1,0:T(8,128)S(1)}, u32[]{:S(2)}, u32[]{:S(2)}) collective-permute-start(f32[256,2048]{1,0:T(8,128)} %collective-permute-done.2.refs_0_), channel_id=1, source_target_pairs={{0,1},{1,0},{2,3},{3,2},{4,5},{5,4},{6,7},{7,6},{8,9},{9,8},{10,11... | collective-permute-start | bytes 6291464 | tf_op jit(solution)/shard_map/ppermute | solution.py:526
  368.9 53.8 %collective-permute-start.7 = (f32[256,2048]{1,0:T(8,128)}, f32[256,2048]{1,0:T(8,128)}, u32[]{:S(2)}, u32[]{:S(2)}) collective-permute-start(f32[256,2048]{1,0:T(8,128)} %collective-permute-done.6.refs_1_), channel_id=1, source_target_pairs={{0,1},{1,0},{2,3},{3,2},{4,5},{5,4},{6,7},{7,6},{8,9},{9,8},{10,11... | collective-permute-start | bytes 6291464 | tf_op jit(solution)/shard_map/ppermute | solution.py:526
  (19 other events, 616.6 us)
